TPU v7x, 32 devices: a whole 2x2x4 slice. The times are simulated.
32 devices in a mesh: vars: 16 (over z, y, x), samp: 2 (over core).
Axes of the slice: x: 2, y: 2, z: 4, core: 2. Of those that a mesh axis runs over, the one named last changes fastest.
Arguments:
- voxel_data: bfloat16 [32768, 1536], P('vars', 'samp'), may hold values from -6 to 6
- omega_blocks: float32 [256, 8, 128, 128], P('vars'), may hold values from -0.3 to 3, as said below
- block_cols: int32 [256, 8], P('vars'), may hold values from 0 to 255, as said below
Outputs:
- gradient: float32 [256, 8, 128, 128], P('vars', None, 'samp')
- omega_next: float32 [256, 8, 128, 128], P('vars', None, 'samp')
Inputs may be any that keep to these rules, and one draw needn't show every extreme that they name: Block row i is held with the rows of its device. block_cols[i, 0] = i. For s >= 1, block_cols[i, s] = j is a block row of another device, and block_cols[j, s] = i. A row names no block twice. The rows of one device name at most 8 blocks of any one other device, and exactly that many for some pair. The diagonal entries of omega_blocks[i, 0] lie between 1 and 3; all other entries lie between -0.3 and 0.3.
All inputs are finite; a program needn't handle non-finite values.
Results may differ from a plain program's by a relative error of at most 0.0034.
Values may be sent and summed in bfloat16 or wider, within the bound.
No kernel may reach another device: no remote copies, remote signals or barrier semaphores. Data moves between devices by JAX's collectives and lax.ppermute only.
A program may use at most 192 MiB of HBM per device.

v0:
```python
import jax
import jax.numpy as jnp
from jax import lax
from jax.sharding import PartitionSpec as P

STEP = 0.5
PENALTY = 0.1


def block_products(omega_low, own_panels, remote_panels):
    first = jnp.einsum(
        "iab,ibn->ian", omega_low[:, 0], own_panels, preferred_element_type=jnp.float32
    )
    others = jnp.einsum(
        "isab,isbn->ian", omega_low[:, 1:], remote_panels, preferred_element_type=jnp.float32
    )
    w_rows = (first + others).astype(jnp.bfloat16)
    own_gram = jnp.einsum("ian,ibn->iab", w_rows, own_panels, preferred_element_type=jnp.float32)
    other_grams = jnp.einsum(
        "ian,isbn->isab", w_rows, remote_panels, preferred_element_type=jnp.float32
    )
    return jnp.concatenate([own_gram[:, None], other_grams], axis=1)


def on_device(voxel_data, omega_blocks, block_cols):
    row_count, kslots, block_width, _ = omega_blocks.shape
    devices = lax.axis_size("vars")
    samp_count = lax.axis_size("samp")
    sample_part = lax.axis_index("samp")
    half_rows = block_width // samp_count
    samples = voxel_data.shape[1]
    total_samples = samples * samp_count
    capacity = 2 * ((row_count // 2 * (kslots - 1) + devices - 2) // (devices - 1))
    entries = row_count * kslots
    panels = voxel_data.reshape(row_count, block_width, samples)
    flat_cols = block_cols.reshape(entries)
    entry_ids = jnp.arange(entries, dtype=jnp.int32)
    owners = flat_cols // row_count
    remote = entry_ids % kslots != 0
    sort_keys = flat_cols * kslots + entry_ids % kslots
    same_peer = (owners[:, None] == owners[None, :]) & remote[:, None] & remote[None, :]
    send_rank = jnp.sum(same_peer & (entry_ids[:, None] < entry_ids[None, :]), axis=0)
    recv_rank = jnp.sum(same_peer & (sort_keys[:, None] < sort_keys[None, :]), axis=0)
    targets = jnp.where(remote, owners * capacity + send_rank, devices * capacity)
    send_index = (
        jnp.full((devices * capacity,), entries, jnp.int32).at[targets].set(entry_ids, mode="drop")
    )
    send_rows = jnp.where(send_index < entries, send_index // kslots, row_count)
    receive_slot = (owners * capacity + recv_rank).reshape(row_count, kslots)[:, 1:]
    mirror_index = jnp.where(remote, entries + owners * capacity + recv_rank, entry_ids)
    omega_low = omega_blocks.astype(jnp.bfloat16)
    padded_panels = jnp.concatenate(
        [panels, jnp.zeros((1, block_width, samples), jnp.bfloat16)], axis=0
    )
    send_panels = jnp.take(padded_panels, send_rows, axis=0).reshape(
        devices, capacity, block_width, samples
    )
    received = lax.all_to_all(send_panels, "vars", split_axis=0, concat_axis=0, tiled=True)
    remote_panels = jnp.take(
        received.reshape(devices * capacity, block_width, samples), receive_slot, axis=0
    )
    grams = block_products(omega_low, panels, remote_panels)
    column_sums = lax.psum_scatter(grams, "samp", scatter_dimension=3, tiled=True)
    row_sums = lax.psum_scatter(grams, "samp", scatter_dimension=2, tiled=True)
    flat_columns = column_sums.reshape(entries, block_width, half_rows)
    padded = jnp.concatenate(
        [flat_columns, jnp.zeros((1, block_width, half_rows), jnp.float32)], axis=0
    )
    outgoing = jnp.take(padded, send_index, axis=0).reshape(
        devices, capacity, block_width, half_rows
    )
    incoming = lax.all_to_all(outgoing, "vars", split_axis=0, concat_axis=0, tiled=True)
    mirror_table = jnp.concatenate(
        [flat_columns, incoming.reshape(devices * capacity, block_width, half_rows)], axis=0
    )
    mirror = jnp.take(mirror_table, mirror_index, axis=0).reshape(
        row_count, kslots, block_width, half_rows
    )
    combined = row_sums + jnp.swapaxes(mirror, 2, 3)
    gradient = combined * (0.5 / total_samples)
    row_start = sample_part * half_rows
    diagonal = jnp.diagonal(omega_blocks[:, 0], axis1=1, axis2=2)
    inverse_half = lax.dynamic_slice_in_dim(1.0 / diagonal, row_start, half_rows, 1)
    row_ids = lax.broadcasted_iota(jnp.int32, (half_rows, block_width), 0) + row_start
    col_ids = lax.broadcasted_iota(jnp.int32, (half_rows, block_width), 1)
    diag_mask = (row_ids == col_ids).astype(jnp.float32)
    gradient = gradient.at[:, 0].add(-diag_mask[None] * inverse_half[:, :, None])
    omega_half = lax.dynamic_slice_in_dim(omega_blocks, row_start, half_rows, 2)
    trial = omega_half - STEP * gradient
    shrunk = jnp.sign(trial) * jnp.maximum(jnp.abs(trial) - STEP * PENALTY, 0.0)
    first_slot = (jnp.arange(kslots) == 0)[None, :, None, None]
    on_diagonal = jnp.logical_and(first_slot, diag_mask[None, None] > 0.5)
    omega_next = jnp.where(on_diagonal, trial, shrunk)
    return (gradient, omega_next)


def solution(mesh):
    in_specs = (P("vars", "samp"), P("vars", None, None, None), P("vars", None))
    out_specs = (P("vars", None, "samp", None), P("vars", None, "samp", None))
    return jax.shard_map(
        on_device, mesh=mesh, in_specs=in_specs, out_specs=out_specs, check_vma=False
    )
```

profile of v0, /device:TPU:14, one launch (start us, length us, event | category | flops | bytes accessed | tf_op | source)
XLA Modules:
  0.0 884.1 jit_solution(17434571516018193292)
XLA Ops:
  7.2 0.8 copy.63
  7.9 0.1 reshape.363
  8.0 0.1 reshape.364
  8.1 0.1 convert_reduce_fusion.1
  8.3 1.0 scatter_custom_fusion
  9.3 0.1 broadcast_in_dim.82
  9.4 2.3 concatenate.18
  11.7 11.0 %gather_fusion = bf16[128,128,768]{2,1,0:T(8,128)(2,1)} fusion(bf16[17,128,768]{2,1,0:T(8,128)(2,1)S(1)} %concatenate.18, s32[1024]{0:T(1024)S(1)} %pad_clamp_fusion.3), kind=kCustom, calls=%fused_computation | custom fusion | bytes 50332160 | tf_op jit(solution)/shard_map/jit(_take)/gather | solution.py:55
  22.7 21.2 %broadcast_select_fusion = bf16[16,8,128,768]{3,2,1,0:T(8,128)(2,1)} fusion(bf16[16,8,128,768]{3,2,1,0:T(8,128)(2,1)} %bitcast.61, pred[16,8]{1,0:T(8,128)(4,1)S(1)} %broadcast_in_dim.82), kind=kLoop, calls=%fused_computation.6 | loop fusion | flops 12582912 | bytes 50331776 | tf_op jit(solution)/shard_map/jit(_take)/select_n | solution.py:55
  43.9 6.9 all-to-all-start
  50.8 0.2 reduce-scatter.5.cloned.1.call-start
  51.0 0.1 reduce_sum.25
  51.1 0.1 compare_and_fusion.1
  51.2 0.1 reshape.378
  51.3 6.4 copy.95
  57.7 552.3 %all-to-all-done = bf16[16,8,128,768]{3,2,1,0:T(8,128)(2,1)} async-done(((bf16[16,8,128,768]{3,2,1,0:T(8,128)(2,1)}), bf16[16,8,128,768]{3,2,1,0:T(8,128)(2,1)}, u32[]{:S(2)}, u32[]{:S(2)}) %all-to-all-start) | async-done | bytes 25165856 | tf_op jit(solution)/shard_map/all_to_all | solution.py:58
  610.0 18.4 %gather_fusion.1 = bf16[112,128,768]{2,1,0:T(8,128)(2,1)} fusion(bf16[128,128,768]{2,1,0:T(8,128)(2,1)} %bitcast.5, s32[1024]{0:T(1024)S(1)} %pad_clamp_fusion.2), kind=kCustom, calls=%fused_computation.1 | custom fusion | bytes 44040640 | tf_op jit(solution)/shard_map/jit(_take)/gather | solution.py:59
  628.4 15.2 %fusion.1 = f32[16,768,128,1]{1,2,3,0:T(8,128)} fusion(bf16[16,7,128,768]{3,2,1,0:T(8,128)(2,1)} %bitcast.65, pred[16,7]{1,0:T(8,128)(4,1)S(1)} %get-tuple-element.26, bf16[16,8,128,128]{3,2,0,1:T(8,128)(2,1)} %copy.95), kind=kOutput, calls=%fused_computation.9 | convolution fusion | flops 2829582336 | bytes 31981680 | tf_op jit(solution)/shard_map/isab,isbn->ian/dot_general | solution.py:14
  643.6 3.9 fusion.4
  647.5 12.2 %fusion.8 = f32[16,7,128,128]{2,3,1,0:T(8,128)} fusion(bf16[16,128,768]{2,1,0:T(8,128)(2,1)S(1)} %fusion.4, bf16[16,7,128,768]{3,2,1,0:T(8,128)(2,1)} %bitcast.66, pred[16,7]{1,0:T(8,128)(4,1)S(1)} %get-tuple-element.26), kind=kOutput, calls=%fused_computation.25 | convolution fusion | flops 2829582336 | bytes 32505968 | tf_op jit(solution)/shard_map/ian,isbn->isab/dot_general | solution.py:19
  659.7 1.0 convolution_bitcast_fusion
  660.7 2.1 copy-done.4
  662.8 3.8 pad_maximum_fusion
  666.6 0.3 reduce-scatter.3.cloned.1.call-start
  666.9 9.4 %copy.73 = f32[16,8,128,128]{3,1,0,2:T(8,128)} copy(f32[16,8,128,128]{2,3,1,0:T(8,128)} %pad_maximum_fusion) | data formatting | bytes 16777216 | tf_op jit(solution)/shard_map/concatenate | solution.py:22
  676.3 0.1 broadcast_in_dim.90
  676.4 24.8 %reduce-scatter.5.cloned.1.call-done = f32[16,8,128,64]{2,3,1,0:T(8,128)} async-done(((f32[16,8,128,128]{2,3,1,0:T(8,128)}), f32[16,8,128,64]{2,3,1,0:T(8,128)}) %reduce-scatter.5.cloned.1.call-update) | async-done | bytes 4194320 | tf_op jit(solution)/shard_map/reduce_scatter | solution.py:63
  701.2 4.7 concatenate.20
  705.9 5.0 gather_fusion.2
  710.9 5.0 bitcast_select_fusion.1
  716.0 4.4 copy.75
  720.4 7.1 all-to-all-start.1
  727.5 4.6 copy.85
  732.1 1.8 gather_fusion.4
  733.9 4.8 constant_dynamic-slice_fusion
  738.7 0.1 convert_compare_fusion
  738.8 0.1 convert_negate_fusion
  738.9 0.1 broadcast_and_fusion
  739.0 84.0 %all-to-all-done.1 = f32[16,8,128,64]{2,3,1,0:T(8,128)} async-done(((f32[16,8,128,64]{2,3,1,0:T(8,128)}), f32[16,8,128,64]{2,3,1,0:T(8,128)}, u32[]{:S(2)}, u32[]{:S(2)}) %all-to-all-start.1) | async-done | bytes 4194336 | tf_op jit(solution)/shard_map/all_to_all | solution.py:72
  823.0 8.4 pad_maximum_fusion.1
  831.4 6.2 gather_fusion.3
  837.6 6.3 fusion.5
  843.9 2.0 copy-done
  845.9 1.5 slice_add_fusion
  847.4 14.5 %scatter-add.4 = f32[16,8,64,128]{3,1,0,2:T(8,128)} dynamic-update-slice(f32[16,8,64,128]{3,1,0,2:T(8,128)} %copy-done, f32[16,1,64,128]{3,1,0,2:T(1,128)S(1)} %slice_add_fusion, s32[]{:T(128)} %constant.142.clone.1, s32[]{:T(128)} %constant.142.clone.1, s32[]{:T(128)} %constant.142.clone.1, s32[]{:T(128)} %constant.142.clone.1) | dynamic-update-slice | bytes 1048580 | tf_op jit(solution)/shard_map/scatter-add | solution.py:87
  861.9 6.8 copy.79
  868.7 3.7 multiply_select_fusion
  872.4 4.4 copy.80
  (29 shorter events, 0.2 us)
Async XLA Ops:
  43.9 566.1 %all-to-all-start = ((bf16[16,8,128,768]{3,2,1,0:T(8,128)(2,1)}), bf16[16,8,128,768]{3,2,1,0:T(8,128)(2,1)}, u32[]{:S(2)}, u32[]{:S(2)}) async-start(bf16[16,8,128,768]{3,2,1,0:T(8,128)(2,1)} %broadcast_select_fusion), calls=%async_computation | async-start | bytes 50331648 | tf_op jit(solution)/shard_map/all_to_all | solution.py:58
  50.8 650.4 %reduce-scatter.5.cloned.1.call-start = ((), (), s32[]{:S(2)}) async-start(), calls=%async_computation.5 | async-start | bytes 12582912 | tf_op jit(solution)/shard_map/reduce_scatter | solution.py:63
  628.4 15.2 %copy-start.2 = (bf16[2048,768]{1,0:T(8,128)(2,1)S(1)}, bf16[2048,768]{1,0:T(8,128)(2,1)}, u32[]{:S(2)}) copy-start(bf16[2048,768]{1,0:T(8,128)(2,1)} %param.5) | copy-start | bytes 9437188
  659.7 3.1 copy-start.4
  666.6 171.0 %reduce-scatter.3.cloned.1.call-start = ((), (), s32[]{:S(2)}) async-start(), calls=%async_computation.4 | async-start | bytes 12582912 | tf_op jit(solution)/shard_map/reduce_scatter | solution.py:64
  720.4 7.1 slice-start
  720.4 102.6 %all-to-all-start.1 = ((f32[16,8,128,64]{2,3,1,0:T(8,128)}), f32[16,8,128,64]{2,3,1,0:T(8,128)}, u32[]{:S(2)}, u32[]{:S(2)}) async-start(f32[16,8,128,64]{2,3,1,0:T(8,128)} %copy.75), calls=%async_computation.3 | async-start | bytes 8388608 | tf_op jit(solution)/shard_map/all_to_all | solution.py:72
  843.9 2.0 copy-start
  861.9 6.8 copy-start.1
  861.9 6.8 copy-start.3
Sparse Core Ops, SparseCore 0:
  666.8 34.3 reduce-scatter.4
  703.5 17.6 reduce-scatter.2
where the time goes:
time: 888 us; the launch traced here: 884 us
  waiting for transfers between devices  661 us (74%)
  local copies, waits for them, and re-layouts  111 us (12%)
  other arithmetic  50.4 us (6%)
  matrix products  32.3 us (4%)
  between operations  14.7 us (2%)
  starting transfers between devices  14.5 us (2%)
    all_to_all x1, waiting for transfers between devices, on_device(): lax.all_to_all(send_panels, 'vars', split_axis=0, concat_axis=0, tiled=True)  552 us
    all_to_all x1, waiting for transfers between devices, on_device(): lax.all_to_all(outgoing, 'vars', split_axis=0, concat_axis=0, tiled=True)  84 us
    unnamed x15, local copies, waits for them, and re-layouts  27.1 us
    reduce_scatter x1, waiting for transfers between devices, on_device(): lax.psum_scatter(grams, 'samp', scatter_dimension=3, tiled=True)  24.8 us
    select_n x1, other arithmetic, on_device(): jnp.take(padded_panels, send_rows, axis=0)  21.2 us
    gather x1, local copies, waits for them, and re-layouts, on_device(): jnp.take(received.reshape(devices * capacity, block_width, samples), rece...  18.4 us
  transfers between devices with their start and end apart: 4, of which 3 were waited for; matrix products, arithmetic and copies ran while one was open for 7% of the time, Pallas kernels for 0%

commit v1 on v0

v1 whole, which is shorter than its diff:
```python
import jax
import jax.numpy as jnp
from jax import lax
from jax.experimental import pallas as pl
from jax.experimental.pallas import tpu as pltpu
from jax.sharding import PartitionSpec as P


STEP = 0.5
PENALTY = 0.1


def line_length(devices):
    bits = devices.bit_length() - 1
    return 1 << -(-bits // 3)


def arrivals(place, length):
    others = [p for p in range(length) if p != place]
    outward = 1 if 2 * place < length else -1
    return sorted(others, key=lambda p: (abs(p - place), outward * (p - place)))


def select_kernel(sources, targets, capacity):
    def body(info_ref, *refs):
        ins, outs = refs[:sources], refs[sources : sources + targets]
        held, came, left = refs[sources + targets :]

        for k in range(sources):

            @pl.when(info_ref[targets * capacity] == k)
            def _(k=k):
                for t in range(targets):
                    for c in range(capacity):
                        panel = info_ref[t * capacity + c]
                        pltpu.make_async_copy(ins[k].at[panel], held.at[t, c], came.at[t]).start()

        for t in range(targets):
            pltpu.make_async_copy(held.at[t], held.at[t], came.at[t]).wait()
            pltpu.make_async_copy(held.at[t], outs[t], left.at[t]).start()
        for t in range(targets):
            pltpu.make_async_copy(held.at[t], outs[t], left.at[t]).wait()

    return body


def select_panels(info, arrays, targets, capacity):
    _, block_width, samples = arrays[0].shape
    shape = jax.ShapeDtypeStruct((capacity, block_width, samples), arrays[0].dtype)
    moved = 2 * targets * capacity * block_width * samples * 2
    return pl.pallas_call(
        select_kernel(len(arrays), targets, capacity),
        out_shape=[shape] * targets,
        in_specs=[pl.BlockSpec(memory_space=pltpu.SMEM)]
        + [pl.BlockSpec(memory_space=pl.ANY)] * len(arrays),
        out_specs=[pl.BlockSpec(memory_space=pl.ANY)] * targets,
        scratch_shapes=[
            pltpu.VMEM((targets, capacity, block_width, samples), arrays[0].dtype),
            pltpu.SemaphoreType.DMA((targets,)),
            pltpu.SemaphoreType.DMA((targets,)),
        ],
        cost_estimate=pl.CostEstimate(flops=0, transcendentals=0, bytes_accessed=moved),
        name="select_panels",
    )(info, *arrays)


def gram_kernel(layout, kslots, capacity, half_rows):
    def body(entry_ref, panel_ref, code_ref, omega_ref, own_ref, *refs):
        arrays = refs[: len(layout)]
        keep_row, keep_col, send_row, send_col, table, sem = refs[len(layout) :]
        row = pl.program_id(0)
        block_width = table.shape[1] // kslots

        def fetch(source, k, c, fixed):
            entry = entry_ref[source * capacity + c]
            i = entry // kslots
            s = entry % kslots
            panel = c if fixed else panel_ref[source * capacity + c]

            @pl.when(entry >= 0)
            def _():
                at = pl.multiple_of(s * block_width, block_width)
                pltpu.make_async_copy(
                    arrays[k].at[panel], table.at[i, pl.ds(at, block_width)], sem.at[i]
                ).start()

        @pl.when(row == 0)
        def _():
            for i in range(table.shape[0]):
                pltpu.make_async_copy(
                    own_ref.at[i], table.at[i, pl.ds(0, block_width)], sem.at[i]
                ).start()
            for k, users in enumerate(layout):
                for source, code in users:
                    if code is None:
                        for c in range(capacity):
                            fetch(source, k, c, True)
                    else:

                        @pl.when(code_ref[source] == code)
                        def _(source=source, k=k):
                            for c in range(capacity):
                                fetch(source, k, c, False)

        pltpu.make_async_copy(table.at[row], table.at[row], sem.at[row]).wait()
        panels = table[row]
        w_row = jnp.zeros((block_width, panels.shape[1]), jnp.float32)
        for s in range(kslots):
            w_row += jnp.dot(
                omega_ref[0, s].astype(jnp.bfloat16),
                panels[s * block_width : (s + 1) * block_width],
                preferred_element_type=jnp.float32,
            )
        w_row = w_row.astype(jnp.bfloat16)
        contract = (((1,), (1,)), ((), ()))
        gram = lax.dot_general(w_row, panels, contract, preferred_element_type=jnp.float32)
        flipped = lax.dot_general(panels, w_row, contract, preferred_element_type=jnp.float32)
        first = code_ref[code_ref.shape[0] - 1] == 0
        for s in range(kslots):
            part = gram[:, s * block_width : (s + 1) * block_width]
            mine = jnp.where(first, part[:half_rows], part[half_rows:])
            other = jnp.where(first, part[half_rows:], part[:half_rows])
            keep_row[0, s] = mine
            send_row[0, s] = other.astype(jnp.bfloat16)
            part = flipped[s * block_width : (s + 1) * block_width]
            mine = jnp.where(first, part[:half_rows], part[half_rows:])
            other = jnp.where(first, part[half_rows:], part[:half_rows])
            keep_col[0, s] = mine
            send_col[0, s] = other.astype(jnp.bfloat16)

    return body


def grams_of(entries, panel_ids, codes, omega_blocks, own, arrays, layout, capacity, half_rows):
    row_count, kslots, block_width, _ = omega_blocks.shape
    samples = own.shape[2]
    half = (1, kslots, half_rows, block_width)
    whole = (row_count, kslots, half_rows, block_width)
    flops = 6 * row_count * kslots * block_width * block_width * samples
    spec = pl.BlockSpec(half, lambda i, *_: (i, 0, 0, 0))
    return pl.pallas_call(
        gram_kernel(layout, kslots, capacity, half_rows),
        out_shape=[jax.ShapeDtypeStruct(whole, jnp.float32)] * 2
        + [jax.ShapeDtypeStruct(whole, jnp.bfloat16)] * 2,
        grid_spec=pltpu.PrefetchScalarGridSpec(
            num_scalar_prefetch=3,
            grid=(row_count,),
            in_specs=[pl.BlockSpec((1, kslots, block_width, block_width), lambda i, *_: (i, 0, 0, 0))]
            + [pl.BlockSpec(memory_space=pl.ANY)] * (1 + len(arrays)),
            out_specs=[spec] * 4,
            scratch_shapes=[
                pltpu.VMEM((row_count, kslots * block_width, samples), jnp.bfloat16),
                pltpu.SemaphoreType.DMA((row_count,)),
            ],
        ),
        compiler_params=pltpu.CompilerParams(
            dimension_semantics=("arbitrary",), vmem_limit_bytes=56 << 20
        ),
        cost_estimate=pl.CostEstimate(
            flops=flops, transcendentals=0, bytes_accessed=(kslots * row_count + 64) * block_width * samples * 2
        ),
        name="grams",
    )(entries, panel_ids, codes, omega_blocks, own, *arrays)


def rows_per_step(row_count):
    return 4 if row_count % 4 == 0 else 1


def outgoing_kernel(slot_ref, keep_ref, came_ref, own_ref, out_ref):
    rows, kslots = keep_ref.shape[:2]
    first = pl.program_id(0) * rows
    for r in range(rows):
        own_ref[r] = keep_ref[r, 0] + came_ref[r, 0].astype(jnp.float32)
        for s in range(1, kslots):
            summed = keep_ref[r, s] + came_ref[r, s].astype(jnp.float32)
            out_ref[slot_ref[(first + r) * kslots + s]] = summed.astype(jnp.bfloat16)


def outgoing_blocks(slots, keep_col, came_col, slot_count):
    row_count, kslots, half_rows, block_width = keep_col.shape
    rows = rows_per_step(row_count)
    spec = pl.BlockSpec((rows, kslots, half_rows, block_width), lambda i, *_: (i, 0, 0, 0))
    return pl.pallas_call(
        outgoing_kernel,
        out_shape=[
            jax.ShapeDtypeStruct((row_count, half_rows, block_width), jnp.float32),
            jax.ShapeDtypeStruct((slot_count, half_rows, block_width), jnp.bfloat16),
        ],
        grid_spec=pltpu.PrefetchScalarGridSpec(
            num_scalar_prefetch=1,
            grid=(row_count // rows,),
            in_specs=[spec, spec],
            out_specs=[
                pl.BlockSpec((rows, half_rows, block_width), lambda i, *_: (i, 0, 0)),
                pl.BlockSpec((slot_count, half_rows, block_width), lambda i, *_: (0, 0, 0)),
            ],
        ),
        compiler_params=pltpu.CompilerParams(dimension_semantics=("arbitrary",)),
        name="outgoing",
    )(slots, keep_col, came_col)


def final_kernel(scale):
    def body(slot_ref, half_ref, keep_ref, came_ref, own_ref, mirror_ref, omega_ref, grad_ref, next_ref):
        rows, kslots, half_rows, block_width = keep_ref.shape
        first = pl.program_id(0) * rows
        start = half_ref[0] * half_rows
        row_ids = lax.broadcasted_iota(jnp.int32, (half_rows, block_width), 0) + start
        col_ids = lax.broadcasted_iota(jnp.int32, (half_rows, block_width), 1)
        on_diagonal = row_ids == col_ids
        for r in range(rows):
            for s in range(kslots):
                omega = omega_ref[r, s]
                if s == 0:
                    mirror = own_ref[r]
                else:
                    mirror = mirror_ref[slot_ref[(first + r) * kslots + s]].astype(jnp.float32)
                gradient = (keep_ref[r, s] + came_ref[r, s].astype(jnp.float32) + mirror) * scale
                if s == 0:
                    inverse = 1.0 / jnp.where(on_diagonal, omega, 1.0)
                    gradient = gradient - jnp.where(on_diagonal, inverse, 0.0)
                trial = omega - STEP * gradient
                size = jnp.maximum(jnp.abs(trial) - STEP * PENALTY, 0.0)
                shrunk = jnp.where(trial < 0.0, -size, size)
                if s == 0:
                    shrunk = jnp.where(on_diagonal, trial, shrunk)
                grad_ref[r, s] = gradient
                next_ref[r, s] = shrunk

    return body


def final_step(slots, sample_part, keep_row, came_row, own_col, incoming, omega_blocks, scale):
    row_count, kslots, half_rows, block_width = keep_row.shape
    rows = rows_per_step(row_count)
    spec = pl.BlockSpec((rows, kslots, half_rows, block_width), lambda i, *_: (i, 0, 0, 0))
    shape = jax.ShapeDtypeStruct(keep_row.shape, jnp.float32)
    return pl.pallas_call(
        final_kernel(scale),
        out_shape=[shape, shape],
        grid_spec=pltpu.PrefetchScalarGridSpec(
            num_scalar_prefetch=2,
            grid=(row_count // rows,),
            in_specs=[
                spec,
                spec,
                pl.BlockSpec((rows, half_rows, block_width), lambda i, *_: (i, 0, 0)),
                pl.BlockSpec(incoming.shape, lambda i, *_: (0, 0, 0)),
                pl.BlockSpec(
                    (rows, kslots, half_rows, block_width),
                    lambda i, slot, half: (i, 0, half[0], 0),
                ),
            ],
            out_specs=[spec, spec],
        ),
        compiler_params=pltpu.CompilerParams(dimension_semantics=("arbitrary",)),
        name="final_step",
    )(slots, sample_part.reshape(1), keep_row, came_row, own_col, incoming, omega_blocks)


def ranks_among(same, keys):
    return jnp.sum((same & (keys[..., None, :] < keys[..., :, None])).astype(jnp.int32), axis=-1)


def step_on_device(voxel_data, omega_blocks, block_cols):
    row_count, kslots, block_width, _ = omega_blocks.shape
    devices = lax.axis_size("vars")
    samp_count = lax.axis_size("samp")
    me = lax.axis_index("vars")
    sample_part = lax.axis_index("samp")
    half_rows = block_width // samp_count
    samples = voxel_data.shape[1]
    total_samples = samples * samp_count
    capacity = 2 * ((row_count // 2 * (kslots - 1) + devices - 2) // (devices - 1))
    entries = row_count * kslots
    length = line_length(devices)
    plane = devices // length
    place, seat = me // plane, me % plane
    panels = voxel_data.reshape(row_count, block_width, samples)

    def along(array, step):
        pairs = [
            (p * plane + b, (p + step) * plane + b)
            for p in range(length)
            if 0 <= p + step < length
            for b in range(plane)
        ]
        return lax.ppermute(array, "vars", pairs)

    def across(array, mask):
        pairs = [(p * plane + b, p * plane + (b ^ mask)) for p in range(length) for b in range(plane)]
        return lax.ppermute(array, "vars", pairs)

    order = [[p] + arrivals(p, length) for p in range(length)]
    offsets = [[order[p][m] - p for p in range(length)] for m in range(length)]
    sources = jnp.array(order, jnp.int32)[place]

    all_cols = lax.all_gather(block_cols, "vars", axis=0, tiled=False)
    panels, all_cols = lax.optimization_barrier((panels, all_cols))

    source_cols = all_cols[sources * plane + seat].reshape(length, entries)
    entry_ids = jnp.arange(entries, dtype=jnp.int32)
    remote = entry_ids % kslots != 0
    targets = place * plane + (seat ^ jnp.arange(1, plane, dtype=jnp.int32))
    hits = (source_cols[:, None, :] // row_count == targets[None, :, None]) & remote
    before = ranks_among(hits[:, :, None, :], jnp.broadcast_to(entry_ids, hits.shape))
    chosen = hits[:, :, None, :] & (
        before[:, :, None, :] == jnp.arange(capacity, dtype=jnp.int32)[None, None, :, None]
    )
    picks = jnp.sum(jnp.where(chosen, entry_ids // kslots, 0), axis=-1).reshape(length, -1)

    flat_cols = block_cols.reshape(entries)
    owners = flat_cols // row_count
    same_peer = (owners[:, None] == owners[None, :]) & remote[:, None] & remote[None, :]
    sort_keys = flat_cols * kslots + entry_ids % kslots
    entry_rank = ranks_among(same_peer, entry_ids)
    key_rank = ranks_among(same_peer, sort_keys)
    mirror_in = owners * capacity + entry_rank
    mirror_out = owners * capacity + key_rank
    peers = (
        sources[:, None] * plane + (seat ^ jnp.arange(plane, dtype=jnp.int32))[None, :]
    ).reshape(-1)
    wanted = (
        remote
        & (owners == peers[:, None])[:, None, :]
        & (key_rank == jnp.arange(capacity, dtype=jnp.int32)[:, None])[None]
    )
    entry_table = (jnp.sum(jnp.where(wanted, entry_ids + 1, 0), axis=-1) - 1).reshape(-1)
    panel_table = jnp.sum(jnp.where(wanted, flat_cols % row_count, 0), axis=-1).reshape(-1)

    came = {0: panels}
    received = []
    codes = []
    for m in range(length):
        if m > 0:
            for step in (-1, 1):
                came[step * m] = along(came[step * (m - 1)], -step)
        options = sorted(set(offsets[m]))
        code = jnp.array([options.index(o) for o in offsets[m]], jnp.int32)[place]
        codes.append((options, code))
        info = jnp.concatenate([picks[m], code[None]])
        sent = select_panels(info, [came[o] for o in options], plane - 1, capacity)
        received.append([across(block, mask + 1) for mask, block in enumerate(sent)])

    arrays, layout, code_values = [], [], [jnp.int32(0)] * (length * plane + 1)
    line_users = {}
    for m in range(length):
        for mask in range(1, plane):
            arrays.append(received[m][mask - 1])
            layout.append([(m * plane + mask, None)])
        if m > 0:
            options, code = codes[m]
            code_values[m * plane] = code
            for number, option in enumerate(options):
                line_users.setdefault(option, []).append((m * plane, number))
    for option in sorted(line_users):
        arrays.append(came[option])
        layout.append(line_users[option])
    code_values[-1] = sample_part
    keep_row, keep_col, send_row, send_col = grams_of(
        entry_table,
        panel_table,
        jnp.stack(code_values),
        omega_blocks,
        panels,
        arrays,
        layout,
        capacity,
        half_rows,
    )

    swap = [(k, samp_count - 1 - k) for k in range(samp_count)]
    came_col = lax.ppermute(send_col, "samp", swap)
    came_row = lax.ppermute(send_row, "samp", swap)
    own_col, outgoing = outgoing_blocks(mirror_out, keep_col, came_col, devices * capacity)
    incoming = lax.all_to_all(
        outgoing.reshape(devices, capacity, half_rows, block_width),
        "vars",
        split_axis=0,
        concat_axis=0,
        tiled=True,
    ).reshape(devices * capacity, half_rows, block_width)
    return tuple(
        final_step(
            mirror_in,
            sample_part,
            keep_row,
            came_row,
            own_col,
            incoming,
            omega_blocks,
            0.5 / total_samples,
        )
    )


def solution(mesh):
    in_specs = (P("vars", "samp"), P("vars", None, None, None), P("vars", None))
    out_specs = (P("vars", None, "samp", None), P("vars", None, "samp", None))
    return jax.shard_map(
        step_on_device, mesh=mesh, in_specs=in_specs, out_specs=out_specs, check_vma=False
    )
```

time: 888 us -> 565 us (0.64)
  waiting for transfers between devices: 661 us -> 382 us
  local copies, waits for them, and re-layouts: 111 us -> 9.19 us
  Pallas kernels: 0 us -> 73.8 us
  starting transfers between devices: 14.5 us -> 62.7 us
  other arithmetic: 50.4 us -> 7.18 us
  matrix products: 32.3 us -> 0 us
  blocking collectives: 0 us -> 28.6 us
  between operations: 14.7 us -> 0.93 us
    all_to_all x2 -> x1, waiting for transfers between devices: 636 us -> 44.2 us  [step_on_device(): lax.all_to_all(outgoing.reshape(devices, capacity, half_rows, block_width...]
    ppermute x0 -> x20, waiting for transfers between devices: none -> 338 us  [the longest x12 209 us: across(): return lax.ppermute(array, 'vars', pairs)]
    pallas_call x0 -> x7, Pallas kernels: none -> 73.8 us  [the longest x1 37.4 us: grams_of(): pl.pallas_call(gram_kernel(layout, kslots, capacity, half_rows), out_shap...]
    ppermute x0 -> x20, starting transfers between devices: none -> 55.4 us  [the longest x12 28.4 us: across(): return lax.ppermute(array, 'vars', pairs)]
    gather x5 -> x2, local copies, waits for them, and re-layouts: 42.4 us -> 0.62 us  [step_on_device(): source_cols = all_cols[sources * plane + seat].reshape(length, entries)]
    dot_general x4 -> x0, matrix products: 32.3 us -> none  [the longest x1 15.2 us: block_products(): jnp.einsum('isab,isbn->ian', omega_low[:, 1:], remote_panels, preferred_e...]
    select_n x6 -> x4, other arithmetic: 29.9 us -> 0.72 us  [the longest x1 0.7 us: step_on_device(): source_cols = all_cols[sources * plane + seat].reshape(length, entries)]
    all_gather x0 -> x1, blocking collectives: none -> 28.6 us  [step_on_device(): all_cols = lax.all_gather(block_cols, 'vars', axis=0, tiled=False)]
  transfers between devices with their start and end apart: 4 -> 21, of which waited for: 3 -> 13; matrix products, arithmetic and copies ran while one was open for 7% -> 2% of each run, Pallas kernels for 0% -> 4%
where the time goes in v1:
time: 565 us
  waiting for transfers between devices  382 us (68%)
  Pallas kernels  73.8 us (13%)
  starting transfers between devices  62.7 us (11%)
  blocking collectives  28.6 us (5%)
  local copies, waits for them, and re-layouts  9.19 us (2%)
  other arithmetic  7.18 us (1%)
    ppermute x12, waiting for transfers between devices, across(): return lax.ppermute(array, 'vars', pairs)  209 us
    ppermute x6, waiting for transfers between devices, along(): return lax.ppermute(array, 'vars', pairs)  121 us
    all_to_all x1, waiting for transfers between devices, step_on_device(): lax.all_to_all(outgoing.reshape(devices, capacity, half_rows, block_width...  44.2 us
    pallas_call x1, Pallas kernels, grams_of(): pl.pallas_call(gram_kernel(layout, kslots, capacity, half_rows), out_shap...  37.4 us
    all_gather x1, blocking collectives, step_on_device(): all_cols = lax.all_gather(block_cols, 'vars', axis=0, tiled=False)  28.6 us
    ppermute x12, starting transfers between devices, across(): return lax.ppermute(array, 'vars', pairs)  28.4 us
    ppermute x6, starting transfers between devices, along(): return lax.ppermute(array, 'vars', pairs)  27 us
    pallas_call x4, Pallas kernels, select_panels(): pl.pallas_call(select_kernel(len(arrays), targets, capacity), out_shape=[...  21.3 us
  transfers between devices with their start and end apart: 21, of which 13 were waited for; matrix products, arithmetic and copies ran while one was open for 2% of the time, Pallas kernels for 4%

profile of v1, /device:TPU:14, one launch (start us, length us, event | category | flops | bytes accessed | tf_op | source)
XLA Modules:
  0.0 564.8 jit_solution(7324648395933841602)
XLA Ops:
  0.6 28.6 %all-gather.1 = s32[16,16,8]{1,2,0:T(8,128)S(1)} all-gather(s32[1,16,8]{1,2,0:T(8,128)} %bitcast.17), channel_id=2, replica_groups=mesh['vars'=16,'samp'=2] {'vars'}, dimensions={0}, use_global_device_ids=true | all-gather | bytes 8704 | tf_op jit(solution)/shard_map/all_gather | solution.py:299
  29.2 7.0 %collective-permute-start.4 = (bf16[16,128,768]{2,1,0:T(8,128)(2,1)}, bf16[16,128,768]{2,1,0:T(8,128)(2,1)S(1)}, u32[]{:S(2)}, u32[]{:S(2)}) collective-permute-start(bf16[16,128,768]{2,1,0:T(8,128)(2,1)} %bitcast.11), channel_id=1, source_target_pairs={{8,0},{10,2},{12,4},{14,6},{16,8},{18,10},{20,12},{22,14},{24,16},... | collective-permute-start | bytes 9437192 | tf_op jit(solution)/shard_map/ppermute | solution.py:289
  36.3 1.9 collective-permute-start.3
  38.2 62.3 %collective-permute-done.4.refs_1_.refs_2_.refs_15_ = bf16[16,128,768]{2,1,0:T(8,128)(2,1)S(1)} collective-permute-done((bf16[16,128,768]{2,1,0:T(8,128)(2,1)}, bf16[16,128,768]{2,1,0:T(8,128)(2,1)S(1)}, u32[]{:S(2)}, u32[]{:S(2)}) %collective-permute-start.4) | collective-permute-done | bytes 3145760 | tf_op jit(solution)/shard_map/ppermute | solution.py:289
  100.5 4.3 collective-permute-start.9
  104.8 4.6 collective-permute-start.8
  109.5 58.9 %collective-permute-done.9.refs_3_.refs_2_.refs_16_ = bf16[16,128,768]{2,1,0:T(8,128)(2,1)} collective-permute-done((bf16[16,128,768]{2,1,0:T(8,128)(2,1)S(1)}, bf16[16,128,768]{2,1,0:T(8,128)(2,1)}, u32[]{:S(2)}, u32[]{:S(2)}) %collective-permute-start.9) | collective-permute-done | bytes 3145760 | tf_op jit(solution)/shard_map/ppermute | solution.py:289
  168.3 4.5 collective-permute-start.14
  172.9 4.6 collective-permute-start.13
  177.5 0.7 fusion.7
  180.3 5.5 select_panels.4
  185.9 2.5 collective-permute-start
  188.4 4.3 collective-permute-start.1
  194.0 1.1 pad_add_fusion.1.info_ref
  195.1 1.2 pad_add_fusion.info_ref
  196.4 5.3 select_panels.5
  201.7 5.2 select_panels.6
  206.9 16.9 %collective-permute-done.refs_0_ = bf16[8,128,768]{2,1,0:T(8,128)(2,1)S(1)} collective-permute-done((bf16[8,128,768]{2,1,0:T(8,128)(2,1)}, bf16[8,128,768]{2,1,0:T(8,128)(2,1)S(1)}, u32[]{:S(2)}, u32[]{:S(2)}) %collective-permute-start) | collective-permute-done | bytes 1572896 | tf_op jit(solution)/shard_map/ppermute | solution.py:293
  223.8 2.0 collective-permute-start.5
  225.9 34.1 %collective-permute-done.1.refs_1_ = bf16[8,128,768]{2,1,0:T(8,128)(2,1)S(1)} collective-permute-done((bf16[8,128,768]{2,1,0:T(8,128)(2,1)}, bf16[8,128,768]{2,1,0:T(8,128)(2,1)S(1)}, u32[]{:S(2)}, u32[]{:S(2)}) %collective-permute-start.1) | collective-permute-done | bytes 1572896 | tf_op jit(solution)/shard_map/ppermute | solution.py:293
  260.0 2.4 collective-permute-start.6
  262.4 1.5 collective-permute-start.10
  264.1 1.1 pad_add_fusion.2.info_ref
  265.2 5.2 select_panels.7
  270.5 2.0 collective-permute-start.11
  272.5 18.9 %collective-permute-done.5.refs_3_ = bf16[8,128,768]{2,1,0:T(8,128)(2,1)} collective-permute-done((bf16[8,128,768]{2,1,0:T(8,128)(2,1)}, bf16[8,128,768]{2,1,0:T(8,128)(2,1)}, u32[]{:S(2)}, u32[]{:S(2)}) %collective-permute-start.5) | collective-permute-done | bytes 1572896 | tf_op jit(solution)/shard_map/ppermute | solution.py:293
  291.4 5.8 %collective-permute-start.12 = (bf16[8,128,768]{2,1,0:T(8,128)(2,1)}, bf16[8,128,768]{2,1,0:T(8,128)(2,1)S(1)}, u32[]{:S(2)}, u32[]{:S(2)}) collective-permute-start(bf16[8,128,768]{2,1,0:T(8,128)(2,1)} %get-tuple-element.32), channel_id=1, source_target_pairs={{0,6},{2,4},{4,2},{6,0},{8,14},{10,12},{12,10},{14,8},{16,22},{18,... | collective-permute-start | bytes 4718600 | tf_op jit(solution)/shard_map/ppermute | solution.py:293
  297.2 34.5 %collective-permute-done.6.refs_4_ = bf16[8,128,768]{2,1,0:T(8,128)(2,1)} collective-permute-done((bf16[8,128,768]{2,1,0:T(8,128)(2,1)}, bf16[8,128,768]{2,1,0:T(8,128)(2,1)}, u32[]{:S(2)}, u32[]{:S(2)}) %collective-permute-start.6) | collective-permute-done | bytes 1572896 | tf_op jit(solution)/shard_map/ppermute | solution.py:293
  331.7 2.0 collective-permute-start.16
  333.7 25.2 %collective-permute-done.10.refs_6_ = bf16[8,128,768]{2,1,0:T(8,128)(2,1)} collective-permute-done((bf16[8,128,768]{2,1,0:T(8,128)(2,1)}, bf16[8,128,768]{2,1,0:T(8,128)(2,1)}, u32[]{:S(2)}, u32[]{:S(2)}) %collective-permute-start.10) | collective-permute-done | bytes 1572896 | tf_op jit(solution)/shard_map/ppermute | solution.py:293
  358.9 5.8 %collective-permute-start.17 = (bf16[8,128,768]{2,1,0:T(8,128)(2,1)}, bf16[8,128,768]{2,1,0:T(8,128)(2,1)}, u32[]{:S(2)}, u32[]{:S(2)}) collective-permute-start(bf16[8,128,768]{2,1,0:T(8,128)(2,1)} %get-tuple-element.35), channel_id=1, source_target_pairs={{0,6},{2,4},{4,2},{6,0},{8,14},{10,12},{12,10},{14,8},{16,22},{18,... | collective-permute-start | bytes 4718600 | tf_op jit(solution)/shard_map/ppermute | solution.py:293
  364.6 0.7 fusion.8
  365.9 0.6 fusion.2
  367.1 0.6 sub.29.entry_ref
  367.7 2.4 stack.4.code_ref
  370.1 28.5 %collective-permute-done.11.refs_7_ = bf16[8,128,768]{2,1,0:T(8,128)(2,1)S(1)} collective-permute-done((bf16[8,128,768]{2,1,0:T(8,128)(2,1)}, bf16[8,128,768]{2,1,0:T(8,128)(2,1)S(1)}, u32[]{:S(2)}, u32[]{:S(2)}) %collective-permute-start.11) | collective-permute-done | bytes 1572896 | tf_op jit(solution)/shard_map/ppermute | solution.py:293
  398.6 27.8 %collective-permute-done.15.refs_9_ = bf16[8,128,768]{2,1,0:T(8,128)(2,1)} collective-permute-done((bf16[8,128,768]{2,1,0:T(8,128)(2,1)}, bf16[8,128,768]{2,1,0:T(8,128)(2,1)}, u32[]{:S(2)}, u32[]{:S(2)}) %collective-permute-start.15) | collective-permute-done | bytes 1572896 | tf_op jit(solution)/shard_map/ppermute | solution.py:293
  426.3 22.9 %collective-permute-done.16.refs_10_ = bf16[8,128,768]{2,1,0:T(8,128)(2,1)} collective-permute-done((bf16[8,128,768]{2,1,0:T(8,128)(2,1)}, bf16[8,128,768]{2,1,0:T(8,128)(2,1)}, u32[]{:S(2)}, u32[]{:S(2)}) %collective-permute-start.16) | collective-permute-done | bytes 1572896 | tf_op jit(solution)/shard_map/ppermute | solution.py:293
  449.2 37.4 %grams.1 = (f32[16,8,64,128]{3,2,1,0:T(8,128)}, f32[16,8,64,128]{3,2,1,0:T(8,128)}, bf16[16,8,64,128]{3,2,1,0:T(8,128)(2,1)}, bf16[16,8,64,128]{3,2,1,0:T(8,128)(2,1)}) custom-call(s32[128]{0:T(128)} %sub.29.entry_ref, s32[128]{0:T(128)} %reshape.307.panel_ref, s32[17]{0:T(128)} %stack.4.code_ref, f32[16,8,128,128]{3,2,1,0:T(8,128)} %omega_ref.3, ...), custom_call_target="tpu_custom_call" | custom-call | flops 9663676416 | bytes 37748736 | tf_op jit(solution)/shard_map/grams/pallas_call | solution.py:141
  486.7 0.6 multiply_add_fusion.1
  487.3 3.8 collective-permute-done.19.came_ref
  491.0 1.3 copy-done.3
  492.4 5.7 %outgoing.1 = (f32[16,64,128]{2,1,0:T(8,128)}, bf16[128,64,128]{2,1,0:T(8,128)(2,1)}) custom-call(s32[128]{0:T(128)} %get-tuple-element.50.slot_ref, f32[16,8,64,128]{3,2,1,0:T(8,128)} %get-tuple-element.38.keep_ref, bf16[16,8,64,128]{3,2,1,0:T(8,128)(2,1)} %copy-done.3), custom_call_target="tpu_custom_call" | custom-call | tf_op jit(solution)/shard_map/outgoing/pallas_call | solution.py:184
  498.0 7.2 %all-to-all-start = ((bf16[16,8,64,128]{3,2,1,0:T(8,128)(2,1)}), bf16[16,8,64,128]{3,2,1,0:T(8,128)(2,1)S(1)}, u32[]{:S(2)}, u32[]{:S(2)}) async-start(bf16[16,8,64,128]{3,2,1,0:T(8,128)(2,1)} %bitcast.16), calls=%async_computation | async-start | bytes 4194304 | tf_op jit(solution)/shard_map/all_to_all | solution.py:377
  505.3 4.5 collective-permute-done.18.came_ref
  509.8 44.2 %all-to-all-done = bf16[16,8,64,128]{3,2,1,0:T(8,128)(2,1)S(1)} async-done(((bf16[16,8,64,128]{3,2,1,0:T(8,128)(2,1)}), bf16[16,8,64,128]{3,2,1,0:T(8,128)(2,1)S(1)}, u32[]{:S(2)}, u32[]{:S(2)}) %all-to-all-start) | async-done | bytes 2097184 | tf_op jit(solution)/shard_map/all_to_all | solution.py:377
  553.9 1.3 copy-done.2
  555.3 9.5 %final_step.1 = (f32[16,8,64,128]{3,2,1,0:T(8,128)}, f32[16,8,64,128]{3,2,1,0:T(8,128)}) custom-call(s32[128]{0:T(128)} %get-tuple-element.51.slot_ref, s32[1]{0:T(128)} %bitcast.half_ref, f32[16,8,64,128]{3,2,1,0:T(8,128)} %get-tuple-element.36.keep_ref, bf16[16,8,64,128]{3,2,1,0:T(8,128)(2,1)} %collective-permute-done.18.came_ref, ...), custom_call_target="tpu_custom_call" | custom-call | tf_op jit(solution)/shard_map/final_step/pallas_call | solution.py:239
  (65 shorter events, 4.8 us)
Async XLA Ops:
  29.2 71.3 %collective-permute-start.4 = (bf16[16,128,768]{2,1,0:T(8,128)(2,1)}, bf16[16,128,768]{2,1,0:T(8,128)(2,1)S(1)}, u32[]{:S(2)}, u32[]{:S(2)}) collective-permute-start(bf16[16,128,768]{2,1,0:T(8,128)(2,1)} %bitcast.11), channel_id=1, source_target_pairs={{8,0},{10,2},{12,4},{14,6},{16,8},{18,10},{20,12},{22,14},{24,16},... | collective-permute-start | bytes 9437192 | tf_op jit(solution)/shard_map/ppermute | solution.py:289
  36.3 68.5 %collective-permute-start.3 = (bf16[16,128,768]{2,1,0:T(8,128)(2,1)}, bf16[16,128,768]{2,1,0:T(8,128)(2,1)S(1)}, u32[]{:S(2)}, u32[]{:S(2)}) collective-permute-start(bf16[16,128,768]{2,1,0:T(8,128)(2,1)} %bitcast.12), channel_id=1, source_target_pairs={{0,8},{2,10},{4,12},{6,14},{8,16},{10,18},{12,20},{14,22},{16,24},... | collective-permute-start | bytes 9437192 | tf_op jit(solution)/shard_map/ppermute | solution.py:289
  100.5 85.4 %copy-start = (bf16[16,128,768]{2,1,0:T(8,128)(2,1)}, bf16[16,128,768]{2,1,0:T(8,128)(2,1)S(1)}, u32[]{:S(2)}) copy-start(bf16[16,128,768]{2,1,0:T(8,128)(2,1)S(1)} %collective-permute-done.4.refs_1_.refs_2_.refs_15_) | copy-start | bytes 9437188
  100.5 67.8 %collective-permute-start.9 = (bf16[16,128,768]{2,1,0:T(8,128)(2,1)S(1)}, bf16[16,128,768]{2,1,0:T(8,128)(2,1)}, u32[]{:S(2)}, u32[]{:S(2)}) collective-permute-start(bf16[16,128,768]{2,1,0:T(8,128)(2,1)S(1)} %collective-permute-done.4.refs_1_.refs_2_.refs_15_), channel_id=1, source_target_pairs={{8,0},{10,2},{12,4},{14,6},{16,8},{18,10},{20,12},{22,14},{24,16},... | collective-permute-start | bytes 9437192 | tf_op jit(solution)/shard_map/ppermute | solution.py:289
  104.8 63.6 %copy-start.1 = (bf16[16,128,768]{2,1,0:T(8,128)(2,1)}, bf16[16,128,768]{2,1,0:T(8,128)(2,1)S(1)}, u32[]{:S(2)}) copy-start(bf16[16,128,768]{2,1,0:T(8,128)(2,1)S(1)} %collective-permute-done.3.refs_0_.refs_1_.refs_14_) | copy-start | bytes 9437188
  104.8 68.0 %collective-permute-start.8 = (bf16[16,128,768]{2,1,0:T(8,128)(2,1)S(1)}, bf16[16,128,768]{2,1,0:T(8,128)(2,1)}, u32[]{:S(2)}, u32[]{:S(2)}) collective-permute-start(bf16[16,128,768]{2,1,0:T(8,128)(2,1)S(1)} %collective-permute-done.3.refs_0_.refs_1_.refs_14_), channel_id=1, source_target_pairs={{0,8},{2,10},{4,12},{6,14},{8,16},{10,18},{12,20},{14,22},{16,24},... | collective-permute-start | bytes 9437192 | tf_op jit(solution)/shard_map/ppermute | solution.py:289
  168.3 94.0 %collective-permute-start.14 = (bf16[16,128,768]{2,1,0:T(8,128)(2,1)}, bf16[16,128,768]{2,1,0:T(8,128)(2,1)}, u32[]{:S(2)}, u32[]{:S(2)}) collective-permute-start(bf16[16,128,768]{2,1,0:T(8,128)(2,1)} %collective-permute-done.9.refs_3_.refs_2_.refs_16_), channel_id=1, source_target_pairs={{8,0},{10,2},{12,4},{14,6},{16,8},{18,10},{20,12},{22,14},{24,16},... | collective-permute-start | bytes 9437192 | tf_op jit(solution)/shard_map/ppermute | solution.py:289
  172.9 89.5 %collective-permute-start.13 = (bf16[16,128,768]{2,1,0:T(8,128)(2,1)}, bf16[16,128,768]{2,1,0:T(8,128)(2,1)}, u32[]{:S(2)}, u32[]{:S(2)}) collective-permute-start(bf16[16,128,768]{2,1,0:T(8,128)(2,1)} %collective-permute-done.8.refs_0_.refs_1_.refs_13_), channel_id=1, source_target_pairs={{0,8},{2,10},{4,12},{6,14},{8,16},{10,18},{12,20},{14,22},{16,24},... | collective-permute-start | bytes 9437192 | tf_op jit(solution)/shard_map/ppermute | solution.py:289
  180.3 12.4 %copy-start.10 = (s32[4]{0:T(128)S(1)}, s32[4]{0:T(128)}, u32[]{:S(2)}) copy-start(s32[4]{0:T(128)} %constant.123.clone) | copy-start | bytes 52
  180.3 13.0 %copy-start.9 = (s32[4]{0:T(128)S(1)}, s32[4]{0:T(128)}, u32[]{:S(2)}) copy-start(s32[4]{0:T(128)} %constant.122.clone) | copy-start | bytes 52
  185.9 38.0 %collective-permute-start = (bf16[8,128,768]{2,1,0:T(8,128)(2,1)}, bf16[8,128,768]{2,1,0:T(8,128)(2,1)S(1)}, u32[]{:S(2)}, u32[]{:S(2)}) collective-permute-start(bf16[8,128,768]{2,1,0:T(8,128)(2,1)} %get-tuple-element.24), channel_id=1, source_target_pairs={{0,2},{2,0},{4,6},{6,4},{8,10},{10,8},{12,14},{14,12},{16,18},{18,... | collective-permute-start | bytes 4718600 | tf_op jit(solution)/shard_map/ppermute | solution.py:293
  188.4 71.6 %collective-permute-start.1 = (bf16[8,128,768]{2,1,0:T(8,128)(2,1)}, bf16[8,128,768]{2,1,0:T(8,128)(2,1)S(1)}, u32[]{:S(2)}, u32[]{:S(2)}) collective-permute-start(bf16[8,128,768]{2,1,0:T(8,128)(2,1)} %get-tuple-element.25), channel_id=1, source_target_pairs={{0,4},{2,6},{4,0},{6,2},{8,12},{10,14},{12,8},{14,10},{16,20},{18,... | collective-permute-start | bytes 4718600 | tf_op jit(solution)/shard_map/ppermute | solution.py:293
  192.7 77.8 %collective-permute-start.2 = (bf16[8,128,768]{2,1,0:T(8,128)(2,1)}, bf16[8,128,768]{2,1,0:T(8,128)(2,1)}, u32[]{:S(2)}, u32[]{:S(2)}) collective-permute-start(bf16[8,128,768]{2,1,0:T(8,128)(2,1)} %get-tuple-element.26), channel_id=1, source_target_pairs={{0,6},{2,4},{4,2},{6,0},{8,14},{10,12},{12,10},{14,8},{16,22},{18,... | collective-permute-start | bytes 4718600 | tf_op jit(solution)/shard_map/ppermute | solution.py:293
  201.6 62.3 %copy-start.8 = (s32[16,8]{0,1:T(8,128)S(1)}, s32[16,8]{0,1:T(8,128)}, u32[]{:S(2)}) copy-start(s32[16,8]{0,1:T(8,128)} %param.10) | copy-start | bytes 1540
  223.8 46.6 %copy-start.4 = (bf16[8,128,768]{2,1,0:T(8,128)(2,1)}, bf16[8,128,768]{2,1,0:T(8,128)(2,1)S(1)}, u32[]{:S(2)}) copy-start(bf16[8,128,768]{2,1,0:T(8,128)(2,1)S(1)} %collective-permute-done.refs_0_) | copy-start | bytes 4718596
  223.8 67.6 %collective-permute-start.5 = (bf16[8,128,768]{2,1,0:T(8,128)(2,1)}, bf16[8,128,768]{2,1,0:T(8,128)(2,1)}, u32[]{:S(2)}, u32[]{:S(2)}) collective-permute-start(bf16[8,128,768]{2,1,0:T(8,128)(2,1)} %get-tuple-element.27), channel_id=1, source_target_pairs={{0,2},{2,0},{4,6},{6,4},{8,10},{10,8},{12,14},{14,12},{16,18},{18,... | collective-permute-start | bytes 4718600 | tf_op jit(solution)/shard_map/ppermute | solution.py:293
  260.0 10.5 %copy-start.5 = (bf16[8,128,768]{2,1,0:T(8,128)(2,1)}, bf16[8,128,768]{2,1,0:T(8,128)(2,1)S(1)}, u32[]{:S(2)}) copy-start(bf16[8,128,768]{2,1,0:T(8,128)(2,1)S(1)} %collective-permute-done.1.refs_1_) | copy-start | bytes 4718596
  260.0 71.6 %collective-permute-start.6 = (bf16[8,128,768]{2,1,0:T(8,128)(2,1)}, bf16[8,128,768]{2,1,0:T(8,128)(2,1)}, u32[]{:S(2)}, u32[]{:S(2)}) collective-permute-start(bf16[8,128,768]{2,1,0:T(8,128)(2,1)} %get-tuple-element.28), channel_id=1, source_target_pairs={{0,4},{2,6},{4,0},{6,2},{8,12},{10,14},{12,8},{14,10},{16,20},{18,... | collective-permute-start | bytes 4718600 | tf_op jit(solution)/shard_map/ppermute | solution.py:293
  262.4 69.3 %collective-permute-start.7 = (bf16[8,128,768]{2,1,0:T(8,128)(2,1)}, bf16[8,128,768]{2,1,0:T(8,128)(2,1)}, u32[]{:S(2)}, u32[]{:S(2)}) collective-permute-start(bf16[8,128,768]{2,1,0:T(8,128)(2,1)} %get-tuple-element.29), channel_id=1, source_target_pairs={{0,6},{2,4},{4,2},{6,0},{8,14},{10,12},{12,10},{14,8},{16,22},{18,... | collective-permute-start | bytes 4718600 | tf_op jit(solution)/shard_map/ppermute | solution.py:293
  262.4 96.5 %collective-permute-start.10 = (bf16[8,128,768]{2,1,0:T(8,128)(2,1)}, bf16[8,128,768]{2,1,0:T(8,128)(2,1)}, u32[]{:S(2)}, u32[]{:S(2)}) collective-permute-start(bf16[8,128,768]{2,1,0:T(8,128)(2,1)} %get-tuple-element.30), channel_id=1, source_target_pairs={{0,2},{2,0},{4,6},{6,4},{8,10},{10,8},{12,14},{14,12},{16,18},{18,... | collective-permute-start | bytes 4718600 | tf_op jit(solution)/shard_map/ppermute | solution.py:293
  270.5 128.1 %collective-permute-start.11 = (bf16[8,128,768]{2,1,0:T(8,128)(2,1)}, bf16[8,128,768]{2,1,0:T(8,128)(2,1)S(1)}, u32[]{:S(2)}, u32[]{:S(2)}) collective-permute-start(bf16[8,128,768]{2,1,0:T(8,128)(2,1)} %get-tuple-element.31), channel_id=1, source_target_pairs={{0,4},{2,6},{4,0},{6,2},{8,12},{10,14},{12,8},{14,10},{16,20},{18,... | collective-permute-start | bytes 4718600 | tf_op jit(solution)/shard_map/ppermute | solution.py:293
  291.4 107.2 %collective-permute-start.12 = (bf16[8,128,768]{2,1,0:T(8,128)(2,1)}, bf16[8,128,768]{2,1,0:T(8,128)(2,1)S(1)}, u32[]{:S(2)}, u32[]{:S(2)}) collective-permute-start(bf16[8,128,768]{2,1,0:T(8,128)(2,1)} %get-tuple-element.32), channel_id=1, source_target_pairs={{0,6},{2,4},{4,2},{6,0},{8,14},{10,12},{12,10},{14,8},{16,22},{18,... | collective-permute-start | bytes 4718600 | tf_op jit(solution)/shard_map/ppermute | solution.py:293
  331.6 94.7 %collective-permute-start.15 = (bf16[8,128,768]{2,1,0:T(8,128)(2,1)}, bf16[8,128,768]{2,1,0:T(8,128)(2,1)}, u32[]{:S(2)}, u32[]{:S(2)}) collective-permute-start(bf16[8,128,768]{2,1,0:T(8,128)(2,1)} %get-tuple-element.33), channel_id=1, source_target_pairs={{0,2},{2,0},{4,6},{6,4},{8,10},{10,8},{12,14},{14,12},{16,18},{18,... | collective-permute-start | bytes 4718600 | tf_op jit(solution)/shard_map/ppermute | solution.py:293
  331.7 117.5 %collective-permute-start.16 = (bf16[8,128,768]{2,1,0:T(8,128)(2,1)}, bf16[8,128,768]{2,1,0:T(8,128)(2,1)}, u32[]{:S(2)}, u32[]{:S(2)}) collective-permute-start(bf16[8,128,768]{2,1,0:T(8,128)(2,1)} %get-tuple-element.34), channel_id=1, source_target_pairs={{0,4},{2,6},{4,0},{6,2},{8,12},{10,14},{12,8},{14,10},{16,20},{18,... | collective-permute-start | bytes 4718600 | tf_op jit(solution)/shard_map/ppermute | solution.py:293
  358.9 90.4 %collective-permute-start.17 = (bf16[8,128,768]{2,1,0:T(8,128)(2,1)}, bf16[8,128,768]{2,1,0:T(8,128)(2,1)}, u32[]{:S(2)}, u32[]{:S(2)}) collective-permute-start(bf16[8,128,768]{2,1,0:T(8,128)(2,1)} %get-tuple-element.35), channel_id=1, source_target_pairs={{0,6},{2,4},{4,2},{6,0},{8,14},{10,12},{12,10},{14,8},{16,22},{18,... | collective-permute-start | bytes 4718600 | tf_op jit(solution)/shard_map/ppermute | solution.py:293
  398.6 50.7 %copy-start.6 = (bf16[8,128,768]{2,1,0:T(8,128)(2,1)}, bf16[8,128,768]{2,1,0:T(8,128)(2,1)S(1)}, u32[]{:S(2)}) copy-start(bf16[8,128,768]{2,1,0:T(8,128)(2,1)S(1)} %collective-permute-done.11.refs_7_) | copy-start | bytes 4718596
  398.6 50.7 %copy-start.7 = (bf16[8,128,768]{2,1,0:T(8,128)(2,1)}, bf16[8,128,768]{2,1,0:T(8,128)(2,1)S(1)}, u32[]{:S(2)}) copy-start(bf16[8,128,768]{2,1,0:T(8,128)(2,1)S(1)} %collective-permute-done.12.refs_8_) | copy-start | bytes 4718596
  486.6 4.4 collective-permute-start.19
  491.0 1.3 copy-start.3
  498.0 55.9 %all-to-all-start = ((bf16[16,8,64,128]{3,2,1,0:T(8,128)(2,1)}), bf16[16,8,64,128]{3,2,1,0:T(8,128)(2,1)S(1)}, u32[]{:S(2)}, u32[]{:S(2)}) async-start(bf16[16,8,64,128]{3,2,1,0:T(8,128)(2,1)} %bitcast.16), calls=%async_computation | async-start | bytes 4194304 | tf_op jit(solution)/shard_map/all_to_all | solution.py:377
  505.3 4.5 collective-permute-start.18
  553.9 1.3 copy-start.2

commit v2 on v1

--- a/solution.py
+++ b/solution.py
@@ -21,20 +21,45 @@
     return sorted(others, key=lambda p: (abs(p - place), outward * (p - place)))
 
 
-def select_kernel(sources, targets, capacity):
+def select_kernel(phase, sources, targets, capacity):
     def body(info_ref, *refs):
-        ins, outs = refs[:sources], refs[sources : sources + targets]
-        held, came, left = refs[sources + targets :]
+        cols, ins = refs[:sources], refs[sources : 2 * sources]
+        outs = refs[2 * sources : 2 * sources + targets]
+        held, counts, came, left = refs[2 * sources + targets :]
+        row_count, kslots = cols[0].shape
+        plane = targets + 1
+        place, seat = info_ref[0], info_ref[1]
+        for t in range(plane):
+            counts[t] = 0
 
         for k in range(sources):
 
-            @pl.when(info_ref[targets * capacity] == k)
+            @pl.when(info_ref[2 + phase] == k)
             def _(k=k):
-                for t in range(targets):
-                    for c in range(capacity):
-                        panel = info_ref[t * capacity + c]
-                        pltpu.make_async_copy(ins[k].at[panel], held.at[t, c], came.at[t]).start()
-
+                def row_step(i, carry):
+                    for s in range(1, kslots):
+                        owner = cols[k][i, s] // row_count
+                        mask = (owner % plane) ^ seat
+
+                        @pl.when((owner // plane == place) & (mask > 0))
+                        def _():
+                            c = counts[mask]
+                            counts[mask] = c + 1
+                            pltpu.make_async_copy(
+                                ins[k].at[i], held.at[mask - 1, c], came.at[mask - 1]
+                            ).start()
+
+                    return carry
+
+                lax.fori_loop(0, row_count, row_step, 0)
+
+        for t in range(targets):
+
+            def fill(c, carry, t=t):
+                pltpu.make_async_copy(ins[0].at[0], held.at[t, c], came.at[t]).start()
+                return carry
+
+            lax.fori_loop(counts[t + 1], capacity, fill, 0)
         for t in range(targets):
             pltpu.make_async_copy(held.at[t], held.at[t], came.at[t]).wait()
             pltpu.make_async_copy(held.at[t], outs[t], left.at[t]).start()
@@ -44,52 +69,57 @@
     return body
 
 
-def select_panels(info, arrays, targets, capacity):
+def select_panels(phase, info, cols, arrays, targets, capacity):
     _, block_width, samples = arrays[0].shape
     shape = jax.ShapeDtypeStruct((capacity, block_width, samples), arrays[0].dtype)
     moved = 2 * targets * capacity * block_width * samples * 2
     return pl.pallas_call(
-        select_kernel(len(arrays), targets, capacity),
+        select_kernel(phase, len(arrays), targets, capacity),
         out_shape=[shape] * targets,
-        in_specs=[pl.BlockSpec(memory_space=pltpu.SMEM)]
+        in_specs=[pl.BlockSpec(memory_space=pltpu.SMEM)] * (1 + len(cols))
         + [pl.BlockSpec(memory_space=pl.ANY)] * len(arrays),
         out_specs=[pl.BlockSpec(memory_space=pl.ANY)] * targets,
         scratch_shapes=[
             pltpu.VMEM((targets, capacity, block_width, samples), arrays[0].dtype),
+            pltpu.SMEM((targets + 1,), jnp.int32),
             pltpu.SemaphoreType.DMA((targets,)),
             pltpu.SemaphoreType.DMA((targets,)),
         ],
         cost_estimate=pl.CostEstimate(flops=0, transcendentals=0, bytes_accessed=moved),
         name="select_panels",
-    )(info, *arrays)
-
-
-def gram_kernel(layout, kslots, capacity, half_rows):
-    def body(entry_ref, panel_ref, code_ref, omega_ref, own_ref, *refs):
+    )(info, *cols, *arrays)
+
+
+def gather_kernel(layout, kslots, capacity):
+    def body(entry_ref, panel_ref, code_ref, late_ref, omega_ref, own_ref, *refs):
         arrays = refs[: len(layout)]
-        keep_row, keep_col, send_row, send_col, table, sem = refs[len(layout) :]
+        part_ref, rows_ref, table, sem = refs[len(layout) :]
         row = pl.program_id(0)
         block_width = table.shape[1] // kslots
 
+        def place(panel, i, s):
+            at = pl.multiple_of(s * block_width, block_width)
+            pltpu.make_async_copy(panel, table.at[i, pl.ds(at, block_width)], sem.at[i]).start()
+
         def fetch(source, k, c, fixed):
             entry = entry_ref[source * capacity + c]
-            i = entry // kslots
-            s = entry % kslots
             panel = c if fixed else panel_ref[source * capacity + c]
 
             @pl.when(entry >= 0)
             def _():
-                at = pl.multiple_of(s * block_width, block_width)
-                pltpu.make_async_copy(
-                    arrays[k].at[panel], table.at[i, pl.ds(at, block_width)], sem.at[i]
-                ).start()
+                place(arrays[k].at[panel], entry // kslots, entry % kslots)
 
         @pl.when(row == 0)
         def _():
             for i in range(table.shape[0]):
-                pltpu.make_async_copy(
-                    own_ref.at[i], table.at[i, pl.ds(0, block_width)], sem.at[i]
-                ).start()
+                place(own_ref.at[i], i, 0)
+            for i in range(table.shape[0]):
+                for s in range(1, kslots):
+
+                    @pl.when(late_ref[i * kslots + s] >= 0)
+                    def _(i=i, s=s):
+                        place(own_ref.at[i], i, s)
+
             for k, users in enumerate(layout):
                 for source, code in users:
                     if code is None:
@@ -103,71 +133,191 @@
                                 fetch(source, k, c, False)
 
         pltpu.make_async_copy(table.at[row], table.at[row], sem.at[row]).wait()
-        panels = table[row]
-        w_row = jnp.zeros((block_width, panels.shape[1]), jnp.float32)
+        rows_ref[0] = table[row]
+        part = jnp.zeros(part_ref.shape[1:], jnp.float32)
         for s in range(kslots):
-            w_row += jnp.dot(
-                omega_ref[0, s].astype(jnp.bfloat16),
-                panels[s * block_width : (s + 1) * block_width],
+            omega = omega_ref[0, s]
+            if s > 0:
+                omega = jnp.where(late_ref[row * kslots + s] >= 0, 0.0, omega)
+            part += jnp.dot(
+                omega.astype(jnp.bfloat16),
+                table[row, s * block_width : (s + 1) * block_width],
                 preferred_element_type=jnp.float32,
             )
-        w_row = w_row.astype(jnp.bfloat16)
-        contract = (((1,), (1,)), ((), ()))
-        gram = lax.dot_general(w_row, panels, contract, preferred_element_type=jnp.float32)
-        flipped = lax.dot_general(panels, w_row, contract, preferred_element_type=jnp.float32)
-        first = code_ref[code_ref.shape[0] - 1] == 0
-        for s in range(kslots):
-            part = gram[:, s * block_width : (s + 1) * block_width]
-            mine = jnp.where(first, part[:half_rows], part[half_rows:])
-            other = jnp.where(first, part[half_rows:], part[:half_rows])
-            keep_row[0, s] = mine
-            send_row[0, s] = other.astype(jnp.bfloat16)
-            part = flipped[s * block_width : (s + 1) * block_width]
-            mine = jnp.where(first, part[:half_rows], part[half_rows:])
-            other = jnp.where(first, part[half_rows:], part[:half_rows])
-            keep_col[0, s] = mine
-            send_col[0, s] = other.astype(jnp.bfloat16)
+        part_ref[0] = part
 
     return body
 
 
-def grams_of(entries, panel_ids, codes, omega_blocks, own, arrays, layout, capacity, half_rows):
+def gather_early(entries, panel_ids, codes, late, omega_blocks, own, arrays, layout, capacity):
     row_count, kslots, block_width, _ = omega_blocks.shape
     samples = own.shape[2]
-    half = (1, kslots, half_rows, block_width)
-    whole = (row_count, kslots, half_rows, block_width)
-    flops = 6 * row_count * kslots * block_width * block_width * samples
-    spec = pl.BlockSpec(half, lambda i, *_: (i, 0, 0, 0))
+    flops = 2 * row_count * kslots * block_width * block_width * samples
     return pl.pallas_call(
-        gram_kernel(layout, kslots, capacity, half_rows),
-        out_shape=[jax.ShapeDtypeStruct(whole, jnp.float32)] * 2
-        + [jax.ShapeDtypeStruct(whole, jnp.bfloat16)] * 2,
+        gather_kernel(layout, kslots, capacity),
+        out_shape=[
+            jax.ShapeDtypeStruct((row_count, block_width, samples), jnp.float32),
+            jax.ShapeDtypeStruct((row_count, kslots * block_width, samples), jnp.bfloat16),
+        ],
+        grid_spec=pltpu.PrefetchScalarGridSpec(
+            num_scalar_prefetch=4,
+            grid=(row_count,),
+            in_specs=[pl.BlockSpec((1, kslots, block_width, block_width), lambda i, *_: (i, 0, 0, 0))]
+            + [pl.BlockSpec(memory_space=pl.ANY)] * (1 + len(arrays)),
+            out_specs=[
+                pl.BlockSpec((1, block_width, samples), lambda i, *_: (i, 0, 0)),
+                pl.BlockSpec((1, kslots * block_width, samples), lambda i, *_: (i, 0, 0)),
+            ],
+            scratch_shapes=[
+                pltpu.VMEM((row_count, kslots * block_width, samples), jnp.bfloat16),
+                pltpu.SemaphoreType.DMA((row_count,)),
+            ],
+        ),
+        compiler_params=pltpu.CompilerParams(
+            dimension_semantics=("arbitrary",), vmem_limit_bytes=56 << 20
+        ),
+        cost_estimate=pl.CostEstimate(
+            flops=flops,
+            transcendentals=0,
+            bytes_accessed=2 * kslots * row_count * block_width * samples * 2,
+        ),
+        name="gather_early",
+    )(entries, panel_ids, codes, late, omega_blocks, own, *arrays)
+
+
+def gram_kernel(line_count, kslots, capacity, half_rows):
+    def body(panel_ref, code_ref, late_ref, omega_ref, part_ref, rows_ref, *refs):
+        lines = refs[:line_count]
+        came = refs[line_count:-7]
+        grams_ref, send_ref, table, held, w_row, sem, held_sem = refs[-7:]
+        row = pl.program_id(0)
+        block_width = w_row.shape[0]
+
+        @pl.when(row == 0)
+        def _():
+            for k in range(line_count):
+
+                @pl.when(code_ref[0] == k)
+                def _(k=k):
+                    for c in range(capacity):
+                        pltpu.make_async_copy(
+                            lines[k].at[panel_ref[c]], held.at[c], held_sem.at[0]
+                        ).start()
+
+            for mask, block in enumerate(came):
+                at = pl.ds((mask + 1) * capacity, capacity)
+                pltpu.make_async_copy(block, held.at[at], held_sem.at[0]).start()
+            for i in range(table.shape[0]):
+                pltpu.make_async_copy(rows_ref.at[i], table.at[i], sem.at[i]).start()
+            pltpu.make_async_copy(held, held, held_sem.at[0]).wait()
+
+        w_row[...] = part_ref[0]
+        pltpu.make_async_copy(table.at[row], table.at[row], sem.at[row]).wait()
+        for s in range(1, kslots):
+            late = late_ref[row * kslots + s]
+
+            @pl.when(late >= 0)
+            def _(s=s, late=late):
+                panel = held[late]
+                table[row, s * block_width : (s + 1) * block_width] = panel
+                w_row[...] += jnp.dot(
+                    omega_ref[0, s].astype(jnp.bfloat16),
+                    panel,
+                    preferred_element_type=jnp.float32,
+                )
+
+        flipped = lax.dot_general(
+            table[row],
+            w_row[...].astype(jnp.bfloat16),
+            (((1,), (1,)), ((), ())),
+            preferred_element_type=jnp.float32,
+        )
+        first = code_ref[1] == 0
+        for s in range(kslots):
+            block = flipped[s * block_width : (s + 1) * block_width]
+            grams_ref[0, s] = block
+            send_ref[0, s] = jnp.where(first, block[half_rows:], block[:half_rows]).astype(
+                jnp.bfloat16
+            )
+
+    return body
+
+
+def grams_of(panel_ids, codes, late, omega_blocks, part, rows, lines, came, capacity, half_rows):
+    row_count, kslots, block_width, _ = omega_blocks.shape
+    samples = part.shape[2]
+    flops = 2 * row_count * kslots * block_width * block_width * samples
+    return pl.pallas_call(
+        gram_kernel(len(lines), kslots, capacity, half_rows),
+        out_shape=[
+            jax.ShapeDtypeStruct(omega_blocks.shape, jnp.float32),
+            jax.ShapeDtypeStruct((row_count, kslots, half_rows, block_width), jnp.bfloat16),
+        ],
         grid_spec=pltpu.PrefetchScalarGridSpec(
             num_scalar_prefetch=3,
             grid=(row_count,),
-            in_specs=[pl.BlockSpec((1, kslots, block_width, block_width), lambda i, *_: (i, 0, 0, 0))]
-            + [pl.BlockSpec(memory_space=pl.ANY)] * (1 + len(arrays)),
-            out_specs=[spec] * 4,
+            in_specs=[
+                pl.BlockSpec((1, kslots, block_width, block_width), lambda i, *_: (i, 0, 0, 0)),
+                pl.BlockSpec((1, block_width, samples), lambda i, *_: (i, 0, 0)),
+            ]
+            + [pl.BlockSpec(memory_space=pl.ANY)] * (1 + len(lines) + len(came)),
+            out_specs=[
+                pl.BlockSpec((1, kslots, block_width, block_width), lambda i, *_: (i, 0, 0, 0)),
+                pl.BlockSpec((1, kslots, half_rows, block_width), lambda i, *_: (i, 0, 0, 0)),
+            ],
             scratch_shapes=[
                 pltpu.VMEM((row_count, kslots * block_width, samples), jnp.bfloat16),
+                pltpu.VMEM(((1 + len(came)) * capacity, block_width, samples), jnp.bfloat16),
+                pltpu.VMEM((block_width, samples), jnp.float32),
                 pltpu.SemaphoreType.DMA((row_count,)),
+                pltpu.SemaphoreType.DMA((1,)),
             ],
         ),
         compiler_params=pltpu.CompilerParams(
             dimension_semantics=("arbitrary",), vmem_limit_bytes=56 << 20
         ),
         cost_estimate=pl.CostEstimate(
-            flops=flops, transcendentals=0, bytes_accessed=(kslots * row_count + 64) * block_width * samples * 2
+            flops=flops,
+            transcendentals=0,
+            bytes_accessed=(kslots + 4) * row_count * block_width * samples * 2,
         ),
         name="grams",
-    )(entries, panel_ids, codes, omega_blocks, own, *arrays)
+    )(panel_ids, codes, late, omega_blocks, part, rows, *lines, *came)
+
+
+def turn_kernel(part_ref, grams_ref, keep_ref, send_ref):
+    first = part_ref[0] == 0
+    half_rows = keep_ref.shape[2]
+    for s in range(keep_ref.shape[1]):
+        turned = grams_ref[0, s].T
+        low, high = turned[:half_rows], turned[half_rows:]
+        keep_ref[0, s] = jnp.where(first, low, high)
+        send_ref[0, s] = jnp.where(first, high, low).astype(jnp.bfloat16)
+
+
+def turned_halves(sample_part, grams, half_rows):
+    row_count, kslots, block_width, _ = grams.shape
+    spec = pl.BlockSpec((1, kslots, half_rows, block_width), lambda i, *_: (i, 0, 0, 0))
+    shape = (row_count, kslots, half_rows, block_width)
+    return pl.pallas_call(
+        turn_kernel,
+        out_shape=[jax.ShapeDtypeStruct(shape, jnp.float32), jax.ShapeDtypeStruct(shape, jnp.bfloat16)],
+        grid_spec=pltpu.PrefetchScalarGridSpec(
+            num_scalar_prefetch=1,
+            grid=(row_count,),
+            in_specs=[pl.BlockSpec((1,) + grams.shape[1:], lambda i, *_: (i, 0, 0, 0))],
+            out_specs=[spec, spec],
+        ),
+        compiler_params=pltpu.CompilerParams(dimension_semantics=("arbitrary",)),
+        name="turn",
+    )(sample_part.reshape(1), grams)
 
 
 def rows_per_step(row_count):
     return 4 if row_count % 4 == 0 else 1
 
 
-def outgoing_kernel(slot_ref, keep_ref, came_ref, own_ref, out_ref):
+def outgoing_kernel(slot_ref, half_ref, keep_ref, came_ref, own_ref, out_ref):
     rows, kslots = keep_ref.shape[:2]
     first = pl.program_id(0) * rows
     for r in range(rows):
@@ -177,8 +327,8 @@
             out_ref[slot_ref[(first + r) * kslots + s]] = summed.astype(jnp.bfloat16)
 
 
-def outgoing_blocks(slots, keep_col, came_col, slot_count):
-    row_count, kslots, half_rows, block_width = keep_col.shape
+def outgoing_blocks(slots, sample_part, grams, came_col, slot_count):
+    row_count, kslots, half_rows, block_width = came_col.shape
     rows = rows_per_step(row_count)
     spec = pl.BlockSpec((rows, kslots, half_rows, block_width), lambda i, *_: (i, 0, 0, 0))
     return pl.pallas_call(
@@ -188,9 +338,15 @@
             jax.ShapeDtypeStruct((slot_count, half_rows, block_width), jnp.bfloat16),
         ],
         grid_spec=pltpu.PrefetchScalarGridSpec(
-            num_scalar_prefetch=1,
+            num_scalar_prefetch=2,
             grid=(row_count // rows,),
-            in_specs=[spec, spec],
+            in_specs=[
+                pl.BlockSpec(
+                    (rows, kslots, half_rows, block_width),
+                    lambda i, slot, half: (i, 0, half[0], 0),
+                ),
+                spec,
+            ],
             out_specs=[
                 pl.BlockSpec((rows, half_rows, block_width), lambda i, *_: (i, 0, 0)),
                 pl.BlockSpec((slot_count, half_rows, block_width), lambda i, *_: (0, 0, 0)),
@@ -198,7 +354,7 @@
         ),
         compiler_params=pltpu.CompilerParams(dimension_semantics=("arbitrary",)),
         name="outgoing",
-    )(slots, keep_col, came_col)
+    )(slots, sample_part.reshape(1), grams, came_col)
 
 
 def final_kernel(scale):
@@ -294,21 +450,22 @@
 
     order = [[p] + arrivals(p, length) for p in range(length)]
     offsets = [[order[p][m] - p for p in range(length)] for m in range(length)]
+    choices = [sorted(set(offsets[m])) for m in range(length)]
     sources = jnp.array(order, jnp.int32)[place]
-
-    all_cols = lax.all_gather(block_cols, "vars", axis=0, tiled=False)
-    panels, all_cols = lax.optimization_barrier((panels, all_cols))
-
-    source_cols = all_cols[sources * plane + seat].reshape(length, entries)
+    facts = [
+        [p, b] + [choices[m].index(offsets[m][p]) for m in range(length)]
+        for p in range(length)
+        for b in range(plane)
+    ]
+    info = lax.dynamic_slice_in_dim(jnp.array(facts, jnp.int32), me, 1, 0)[0]
+
+    came_cols = {0: block_cols}
+    for m in range(1, length):
+        for step in (-1, 1):
+            came_cols[step * m] = along(came_cols[step * (m - 1)], -step)
+
     entry_ids = jnp.arange(entries, dtype=jnp.int32)
     remote = entry_ids % kslots != 0
-    targets = place * plane + (seat ^ jnp.arange(1, plane, dtype=jnp.int32))
-    hits = (source_cols[:, None, :] // row_count == targets[None, :, None]) & remote
-    before = ranks_among(hits[:, :, None, :], jnp.broadcast_to(entry_ids, hits.shape))
-    chosen = hits[:, :, None, :] & (
-        before[:, :, None, :] == jnp.arange(capacity, dtype=jnp.int32)[None, None, :, None]
-    )
-    picks = jnp.sum(jnp.where(chosen, entry_ids // kslots, 0), axis=-1).reshape(length, -1)
 
     flat_cols = block_cols.reshape(entries)
     owners = flat_cols // row_count
@@ -329,51 +486,70 @@
     entry_table = (jnp.sum(jnp.where(wanted, entry_ids + 1, 0), axis=-1) - 1).reshape(-1)
     panel_table = jnp.sum(jnp.where(wanted, flat_cols % row_count, 0), axis=-1).reshape(-1)
 
+    late_hit = remote & (owners // plane == sources[-1])
+    late = jnp.where(late_hit, ((owners % plane) ^ seat) * capacity + key_rank, -1)
+
     came = {0: panels}
     received = []
-    codes = []
     for m in range(length):
         if m > 0:
             for step in (-1, 1):
                 came[step * m] = along(came[step * (m - 1)], -step)
-        options = sorted(set(offsets[m]))
-        code = jnp.array([options.index(o) for o in offsets[m]], jnp.int32)[place]
-        codes.append((options, code))
-        info = jnp.concatenate([picks[m], code[None]])
-        sent = select_panels(info, [came[o] for o in options], plane - 1, capacity)
+        sent = select_panels(
+            m,
+            info,
+            [came_cols[o] for o in choices[m]],
+            [came[o] for o in choices[m]],
+            plane - 1,
+            capacity,
+        )
         received.append([across(block, mask + 1) for mask, block in enumerate(sent)])
 
-    arrays, layout, code_values = [], [], [jnp.int32(0)] * (length * plane + 1)
-    line_users = {}
-    for m in range(length):
+    last = length - 1
+    arrays, layout, line_users = [], [], {}
+    code_values = [jnp.int32(0)] * (last * plane)
+    for m in range(last):
         for mask in range(1, plane):
             arrays.append(received[m][mask - 1])
             layout.append([(m * plane + mask, None)])
         if m > 0:
-            options, code = codes[m]
-            code_values[m * plane] = code
-            for number, option in enumerate(options):
+            code_values[m * plane] = info[2 + m]
+            for number, option in enumerate(choices[m]):
                 line_users.setdefault(option, []).append((m * plane, number))
     for option in sorted(line_users):
         arrays.append(came[option])
         layout.append(line_users[option])
-    code_values[-1] = sample_part
-    keep_row, keep_col, send_row, send_col = grams_of(
-        entry_table,
-        panel_table,
+    early = last * plane * capacity
+    part, rows = gather_early(
+        entry_table[:early],
+        panel_table[:early],
         jnp.stack(code_values),
+        late,
         omega_blocks,
         panels,
         arrays,
         layout,
         capacity,
+    )
+    grams, send_col = grams_of(
+        panel_table[early : early + capacity],
+        jnp.stack([info[2 + last], sample_part]),
+        late,
+        omega_blocks,
+        part,
+        rows,
+        [came[o] for o in choices[last]],
+        received[last],
+        capacity,
         half_rows,
     )
 
     swap = [(k, samp_count - 1 - k) for k in range(samp_count)]
     came_col = lax.ppermute(send_col, "samp", swap)
-    came_row = lax.ppermute(send_row, "samp", swap)
-    own_col, outgoing = outgoing_blocks(mirror_out, keep_col, came_col, devices * capacity)
+    own_col, outgoing = outgoing_blocks(
+        mirror_out, sample_part, grams, came_col, devices * capacity
+    )
+    outgoing, grams = lax.optimization_barrier((outgoing, grams))
     incoming = lax.all_to_all(
         outgoing.reshape(devices, capacity, half_rows, block_width),
         "vars",
@@ -381,6 +557,8 @@
         concat_axis=0,
         tiled=True,
     ).reshape(devices * capacity, half_rows, block_width)
+    keep_row, send_row = turned_halves(sample_part, grams, half_rows)
+    came_row = lax.ppermute(send_row, "samp", swap)
     return tuple(
         final_step(
             mirror_in,

time: 565 us -> 615 us (1.088)
  waiting for transfers between devices: 382 us -> 424 us
  Pallas kernels: 73.8 us -> 113 us
  blocking collectives: 28.6 us -> 0 us
    ppermute x6 -> x12, waiting for transfers between devices: 121 us -> 176 us  [along(): return lax.ppermute(array, 'vars', pairs)]
    pallas_call x5 -> x7, Pallas kernels: 58.6 us -> 97.8 us  [the longest x1 32.8 us: grams_of(): pl.pallas_call(gram_kernel(len(lines), kslots, capacity, half_rows), out_...]
    all_gather x1 -> x0, blocking collectives: 28.6 us -> none  [step_on_device(): all_cols = lax.all_gather(block_cols, 'vars', axis=0, tiled=False)]
    ppermute x12, starting transfers between devices: 28.4 us -> 13.1 us  [across(): return lax.ppermute(array, 'vars', pairs)]
    ppermute x6 -> x12, starting transfers between devices: 27 us -> 41.2 us  [along(): return lax.ppermute(array, 'vars', pairs)]
    all_to_all x1, waiting for transfers between devices: 44.2 us -> 31.1 us  [step_on_device(): lax.all_to_all(outgoing.reshape(devices, capacity, half_rows, block_width...]
  transfers between devices with their start and end apart: 21 -> 27, of which waited for: 13 -> 10; matrix products, arithmetic and copies ran while one was open for 2% -> 2% of each run, Pallas kernels for 4% -> 11%
where the time goes in v2:
time: 615 us; the launch traced here: 613 us
  waiting for transfers between devices  424 us (69%)
  Pallas kernels  113 us (18%)
  starting transfers between devices  59.5 us (10%)
  local copies, waits for them, and re-layouts  11.4 us (2%)
    ppermute x12, waiting for transfers between devices, across(): return lax.ppermute(array, 'vars', pairs)  208 us
    ppermute x12, waiting for transfers between devices, along(): return lax.ppermute(array, 'vars', pairs)  176 us
    ppermute x12, starting transfers between devices, along(): return lax.ppermute(array, 'vars', pairs)  41.2 us
    pallas_call x1, Pallas kernels, grams_of(): pl.pallas_call(gram_kernel(len(lines), kslots, capacity, half_rows), out_...  32.8 us
    all_to_all x1, waiting for transfers between devices, step_on_device(): lax.all_to_all(outgoing.reshape(devices, capacity, half_rows, block_width...  31.1 us
    pallas_call x1, Pallas kernels, gather_early(): pl.pallas_call(gather_kernel(layout, kslots, capacity), out_shape=[jax.Sh...  27.3 us
    pallas_call x4, Pallas kernels, select_panels(): pl.pallas_call(select_kernel(phase, len(arrays), targets, capacity), out_...  24.9 us
    ppermute x12, starting transfers between devices, across(): return lax.ppermute(array, 'vars', pairs)  13.1 us
  transfers between devices with their start and end apart: 27, of which 10 were waited for; matrix products, arithmetic and copies ran while one was open for 2% of the time, Pallas kernels for 11%

profile of v2, /device:TPU:14, one launch (start us, length us, event | category | flops | bytes accessed | tf_op | source)
XLA Modules:
  0.0 612.8 jit_solution(16207260844547308551)
XLA Ops:
  0.6 3.5 collective-permute-start.5
  4.1 4.0 collective-permute-start.6
  8.1 64.6 %collective-permute-done.5.refs_2_.refs_5_.refs_10_ = bf16[16,128,768]{2,1,0:T(8,128)(2,1)} collective-permute-done((bf16[16,128,768]{2,1,0:T(8,128)(2,1)}, bf16[16,128,768]{2,1,0:T(8,128)(2,1)}, u32[]{:S(2)}, u32[]{:S(2)}) %collective-permute-start.5) | collective-permute-done | bytes 3145760 | tf_op jit(solution)/shard_map/ppermute | solution.py:445
  72.7 3.5 collective-permute-start.12
  76.2 3.7 collective-permute-start.13
  79.9 1.4 copy.15.refs_0_
  81.2 1.2 fusion.6
  82.4 6.1 select_panels.4
  89.2 54.6 %collective-permute-done.12.refs_4_.refs_9_.refs_5_.refs_1_ = bf16[16,128,768]{2,1,0:T(8,128)(2,1)S(1)} collective-permute-done((bf16[16,128,768]{2,1,0:T(8,128)(2,1)}, bf16[16,128,768]{2,1,0:T(8,128)(2,1)S(1)}, u32[]{:S(2)}, u32[]{:S(2)}) %collective-permute-start.12) | collective-permute-done | bytes 3145760 | tf_op jit(solution)/shard_map/ppermute | solution.py:445
  143.8 3.5 collective-permute-start.17
  147.3 4.0 collective-permute-start.18
  151.3 1.9 collective-permute-start.3
  153.2 3.9 collective-permute-start.4
  157.1 56.9 %collective-permute-done.3.refs_0_.refs_1_ = s32[16,8]{1,0:T(8,128)S(1)} collective-permute-done((s32[16,8]{1,0:T(8,128)S(1)}, s32[16,8]{1,0:T(8,128)S(1)}, u32[]{:S(2)}, u32[]{:S(2)}) %collective-permute-start.3) | collective-permute-done | bytes 544 | tf_op jit(solution)/shard_map/ppermute | solution.py:445
  214.1 3.5 collective-permute-start.10
  217.6 3.9 collective-permute-start.11
  221.5 1.9 collective-permute-start.19
  223.5 3.9 collective-permute-start.20
  227.4 5.9 select_panels.5
  233.9 1.5 collective-permute-start.2
  235.4 1.5 collective-permute-start.7
  236.9 6.4 %select_panels.6 = (bf16[8,128,768]{2,1,0:T(8,128)(2,1)}, bf16[8,128,768]{2,1,0:T(8,128)(2,1)}, bf16[8,128,768]{2,1,0:T(8,128)(2,1)}) custom-call(s32[6]{0:T(128)} %get-tuple-element.50.info_ref, s32[16,8]{1,0:T(8,128)} %copy-done.6, s32[16,8]{1,0:T(8,128)} %copy-done.8, s32[16,8]{1,0:T(8,128)} %copy-done.9, s32[16,8]{1,0:T(8,128)} %copy-done.7, ...), custom_call_target="tpu_custom_call" | custom-call | bytes 9437184 | tf_op jit(solution)/shard_map/select_panels/pallas_call | solution.py:76
  243.3 56.7 %collective-permute-done.1.refs_1_ = bf16[8,128,768]{2,1,0:T(8,128)(2,1)} collective-permute-done((bf16[8,128,768]{2,1,0:T(8,128)(2,1)}, bf16[8,128,768]{2,1,0:T(8,128)(2,1)}, u32[]{:S(2)}, u32[]{:S(2)}) %collective-permute-start.1) | collective-permute-done | bytes 1572896 | tf_op jit(solution)/shard_map/ppermute | solution.py:449
  300.6 1.5 collective-permute-start.9
  302.1 1.5 collective-permute-start.14
  303.7 0.7 constant_dynamic-slice_fusion.1
  305.2 1.5 collective-permute-start.16
  306.7 6.5 %select_panels.7 = (bf16[8,128,768]{2,1,0:T(8,128)(2,1)}, bf16[8,128,768]{2,1,0:T(8,128)(2,1)}, bf16[8,128,768]{2,1,0:T(8,128)(2,1)}) custom-call(s32[6]{0:T(128)} %get-tuple-element.50.info_ref, s32[16,8]{1,0:T(8,128)} %copy-done.10, s32[16,8]{1,0:T(8,128)} %copy-done.6, s32[16,8]{1,0:T(8,128)} %copy-done.7, s32[16,8]{1,0:T(8,128)} %copy-done.11, ...), custom_call_target="tpu_custom_call" | custom-call | bytes 9437184 | tf_op jit(solution)/shard_map/select_panels/pallas_call | solution.py:76
  313.2 59.6 %collective-permute-done.8.refs_4_ = bf16[8,128,768]{2,1,0:T(8,128)(2,1)} collective-permute-done((bf16[8,128,768]{2,1,0:T(8,128)(2,1)}, bf16[8,128,768]{2,1,0:T(8,128)(2,1)}, u32[]{:S(2)}, u32[]{:S(2)}) %collective-permute-start.8) | collective-permute-done | bytes 1572896 | tf_op jit(solution)/shard_map/ppermute | solution.py:449
  373.4 1.3 collective-permute-start.22
  374.6 1.7 collective-permute-start.23
  379.6 1.9 stack.8.code_ref
  381.4 1.2 pad_add_fusion.code_ref
  382.6 1.2 and_select_fusion.3
  384.4 55.8 %collective-permute-done.15.refs_7_ = bf16[8,128,768]{2,1,0:T(8,128)(2,1)S(1)} collective-permute-done((bf16[8,128,768]{2,1,0:T(8,128)(2,1)}, bf16[8,128,768]{2,1,0:T(8,128)(2,1)S(1)}, u32[]{:S(2)}, u32[]{:S(2)}) %collective-permute-start.15) | collective-permute-done | bytes 1572896 | tf_op jit(solution)/shard_map/ppermute | solution.py:449
  440.1 1.1 copy-done.3
  441.3 27.3 %gather_early.1 = (f32[16,128,768]{2,1,0:T(8,128)}, bf16[16,1024,768]{2,1,0:T(8,128)(2,1)}) custom-call(s32[96]{0:T(128)} %slice.46.entry_ref, s32[96]{0:T(128)} %slice.48.panel_ref, s32[12]{0:T(128)} %stack.8.code_ref, s32[128]{0:T(128)} %get-tuple-element.54.late_ref, f32[16,8,128,128]{3,2,1,0:T(8,128)} %omega_ref.5, bf16[16,128,768]{2,1,0:T(8,128)(2,1)} %bitcast.18, ...), custom_call_target="tpu_custom_call" | custom-call | flops 3221225472 | bytes 50331648 | tf_op jit(solution)/shard_map/gather_early/pallas_call | solution.py:156
  468.6 35.5 %collective-permute-done.22.refs_5_ = bf16[8,128,768]{2,1,0:T(8,128)(2,1)} collective-permute-done((bf16[8,128,768]{2,1,0:T(8,128)(2,1)}, bf16[8,128,768]{2,1,0:T(8,128)(2,1)}, u32[]{:S(2)}, u32[]{:S(2)}) %collective-permute-start.22) | collective-permute-done | bytes 1572896 | tf_op jit(solution)/shard_map/ppermute | solution.py:449
  504.1 32.8 %grams.1 = (f32[16,8,128,128]{3,2,1,0:T(8,128)}, bf16[16,8,64,128]{3,2,1,0:T(8,128)(2,1)}) custom-call(s32[8]{0:T(128)} %slice_bitcast_fusion.panel_ref, s32[2]{0:T(128)} %pad_add_fusion.code_ref, s32[128]{0:T(128)} %get-tuple-element.54.late_ref, f32[16,8,128,128]{3,2,1,0:T(8,128)} %omega_ref.5, f32[16,128,768]{2,1,0:T(8,128)} %get-tuple-element.33.part_ref, ...), custom_call_target="tpu_custom_call" | custom-call | flops 3221225472 | bytes 37748736 | tf_op jit(solution)/shard_map/grams/pallas_call | solution.py:250
  537.0 4.4 collective-permute-done.24.came_ref
  541.4 1.3 copy-done.2
  542.7 5.7 outgoing.1
  548.4 5.1 all-to-all-start
  553.5 12.7 %turn.1 = (f32[16,8,64,128]{3,2,1,0:T(8,128)}, bf16[16,8,64,128]{3,2,1,0:T(8,128)(2,1)}) custom-call(s32[1]{0:T(128)} %bitcast.half_ref.part_ref, f32[16,8,128,128]{3,2,1,0:T(8,128)} %get-tuple-element.41.keep_ref.grams_ref), custom_call_target="tpu_custom_call" | custom-call | tf_op jit(solution)/shard_map/turn/pallas_call | solution.py:302
  566.2 4.5 collective-permute-done.25.came_ref
  570.7 31.1 %all-to-all-done = bf16[16,8,64,128]{3,2,1,0:T(8,128)(2,1)S(1)} async-done(((bf16[16,8,64,128]{3,2,1,0:T(8,128)(2,1)}), bf16[16,8,64,128]{3,2,1,0:T(8,128)(2,1)S(1)}, u32[]{:S(2)}, u32[]{:S(2)}) %all-to-all-start) | async-done | bytes 2097184 | tf_op jit(solution)/shard_map/all_to_all | solution.py:553
  601.8 1.4 copy-done.1
  603.2 9.6 %final_step.1 = (f32[16,8,64,128]{3,2,1,0:T(8,128)}, f32[16,8,64,128]{3,2,1,0:T(8,128)}) custom-call(s32[128]{0:T(128)} %get-tuple-element.59.slot_ref, s32[1]{0:T(128)} %bitcast.half_ref.part_ref, f32[16,8,64,128]{3,2,1,0:T(8,128)} %get-tuple-element.42.keep_ref, bf16[16,8,64,128]{3,2,1,0:T(8,128)(2,1)} %collective-permute-done.25.came_ref, ...), custom_call_target="tpu_custom_call" | custom-call | tf_op jit(solution)/shard_map/final_step/pallas_call | solution.py:395
  (64 shorter events, 7.0 us)
Async XLA Ops:
  0.6 72.1 %collective-permute-start.5 = (bf16[16,128,768]{2,1,0:T(8,128)(2,1)}, bf16[16,128,768]{2,1,0:T(8,128)(2,1)}, u32[]{:S(2)}, u32[]{:S(2)}) collective-permute-start(bf16[16,128,768]{2,1,0:T(8,128)(2,1)} %bitcast.15), channel_id=1, source_target_pairs={{0,8},{2,10},{4,12},{6,14},{8,16},{10,18},{12,20},{14,22},{16,24},... | collective-permute-start | bytes 9437192 | tf_op jit(solution)/shard_map/ppermute | solution.py:445
  4.1 72.0 %collective-permute-start.6 = (bf16[16,128,768]{2,1,0:T(8,128)(2,1)}, bf16[16,128,768]{2,1,0:T(8,128)(2,1)}, u32[]{:S(2)}, u32[]{:S(2)}) collective-permute-start(bf16[16,128,768]{2,1,0:T(8,128)(2,1)} %bitcast.16), channel_id=1, source_target_pairs={{8,0},{10,2},{12,4},{14,6},{16,8},{18,10},{20,12},{22,14},{24,16},... | collective-permute-start | bytes 9437192 | tf_op jit(solution)/shard_map/ppermute | solution.py:445
  72.7 71.1 %collective-permute-start.12 = (bf16[16,128,768]{2,1,0:T(8,128)(2,1)}, bf16[16,128,768]{2,1,0:T(8,128)(2,1)S(1)}, u32[]{:S(2)}, u32[]{:S(2)}) collective-permute-start(bf16[16,128,768]{2,1,0:T(8,128)(2,1)} %collective-permute-done.5.refs_2_.refs_5_.refs_10_), channel_id=1, source_target_pairs={{0,8},{2,10},{4,12},{6,14},{8,16},{10,18},{12,20},{14,22},{16,24},... | collective-permute-start | bytes 9437192 | tf_op jit(solution)/shard_map/ppermute | solution.py:445
  76.2 71.1 %collective-permute-start.13 = (bf16[16,128,768]{2,1,0:T(8,128)(2,1)}, bf16[16,128,768]{2,1,0:T(8,128)(2,1)}, u32[]{:S(2)}, u32[]{:S(2)}) collective-permute-start(bf16[16,128,768]{2,1,0:T(8,128)(2,1)} %collective-permute-done.6.refs_3_.refs_6_.refs_11_), channel_id=1, source_target_pairs={{8,0},{10,2},{12,4},{14,6},{16,8},{18,10},{20,12},{22,14},{24,16},... | collective-permute-start | bytes 9437192 | tf_op jit(solution)/shard_map/ppermute | solution.py:445
  82.4 68.8 %copy-start.5 = (s32[16,8]{1,0:T(8,128)S(1)}, s32[16,8]{1,0:T(8,128)}, u32[]{:S(2)}) copy-start(s32[16,8]{1,0:T(8,128)} %copy.15.refs_0_) | copy-start | bytes 1540
  88.6 146.8 %collective-permute-start = (bf16[8,128,768]{2,1,0:T(8,128)(2,1)}, bf16[8,128,768]{2,1,0:T(8,128)(2,1)}, u32[]{:S(2)}, u32[]{:S(2)}) collective-permute-start(bf16[8,128,768]{2,1,0:T(8,128)(2,1)} %get-tuple-element.24), channel_id=1, source_target_pairs={{0,2},{2,0},{4,6},{6,4},{8,10},{10,8},{12,14},{14,12},{16,18},{18,... | collective-permute-start | bytes 4718600 | tf_op jit(solution)/shard_map/ppermute | solution.py:449
  143.8 89.5 %copy-start = (bf16[16,128,768]{2,1,0:T(8,128)(2,1)}, bf16[16,128,768]{2,1,0:T(8,128)(2,1)S(1)}, u32[]{:S(2)}) copy-start(bf16[16,128,768]{2,1,0:T(8,128)(2,1)S(1)} %collective-permute-done.12.refs_4_.refs_9_.refs_5_.refs_1_) | copy-start | bytes 9437188
  143.8 160.9 %collective-permute-start.17 = (bf16[16,128,768]{2,1,0:T(8,128)(2,1)S(1)}, bf16[16,128,768]{2,1,0:T(8,128)(2,1)}, u32[]{:S(2)}, u32[]{:S(2)}) collective-permute-start(bf16[16,128,768]{2,1,0:T(8,128)(2,1)S(1)} %collective-permute-done.12.refs_4_.refs_9_.refs_5_.refs_1_), channel_id=1, source_target_pairs={{0,8},{2,10},{4,12},{6,14},{8,16},{10,18},{12,20},{14,22},{16,24},... | collective-permute-start | bytes 9437192 | tf_op jit(solution)/shard_map/ppermute | solution.py:445
  147.3 157.9 %collective-permute-start.18 = (bf16[16,128,768]{2,1,0:T(8,128)(2,1)}, bf16[16,128,768]{2,1,0:T(8,128)(2,1)}, u32[]{:S(2)}, u32[]{:S(2)}) collective-permute-start(bf16[16,128,768]{2,1,0:T(8,128)(2,1)} %collective-permute-done.13.refs_7_.refs_12_.refs_6_.refs_2_), channel_id=1, source_target_pairs={{8,0},{10,2},{12,4},{14,6},{16,8},{18,10},{20,12},{22,14},{24,16},... | collective-permute-start | bytes 9437192 | tf_op jit(solution)/shard_map/ppermute | solution.py:445
  151.3 62.8 %collective-permute-start.3 = (s32[16,8]{1,0:T(8,128)S(1)}, s32[16,8]{1,0:T(8,128)S(1)}, u32[]{:S(2)}, u32[]{:S(2)}) collective-permute-start(s32[16,8]{1,0:T(8,128)S(1)} %copy-done.5), channel_id=1, source_target_pairs={{0,8},{2,10},{4,12},{6,14},{8,16},{10,18},{12,20},{14,22},{16,24},... | collective-permute-start | bytes 1544 | tf_op jit(solution)/shard_map/ppermute | solution.py:445
  153.2 64.4 %collective-permute-start.4 = (s32[16,8]{1,0:T(8,128)S(1)}, s32[16,8]{1,0:T(8,128)S(1)}, u32[]{:S(2)}, u32[]{:S(2)}) collective-permute-start(s32[16,8]{1,0:T(8,128)S(1)} %copy-done.5), channel_id=1, source_target_pairs={{8,0},{10,2},{12,4},{14,6},{16,8},{18,10},{20,12},{22,14},{24,16},... | collective-permute-start | bytes 1544 | tf_op jit(solution)/shard_map/ppermute | solution.py:445
  214.1 13.3 %copy-start.8 = (s32[16,8]{1,0:T(8,128)}, s32[16,8]{1,0:T(8,128)S(1)}, u32[]{:S(2)}) copy-start(s32[16,8]{1,0:T(8,128)S(1)} %collective-permute-done.3.refs_0_.refs_1_) | copy-start | bytes 1540
  214.1 7.4 %collective-permute-start.10 = (s32[16,8]{1,0:T(8,128)S(1)}, s32[16,8]{1,0:T(8,128)S(1)}, u32[]{:S(2)}, u32[]{:S(2)}) collective-permute-start(s32[16,8]{1,0:T(8,128)S(1)} %collective-permute-done.3.refs_0_.refs_1_), channel_id=1, source_target_pairs={{0,8},{2,10},{4,12},{6,14},{8,16},{10,18},{12,20},{14,22},{16,24},... | collective-permute-start | bytes 1544 | tf_op jit(solution)/shard_map/ppermute | solution.py:445
  217.6 9.8 %copy-start.9 = (s32[16,8]{1,0:T(8,128)}, s32[16,8]{1,0:T(8,128)S(1)}, u32[]{:S(2)}) copy-start(s32[16,8]{1,0:T(8,128)S(1)} %collective-permute-done.4.refs_1_.refs_2_) | copy-start | bytes 1540
  217.6 5.9 collective-permute-start.11
  221.5 11.8 %copy-start.6 = (s32[16,8]{1,0:T(8,128)}, s32[16,8]{1,0:T(8,128)S(1)}, u32[]{:S(2)}) copy-start(s32[16,8]{1,0:T(8,128)S(1)} %collective-permute-done.10.refs_0_.refs_1_) | copy-start | bytes 1540
  221.5 11.8 %collective-permute-start.19 = (s32[16,8]{1,0:T(8,128)S(1)}, s32[16,8]{1,0:T(8,128)S(1)}, u32[]{:S(2)}, u32[]{:S(2)}) collective-permute-start(s32[16,8]{1,0:T(8,128)S(1)} %collective-permute-done.10.refs_0_.refs_1_), channel_id=1, source_target_pairs={{0,8},{2,10},{4,12},{6,14},{8,16},{10,18},{12,20},{14,22},{16,24},... | collective-permute-start | bytes 1544 | tf_op jit(solution)/shard_map/ppermute | solution.py:445
  223.5 9.8 %copy-start.7 = (s32[16,8]{1,0:T(8,128)}, s32[16,8]{1,0:T(8,128)S(1)}, u32[]{:S(2)}) copy-start(s32[16,8]{1,0:T(8,128)S(1)} %collective-permute-done.11.refs_3_.refs_2_) | copy-start | bytes 1540
  223.5 10.4 %collective-permute-start.20 = (s32[16,8]{1,0:T(8,128)S(1)}, s32[16,8]{1,0:T(8,128)S(1)}, u32[]{:S(2)}, u32[]{:S(2)}) collective-permute-start(s32[16,8]{1,0:T(8,128)S(1)} %collective-permute-done.11.refs_3_.refs_2_), channel_id=1, source_target_pairs={{8,0},{10,2},{12,4},{14,6},{16,8},{18,10},{20,12},{22,14},{24,16},... | collective-permute-start | bytes 1544 | tf_op jit(solution)/shard_map/ppermute | solution.py:445
  233.3 10.0 %copy-start.10 = (s32[16,8]{1,0:T(8,128)}, s32[16,8]{1,0:T(8,128)S(1)}, u32[]{:S(2)}) copy-start(s32[16,8]{1,0:T(8,128)S(1)} %collective-permute-done.19.refs_0_) | copy-start | bytes 1540
  233.3 66.7 %collective-permute-start.1 = (bf16[8,128,768]{2,1,0:T(8,128)(2,1)}, bf16[8,128,768]{2,1,0:T(8,128)(2,1)}, u32[]{:S(2)}, u32[]{:S(2)}) collective-permute-start(bf16[8,128,768]{2,1,0:T(8,128)(2,1)} %get-tuple-element.25), channel_id=1, source_target_pairs={{0,4},{2,6},{4,0},{6,2},{8,12},{10,14},{12,8},{14,10},{16,20},{18,... | collective-permute-start | bytes 4718600 | tf_op jit(solution)/shard_map/ppermute | solution.py:449
  233.9 9.4 %copy-start.11 = (s32[16,8]{1,0:T(8,128)}, s32[16,8]{1,0:T(8,128)S(1)}, u32[]{:S(2)}) copy-start(s32[16,8]{1,0:T(8,128)S(1)} %collective-permute-done.20.refs_3_) | copy-start | bytes 1540
  233.9 66.7 %collective-permute-start.2 = (bf16[8,128,768]{2,1,0:T(8,128)(2,1)}, bf16[8,128,768]{2,1,0:T(8,128)(2,1)}, u32[]{:S(2)}, u32[]{:S(2)}) collective-permute-start(bf16[8,128,768]{2,1,0:T(8,128)(2,1)} %get-tuple-element.26), channel_id=1, source_target_pairs={{0,6},{2,4},{4,2},{6,0},{8,14},{10,12},{12,10},{14,8},{16,22},{18,... | collective-permute-start | bytes 4718600 | tf_op jit(solution)/shard_map/ppermute | solution.py:449
  235.4 66.7 %collective-permute-start.7 = (bf16[8,128,768]{2,1,0:T(8,128)(2,1)}, bf16[8,128,768]{2,1,0:T(8,128)(2,1)}, u32[]{:S(2)}, u32[]{:S(2)}) collective-permute-start(bf16[8,128,768]{2,1,0:T(8,128)(2,1)} %get-tuple-element.27), channel_id=1, source_target_pairs={{0,2},{2,0},{4,6},{6,4},{8,10},{10,8},{12,14},{14,12},{16,18},{18,... | collective-permute-start | bytes 4718600 | tf_op jit(solution)/shard_map/ppermute | solution.py:449
  300.1 72.8 %collective-permute-start.8 = (bf16[8,128,768]{2,1,0:T(8,128)(2,1)}, bf16[8,128,768]{2,1,0:T(8,128)(2,1)}, u32[]{:S(2)}, u32[]{:S(2)}) collective-permute-start(bf16[8,128,768]{2,1,0:T(8,128)(2,1)} %get-tuple-element.28), channel_id=1, source_target_pairs={{0,4},{2,6},{4,0},{6,2},{8,12},{10,14},{12,8},{14,10},{16,20},{18,... | collective-permute-start | bytes 4718600 | tf_op jit(solution)/shard_map/ppermute | solution.py:449
  300.6 72.8 %collective-permute-start.9 = (bf16[8,128,768]{2,1,0:T(8,128)(2,1)}, bf16[8,128,768]{2,1,0:T(8,128)(2,1)}, u32[]{:S(2)}, u32[]{:S(2)}) collective-permute-start(bf16[8,128,768]{2,1,0:T(8,128)(2,1)} %get-tuple-element.29), channel_id=1, source_target_pairs={{0,6},{2,4},{4,2},{6,0},{8,14},{10,12},{12,10},{14,8},{16,22},{18,... | collective-permute-start | bytes 4718600 | tf_op jit(solution)/shard_map/ppermute | solution.py:449
  302.1 72.5 %collective-permute-start.14 = (bf16[8,128,768]{2,1,0:T(8,128)(2,1)}, bf16[8,128,768]{2,1,0:T(8,128)(2,1)}, u32[]{:S(2)}, u32[]{:S(2)}) collective-permute-start(bf16[8,128,768]{2,1,0:T(8,128)(2,1)} %get-tuple-element.30), channel_id=1, source_target_pairs={{0,2},{2,0},{4,6},{6,4},{8,10},{10,8},{12,14},{14,12},{16,18},{18,... | collective-permute-start | bytes 4718600 | tf_op jit(solution)/shard_map/ppermute | solution.py:449
  304.7 135.5 %collective-permute-start.15 = (bf16[8,128,768]{2,1,0:T(8,128)(2,1)}, bf16[8,128,768]{2,1,0:T(8,128)(2,1)S(1)}, u32[]{:S(2)}, u32[]{:S(2)}) collective-permute-start(bf16[8,128,768]{2,1,0:T(8,128)(2,1)} %get-tuple-element.31), channel_id=1, source_target_pairs={{0,4},{2,6},{4,0},{6,2},{8,12},{10,14},{12,8},{14,10},{16,20},{18,... | collective-permute-start | bytes 4718600 | tf_op jit(solution)/shard_map/ppermute | solution.py:449
  305.2 134.9 %collective-permute-start.16 = (bf16[8,128,768]{2,1,0:T(8,128)(2,1)}, bf16[8,128,768]{2,1,0:T(8,128)(2,1)}, u32[]{:S(2)}, u32[]{:S(2)}) collective-permute-start(bf16[8,128,768]{2,1,0:T(8,128)(2,1)} %get-tuple-element.32), channel_id=1, source_target_pairs={{0,6},{2,4},{4,2},{6,0},{8,14},{10,12},{12,10},{14,8},{16,22},{18,... | collective-permute-start | bytes 4718600 | tf_op jit(solution)/shard_map/ppermute | solution.py:449
  372.8 95.8 %collective-permute-start.21 = (bf16[8,128,768]{2,1,0:T(8,128)(2,1)}, bf16[8,128,768]{2,1,0:T(8,128)(2,1)S(1)}, u32[]{:S(2)}, u32[]{:S(2)}) collective-permute-start(bf16[8,128,768]{2,1,0:T(8,128)(2,1)} %get-tuple-element.35), channel_id=1, source_target_pairs={{0,2},{2,0},{4,6},{6,4},{8,10},{10,8},{12,14},{14,12},{16,18},{18,... | collective-permute-start | bytes 4718600 | tf_op jit(solution)/shard_map/ppermute | solution.py:449
  373.4 130.7 %collective-permute-start.22 = (bf16[8,128,768]{2,1,0:T(8,128)(2,1)}, bf16[8,128,768]{2,1,0:T(8,128)(2,1)}, u32[]{:S(2)}, u32[]{:S(2)}) collective-permute-start(bf16[8,128,768]{2,1,0:T(8,128)(2,1)} %get-tuple-element.36), channel_id=1, source_target_pairs={{0,4},{2,6},{4,0},{6,2},{8,12},{10,14},{12,8},{14,10},{16,20},{18,... | collective-permute-start | bytes 4718600 | tf_op jit(solution)/shard_map/ppermute | solution.py:449
  374.6 129.5 %collective-permute-start.23 = (bf16[8,128,768]{2,1,0:T(8,128)(2,1)}, bf16[8,128,768]{2,1,0:T(8,128)(2,1)}, u32[]{:S(2)}, u32[]{:S(2)}) collective-permute-start(bf16[8,128,768]{2,1,0:T(8,128)(2,1)} %get-tuple-element.37), channel_id=1, source_target_pairs={{0,6},{2,4},{4,2},{6,0},{8,14},{10,12},{12,10},{14,8},{16,22},{18,... | collective-permute-start | bytes 4718600 | tf_op jit(solution)/shard_map/ppermute | solution.py:449
  440.1 1.1 copy-start.3
  468.6 35.5 %copy-start.4 = (bf16[8,128,768]{2,1,0:T(8,128)(2,1)}, bf16[8,128,768]{2,1,0:T(8,128)(2,1)S(1)}, u32[]{:S(2)}) copy-start(bf16[8,128,768]{2,1,0:T(8,128)(2,1)S(1)} %collective-permute-done.21.refs_4_) | copy-start | bytes 4718596
  536.9 4.4 collective-permute-start.24
  541.4 1.3 copy-start.2
  548.4 53.4 %all-to-all-start = ((bf16[16,8,64,128]{3,2,1,0:T(8,128)(2,1)}), bf16[16,8,64,128]{3,2,1,0:T(8,128)(2,1)S(1)}, u32[]{:S(2)}, u32[]{:S(2)}) async-start(bf16[16,8,64,128]{3,2,1,0:T(8,128)(2,1)} %bitcast.20), calls=%async_computation | async-start | bytes 4194304 | tf_op jit(solution)/shard_map/all_to_all | solution.py:553
  566.2 4.5 collective-permute-start.25
  601.8 1.4 copy-start.1

commit v3 on v2

--- a/solution.py
+++ b/solution.py
@@ -93,7 +93,7 @@
 def gather_kernel(layout, kslots, capacity):
     def body(entry_ref, panel_ref, code_ref, late_ref, omega_ref, own_ref, *refs):
         arrays = refs[: len(layout)]
-        part_ref, rows_ref, table, sem = refs[len(layout) :]
+        part_ref, rows_ref, omega_late, table, sem = refs[len(layout) :]
         row = pl.program_id(0)
         block_width = table.shape[1] // kslots
 
@@ -136,11 +136,17 @@
         rows_ref[0] = table[row]
         part = jnp.zeros(part_ref.shape[1:], jnp.float32)
         for s in range(kslots):
-            omega = omega_ref[0, s]
+            omega = omega_ref[0, s].astype(jnp.bfloat16)
             if s > 0:
-                omega = jnp.where(late_ref[row * kslots + s] >= 0, 0.0, omega)
+                late = late_ref[row * kslots + s]
+
+                @pl.when(late >= 0)
+                def _(late=late, omega=omega):
+                    omega_late[late] = omega
+
+                omega = jnp.where(late >= 0, jnp.zeros_like(omega), omega)
             part += jnp.dot(
-                omega.astype(jnp.bfloat16),
+                omega,
                 table[row, s * block_width : (s + 1) * block_width],
                 preferred_element_type=jnp.float32,
             )
@@ -149,7 +155,9 @@
     return body
 
 
-def gather_early(entries, panel_ids, codes, late, omega_blocks, own, arrays, layout, capacity):
+def gather_early(
+    entries, panel_ids, codes, late, omega_blocks, own, arrays, layout, capacity, late_count
+):
     row_count, kslots, block_width, _ = omega_blocks.shape
     samples = own.shape[2]
     flops = 2 * row_count * kslots * block_width * block_width * samples
@@ -158,6 +166,7 @@
         out_shape=[
             jax.ShapeDtypeStruct((row_count, block_width, samples), jnp.float32),
             jax.ShapeDtypeStruct((row_count, kslots * block_width, samples), jnp.bfloat16),
+            jax.ShapeDtypeStruct((late_count, block_width, block_width), jnp.bfloat16),
         ],
         grid_spec=pltpu.PrefetchScalarGridSpec(
             num_scalar_prefetch=4,
@@ -167,6 +176,7 @@
             out_specs=[
                 pl.BlockSpec((1, block_width, samples), lambda i, *_: (i, 0, 0)),
                 pl.BlockSpec((1, kslots * block_width, samples), lambda i, *_: (i, 0, 0)),
+                pl.BlockSpec((late_count, block_width, block_width), lambda i, *_: (0, 0, 0)),
             ],
             scratch_shapes=[
                 pltpu.VMEM((row_count, kslots * block_width, samples), jnp.bfloat16),
@@ -193,8 +203,17 @@
         row = pl.program_id(0)
         block_width = w_row.shape[0]
 
+        slots = table.shape[0]
+        slot = row % slots
+
+        def start(i):
+            pltpu.make_async_copy(rows_ref.at[i], table.at[i % slots], sem.at[i % slots]).start()
+
         @pl.when(row == 0)
         def _():
+            for mask, block in enumerate(came):
+                at = pl.ds((mask + 1) * capacity, capacity)
+                pltpu.make_async_copy(block, held.at[at], held_sem.at[0]).start()
             for k in range(line_count):
 
                 @pl.when(code_ref[0] == k)
@@ -204,30 +223,27 @@
                             lines[k].at[panel_ref[c]], held.at[c], held_sem.at[0]
                         ).start()
 
-            for mask, block in enumerate(came):
-                at = pl.ds((mask + 1) * capacity, capacity)
-                pltpu.make_async_copy(block, held.at[at], held_sem.at[0]).start()
-            for i in range(table.shape[0]):
-                pltpu.make_async_copy(rows_ref.at[i], table.at[i], sem.at[i]).start()
+            for i in range(slots - 1):
+                start(i)
             pltpu.make_async_copy(held, held, held_sem.at[0]).wait()
 
+        @pl.when(row + slots - 1 < pl.num_programs(0))
+        def _():
+            start(row + slots - 1)
+
         w_row[...] = part_ref[0]
-        pltpu.make_async_copy(table.at[row], table.at[row], sem.at[row]).wait()
+        pltpu.make_async_copy(table.at[slot], table.at[slot], sem.at[slot]).wait()
         for s in range(1, kslots):
             late = late_ref[row * kslots + s]
 
             @pl.when(late >= 0)
             def _(s=s, late=late):
                 panel = held[late]
-                table[row, s * block_width : (s + 1) * block_width] = panel
-                w_row[...] += jnp.dot(
-                    omega_ref[0, s].astype(jnp.bfloat16),
-                    panel,
-                    preferred_element_type=jnp.float32,
-                )
+                table[slot, s * block_width : (s + 1) * block_width] = panel
+                w_row[...] += jnp.dot(omega_ref[late], panel, preferred_element_type=jnp.float32)
 
         flipped = lax.dot_general(
-            table[row],
+            table[slot],
             w_row[...].astype(jnp.bfloat16),
             (((1,), (1,)), ((), ())),
             preferred_element_type=jnp.float32,
@@ -243,21 +259,23 @@
     return body
 
 
-def grams_of(panel_ids, codes, late, omega_blocks, part, rows, lines, came, capacity, half_rows):
-    row_count, kslots, block_width, _ = omega_blocks.shape
-    samples = part.shape[2]
+def grams_of(panel_ids, codes, late, omega_late, part, rows, lines, came, capacity, half_rows):
+    row_count, block_width, samples = part.shape
+    kslots = rows.shape[1] // block_width
+    slots = min(4, row_count)
+    whole = (row_count, kslots, block_width, block_width)
     flops = 2 * row_count * kslots * block_width * block_width * samples
     return pl.pallas_call(
         gram_kernel(len(lines), kslots, capacity, half_rows),
         out_shape=[
-            jax.ShapeDtypeStruct(omega_blocks.shape, jnp.float32),
+            jax.ShapeDtypeStruct(whole, jnp.float32),
             jax.ShapeDtypeStruct((row_count, kslots, half_rows, block_width), jnp.bfloat16),
         ],
         grid_spec=pltpu.PrefetchScalarGridSpec(
             num_scalar_prefetch=3,
             grid=(row_count,),
             in_specs=[
-                pl.BlockSpec((1, kslots, block_width, block_width), lambda i, *_: (i, 0, 0, 0)),
+                pl.BlockSpec(omega_late.shape, lambda i, *_: (0, 0, 0)),
                 pl.BlockSpec((1, block_width, samples), lambda i, *_: (i, 0, 0)),
             ]
             + [pl.BlockSpec(memory_space=pl.ANY)] * (1 + len(lines) + len(came)),
@@ -266,10 +284,10 @@
                 pl.BlockSpec((1, kslots, half_rows, block_width), lambda i, *_: (i, 0, 0, 0)),
             ],
             scratch_shapes=[
-                pltpu.VMEM((row_count, kslots * block_width, samples), jnp.bfloat16),
+                pltpu.VMEM((slots, kslots * block_width, samples), jnp.bfloat16),
                 pltpu.VMEM(((1 + len(came)) * capacity, block_width, samples), jnp.bfloat16),
                 pltpu.VMEM((block_width, samples), jnp.float32),
-                pltpu.SemaphoreType.DMA((row_count,)),
+                pltpu.SemaphoreType.DMA((slots,)),
                 pltpu.SemaphoreType.DMA((1,)),
             ],
         ),
@@ -282,7 +300,7 @@
             bytes_accessed=(kslots + 4) * row_count * block_width * samples * 2,
         ),
         name="grams",
-    )(panel_ids, codes, late, omega_blocks, part, rows, *lines, *came)
+    )(panel_ids, codes, late, omega_late, part, rows, *lines, *came)
 
 
 def turn_kernel(part_ref, grams_ref, keep_ref, send_ref):
@@ -520,7 +538,7 @@
         arrays.append(came[option])
         layout.append(line_users[option])
     early = last * plane * capacity
-    part, rows = gather_early(
+    part, rows, omega_late = gather_early(
         entry_table[:early],
         panel_table[:early],
         jnp.stack(code_values),
@@ -530,12 +548,13 @@
         arrays,
         layout,
         capacity,
+        plane * capacity,
     )
     grams, send_col = grams_of(
         panel_table[early : early + capacity],
         jnp.stack([info[2 + last], sample_part]),
         late,
-        omega_blocks,
+        omega_late,
         part,
         rows,
         [came[o] for o in choices[last]],

time: 615 us -> 608 us (0.989)
    pallas_call x1, Pallas kernels: 32.8 us -> 25.6 us  [grams_of(): pl.pallas_call(gram_kernel(len(lines), kslots, capacity, half_rows), out_...]
where the time goes in v3:
time: 608 us; the launch traced here: 606 us
  waiting for transfers between devices  420 us (69%)
  Pallas kernels  109 us (18%)
  starting transfers between devices  60.1 us (10%)
  local copies, waits for them, and re-layouts  11.6 us (2%)
    ppermute x12, waiting for transfers between devices, across(): return lax.ppermute(array, 'vars', pairs)  204 us
    ppermute x12, waiting for transfers between devices, along(): return lax.ppermute(array, 'vars', pairs)  176 us
    ppermute x12, starting transfers between devices, along(): return lax.ppermute(array, 'vars', pairs)  41.2 us
    all_to_all x1, waiting for transfers between devices, step_on_device(): lax.all_to_all(outgoing.reshape(devices, capacity, half_rows, block_width...  31.1 us
    pallas_call x1, Pallas kernels, gather_early(): pl.pallas_call(gather_kernel(layout, kslots, capacity), out_shape=[jax.Sh...  30.9 us
    pallas_call x1, Pallas kernels, grams_of(): pl.pallas_call(gram_kernel(len(lines), kslots, capacity, half_rows), out_...  25.6 us
    pallas_call x4, Pallas kernels, select_panels(): pl.pallas_call(select_kernel(phase, len(arrays), targets, capacity), out_...  24.9 us
    ppermute x12, starting transfers between devices, across(): return lax.ppermute(array, 'vars', pairs)  13.1 us
  transfers between devices with their start and end apart: 27, of which 10 were waited for; matrix products, arithmetic and copies ran while one was open for 2% of the time, Pallas kernels for 11%

profile of v3, /device:TPU:14, one launch (start us, length us, event | category | flops | bytes accessed | tf_op | source)
XLA Modules:
  0.0 606.2 jit_solution(2567017839210530039)
XLA Ops:
  0.6 3.5 collective-permute-start.5
  4.1 4.0 collective-permute-start.6
  8.1 64.6 %collective-permute-done.5.refs_2_.refs_5_.refs_10_ = bf16[16,128,768]{2,1,0:T(8,128)(2,1)} collective-permute-done((bf16[16,128,768]{2,1,0:T(8,128)(2,1)}, bf16[16,128,768]{2,1,0:T(8,128)(2,1)}, u32[]{:S(2)}, u32[]{:S(2)}) %collective-permute-start.5) | collective-permute-done | bytes 3145760 | tf_op jit(solution)/shard_map/ppermute | solution.py:463
  72.7 3.5 collective-permute-start.12
  76.2 3.7 collective-permute-start.13
  79.9 1.4 copy.15.refs_0_
  81.2 1.2 fusion.6
  82.4 6.1 %select_panels.4 = (bf16[8,128,768]{2,1,0:T(8,128)(2,1)}, bf16[8,128,768]{2,1,0:T(8,128)(2,1)}, bf16[8,128,768]{2,1,0:T(8,128)(2,1)}) custom-call(s32[6]{0:T(128)} %get-tuple-element.52.info_ref, s32[16,8]{1,0:T(8,128)} %copy.15.refs_0_, bf16[16,128,768]{2,1,0:T(8,128)(2,1)} %bitcast.17), custom_call_target="tpu_custom_call" | custom-call | bytes 9437184 | tf_op jit(solution)/shard_map/select_panels/pallas_call | solution.py:76
  89.2 54.6 %collective-permute-done.12.refs_4_.refs_9_.refs_5_.refs_1_ = bf16[16,128,768]{2,1,0:T(8,128)(2,1)S(1)} collective-permute-done((bf16[16,128,768]{2,1,0:T(8,128)(2,1)}, bf16[16,128,768]{2,1,0:T(8,128)(2,1)S(1)}, u32[]{:S(2)}, u32[]{:S(2)}) %collective-permute-start.12) | collective-permute-done | bytes 3145760 | tf_op jit(solution)/shard_map/ppermute | solution.py:463
  143.8 3.5 collective-permute-start.17
  147.3 4.0 collective-permute-start.18
  151.3 1.9 collective-permute-start.3
  153.2 3.9 collective-permute-start.4
  157.1 56.9 %collective-permute-done.3.refs_0_.refs_1_ = s32[16,8]{1,0:T(8,128)S(1)} collective-permute-done((s32[16,8]{1,0:T(8,128)S(1)}, s32[16,8]{1,0:T(8,128)S(1)}, u32[]{:S(2)}, u32[]{:S(2)}) %collective-permute-start.3) | collective-permute-done | bytes 544 | tf_op jit(solution)/shard_map/ppermute | solution.py:463
  214.1 3.5 collective-permute-start.10
  217.6 3.9 collective-permute-start.11
  221.5 1.9 collective-permute-start.19
  223.5 3.9 collective-permute-start.20
  227.4 5.9 select_panels.5
  233.9 1.5 collective-permute-start.2
  235.4 1.5 collective-permute-start.7
  236.9 6.4 %select_panels.6 = (bf16[8,128,768]{2,1,0:T(8,128)(2,1)}, bf16[8,128,768]{2,1,0:T(8,128)(2,1)}, bf16[8,128,768]{2,1,0:T(8,128)(2,1)}) custom-call(s32[6]{0:T(128)} %get-tuple-element.52.info_ref, s32[16,8]{1,0:T(8,128)} %copy-done.6, s32[16,8]{1,0:T(8,128)} %copy-done.8, s32[16,8]{1,0:T(8,128)} %copy-done.9, s32[16,8]{1,0:T(8,128)} %copy-done.7, ...), custom_call_target="tpu_custom_call" | custom-call | bytes 9437184 | tf_op jit(solution)/shard_map/select_panels/pallas_call | solution.py:76
  243.3 56.7 %collective-permute-done.1.refs_1_ = bf16[8,128,768]{2,1,0:T(8,128)(2,1)} collective-permute-done((bf16[8,128,768]{2,1,0:T(8,128)(2,1)}, bf16[8,128,768]{2,1,0:T(8,128)(2,1)}, u32[]{:S(2)}, u32[]{:S(2)}) %collective-permute-start.1) | collective-permute-done | bytes 1572896 | tf_op jit(solution)/shard_map/ppermute | solution.py:467
  300.6 1.5 collective-permute-start.9
  302.1 1.5 collective-permute-start.14
  303.7 0.7 constant_dynamic-slice_fusion.1
  305.2 1.5 collective-permute-start.16
  306.7 6.5 %select_panels.7 = (bf16[8,128,768]{2,1,0:T(8,128)(2,1)}, bf16[8,128,768]{2,1,0:T(8,128)(2,1)}, bf16[8,128,768]{2,1,0:T(8,128)(2,1)}) custom-call(s32[6]{0:T(128)} %get-tuple-element.52.info_ref, s32[16,8]{1,0:T(8,128)} %copy-done.10, s32[16,8]{1,0:T(8,128)} %copy-done.6, s32[16,8]{1,0:T(8,128)} %copy-done.7, s32[16,8]{1,0:T(8,128)} %copy-done.11, ...), custom_call_target="tpu_custom_call" | custom-call | bytes 9437184 | tf_op jit(solution)/shard_map/select_panels/pallas_call | solution.py:76
  313.2 59.6 %collective-permute-done.8.refs_4_ = bf16[8,128,768]{2,1,0:T(8,128)(2,1)} collective-permute-done((bf16[8,128,768]{2,1,0:T(8,128)(2,1)}, bf16[8,128,768]{2,1,0:T(8,128)(2,1)}, u32[]{:S(2)}, u32[]{:S(2)}) %collective-permute-start.8) | collective-permute-done | bytes 1572896 | tf_op jit(solution)/shard_map/ppermute | solution.py:467
  373.4 1.3 collective-permute-start.22
  374.6 1.7 collective-permute-start.23
  379.7 1.9 stack.8.code_ref
  381.6 1.4 pad_add_fusion.code_ref
  383.0 1.2 and_select_fusion.3
  384.7 55.4 %collective-permute-done.15.refs_7_ = bf16[8,128,768]{2,1,0:T(8,128)(2,1)S(1)} collective-permute-done((bf16[8,128,768]{2,1,0:T(8,128)(2,1)}, bf16[8,128,768]{2,1,0:T(8,128)(2,1)S(1)}, u32[]{:S(2)}, u32[]{:S(2)}) %collective-permute-start.15) | collective-permute-done | bytes 1572896 | tf_op jit(solution)/shard_map/ppermute | solution.py:467
  440.1 1.1 copy-done.3
  441.3 30.9 %gather_early.1 = (f32[16,128,768]{2,1,0:T(8,128)}, bf16[16,1024,768]{2,1,0:T(8,128)(2,1)}, bf16[32,128,128]{2,1,0:T(8,128)(2,1)}) custom-call(s32[96]{0:T(128)} %slice.46.entry_ref, s32[96]{0:T(128)} %slice.48.panel_ref, s32[12]{0:T(128)} %stack.8.code_ref, s32[128]{0:T(128)} %get-tuple-element.56.late_ref, f32[16,8,128,128]{3,2,1,0:T(8,128)} %omega_ref.3, ...), custom_call_target="tpu_custom_call" | custom-call | flops 3221225472 | bytes 50331648 | tf_op jit(solution)/shard_map/gather_early/pallas_call | solution.py:164
  472.2 31.9 %collective-permute-done.22.refs_5_ = bf16[8,128,768]{2,1,0:T(8,128)(2,1)} collective-permute-done((bf16[8,128,768]{2,1,0:T(8,128)(2,1)}, bf16[8,128,768]{2,1,0:T(8,128)(2,1)}, u32[]{:S(2)}, u32[]{:S(2)}) %collective-permute-start.22) | collective-permute-done | bytes 1572896 | tf_op jit(solution)/shard_map/ppermute | solution.py:467
  504.1 25.6 %grams.1 = (f32[16,8,128,128]{3,2,1,0:T(8,128)}, bf16[16,8,64,128]{3,2,1,0:T(8,128)(2,1)}) custom-call(s32[8]{0:T(128)} %slice_bitcast_fusion.panel_ref, s32[2]{0:T(128)} %pad_add_fusion.code_ref, s32[128]{0:T(128)} %get-tuple-element.56.late_ref, bf16[32,128,128]{2,1,0:T(8,128)(2,1)} %get-tuple-element.34.omega_ref, ...), custom_call_target="tpu_custom_call" | custom-call | flops 3221225472 | bytes 37748736 | tf_op jit(solution)/shard_map/grams/pallas_call | solution.py:268
  529.8 4.4 collective-permute-done.24.came_ref
  534.2 1.3 copy-done.2
  535.5 5.7 outgoing.1
  541.2 5.7 all-to-all-start
  546.9 12.7 %turn.1 = (f32[16,8,64,128]{3,2,1,0:T(8,128)}, bf16[16,8,64,128]{3,2,1,0:T(8,128)(2,1)}) custom-call(s32[1]{0:T(128)} %bitcast.half_ref.part_ref, f32[16,8,128,128]{3,2,1,0:T(8,128)} %get-tuple-element.43.keep_ref.grams_ref), custom_call_target="tpu_custom_call" | custom-call | tf_op jit(solution)/shard_map/turn/pallas_call | solution.py:320
  559.6 4.5 collective-permute-done.25.came_ref
  564.1 31.1 %all-to-all-done = bf16[16,8,64,128]{3,2,1,0:T(8,128)(2,1)S(1)} async-done(((bf16[16,8,64,128]{3,2,1,0:T(8,128)(2,1)}), bf16[16,8,64,128]{3,2,1,0:T(8,128)(2,1)S(1)}, u32[]{:S(2)}, u32[]{:S(2)}) %all-to-all-start) | async-done | bytes 2097184 | tf_op jit(solution)/shard_map/all_to_all | solution.py:572
  595.2 1.4 copy-done.1
  596.6 9.6 %final_step.1 = (f32[16,8,64,128]{3,2,1,0:T(8,128)}, f32[16,8,64,128]{3,2,1,0:T(8,128)}) custom-call(s32[128]{0:T(128)} %get-tuple-element.61.slot_ref, s32[1]{0:T(128)} %bitcast.half_ref.part_ref, f32[16,8,64,128]{3,2,1,0:T(8,128)} %get-tuple-element.44.keep_ref, bf16[16,8,64,128]{3,2,1,0:T(8,128)(2,1)} %collective-permute-done.25.came_ref, ...), custom_call_target="tpu_custom_call" | custom-call | tf_op jit(solution)/shard_map/final_step/pallas_call | solution.py:413
  (64 shorter events, 7.1 us)
Async XLA Ops:
  0.6 72.1 %collective-permute-start.5 = (bf16[16,128,768]{2,1,0:T(8,128)(2,1)}, bf16[16,128,768]{2,1,0:T(8,128)(2,1)}, u32[]{:S(2)}, u32[]{:S(2)}) collective-permute-start(bf16[16,128,768]{2,1,0:T(8,128)(2,1)} %bitcast.15), channel_id=1, source_target_pairs={{0,8},{2,10},{4,12},{6,14},{8,16},{10,18},{12,20},{14,22},{16,24},... | collective-permute-start | bytes 9437192 | tf_op jit(solution)/shard_map/ppermute | solution.py:463
  4.1 72.0 %collective-permute-start.6 = (bf16[16,128,768]{2,1,0:T(8,128)(2,1)}, bf16[16,128,768]{2,1,0:T(8,128)(2,1)}, u32[]{:S(2)}, u32[]{:S(2)}) collective-permute-start(bf16[16,128,768]{2,1,0:T(8,128)(2,1)} %bitcast.16), channel_id=1, source_target_pairs={{8,0},{10,2},{12,4},{14,6},{16,8},{18,10},{20,12},{22,14},{24,16},... | collective-permute-start | bytes 9437192 | tf_op jit(solution)/shard_map/ppermute | solution.py:463
  72.7 71.1 %collective-permute-start.12 = (bf16[16,128,768]{2,1,0:T(8,128)(2,1)}, bf16[16,128,768]{2,1,0:T(8,128)(2,1)S(1)}, u32[]{:S(2)}, u32[]{:S(2)}) collective-permute-start(bf16[16,128,768]{2,1,0:T(8,128)(2,1)} %collective-permute-done.5.refs_2_.refs_5_.refs_10_), channel_id=1, source_target_pairs={{0,8},{2,10},{4,12},{6,14},{8,16},{10,18},{12,20},{14,22},{16,24},... | collective-permute-start | bytes 9437192 | tf_op jit(solution)/shard_map/ppermute | solution.py:463
  76.2 71.1 %collective-permute-start.13 = (bf16[16,128,768]{2,1,0:T(8,128)(2,1)}, bf16[16,128,768]{2,1,0:T(8,128)(2,1)}, u32[]{:S(2)}, u32[]{:S(2)}) collective-permute-start(bf16[16,128,768]{2,1,0:T(8,128)(2,1)} %collective-permute-done.6.refs_3_.refs_6_.refs_11_), channel_id=1, source_target_pairs={{8,0},{10,2},{12,4},{14,6},{16,8},{18,10},{20,12},{22,14},{24,16},... | collective-permute-start | bytes 9437192 | tf_op jit(solution)/shard_map/ppermute | solution.py:463
  82.4 68.8 %copy-start.5 = (s32[16,8]{1,0:T(8,128)S(1)}, s32[16,8]{1,0:T(8,128)}, u32[]{:S(2)}) copy-start(s32[16,8]{1,0:T(8,128)} %copy.15.refs_0_) | copy-start | bytes 1540
  88.6 146.8 %collective-permute-start = (bf16[8,128,768]{2,1,0:T(8,128)(2,1)}, bf16[8,128,768]{2,1,0:T(8,128)(2,1)}, u32[]{:S(2)}, u32[]{:S(2)}) collective-permute-start(bf16[8,128,768]{2,1,0:T(8,128)(2,1)} %get-tuple-element.25), channel_id=1, source_target_pairs={{0,2},{2,0},{4,6},{6,4},{8,10},{10,8},{12,14},{14,12},{16,18},{18,... | collective-permute-start | bytes 4718600 | tf_op jit(solution)/shard_map/ppermute | solution.py:467
  143.8 89.5 %copy-start = (bf16[16,128,768]{2,1,0:T(8,128)(2,1)}, bf16[16,128,768]{2,1,0:T(8,128)(2,1)S(1)}, u32[]{:S(2)}) copy-start(bf16[16,128,768]{2,1,0:T(8,128)(2,1)S(1)} %collective-permute-done.12.refs_4_.refs_9_.refs_5_.refs_1_) | copy-start | bytes 9437188
  143.8 160.9 %collective-permute-start.17 = (bf16[16,128,768]{2,1,0:T(8,128)(2,1)S(1)}, bf16[16,128,768]{2,1,0:T(8,128)(2,1)}, u32[]{:S(2)}, u32[]{:S(2)}) collective-permute-start(bf16[16,128,768]{2,1,0:T(8,128)(2,1)S(1)} %collective-permute-done.12.refs_4_.refs_9_.refs_5_.refs_1_), channel_id=1, source_target_pairs={{0,8},{2,10},{4,12},{6,14},{8,16},{10,18},{12,20},{14,22},{16,24},... | collective-permute-start | bytes 9437192 | tf_op jit(solution)/shard_map/ppermute | solution.py:463
  147.3 157.9 %collective-permute-start.18 = (bf16[16,128,768]{2,1,0:T(8,128)(2,1)}, bf16[16,128,768]{2,1,0:T(8,128)(2,1)}, u32[]{:S(2)}, u32[]{:S(2)}) collective-permute-start(bf16[16,128,768]{2,1,0:T(8,128)(2,1)} %collective-permute-done.13.refs_7_.refs_12_.refs_6_.refs_2_), channel_id=1, source_target_pairs={{8,0},{10,2},{12,4},{14,6},{16,8},{18,10},{20,12},{22,14},{24,16},... | collective-permute-start | bytes 9437192 | tf_op jit(solution)/shard_map/ppermute | solution.py:463
  151.3 62.8 %collective-permute-start.3 = (s32[16,8]{1,0:T(8,128)S(1)}, s32[16,8]{1,0:T(8,128)S(1)}, u32[]{:S(2)}, u32[]{:S(2)}) collective-permute-start(s32[16,8]{1,0:T(8,128)S(1)} %copy-done.5), channel_id=1, source_target_pairs={{0,8},{2,10},{4,12},{6,14},{8,16},{10,18},{12,20},{14,22},{16,24},... | collective-permute-start | bytes 1544 | tf_op jit(solution)/shard_map/ppermute | solution.py:463
  153.2 64.4 %collective-permute-start.4 = (s32[16,8]{1,0:T(8,128)S(1)}, s32[16,8]{1,0:T(8,128)S(1)}, u32[]{:S(2)}, u32[]{:S(2)}) collective-permute-start(s32[16,8]{1,0:T(8,128)S(1)} %copy-done.5), channel_id=1, source_target_pairs={{8,0},{10,2},{12,4},{14,6},{16,8},{18,10},{20,12},{22,14},{24,16},... | collective-permute-start | bytes 1544 | tf_op jit(solution)/shard_map/ppermute | solution.py:463
  214.1 13.3 %copy-start.8 = (s32[16,8]{1,0:T(8,128)}, s32[16,8]{1,0:T(8,128)S(1)}, u32[]{:S(2)}) copy-start(s32[16,8]{1,0:T(8,128)S(1)} %collective-permute-done.3.refs_0_.refs_1_) | copy-start | bytes 1540
  214.1 7.4 %collective-permute-start.10 = (s32[16,8]{1,0:T(8,128)S(1)}, s32[16,8]{1,0:T(8,128)S(1)}, u32[]{:S(2)}, u32[]{:S(2)}) collective-permute-start(s32[16,8]{1,0:T(8,128)S(1)} %collective-permute-done.3.refs_0_.refs_1_), channel_id=1, source_target_pairs={{0,8},{2,10},{4,12},{6,14},{8,16},{10,18},{12,20},{14,22},{16,24},... | collective-permute-start | bytes 1544 | tf_op jit(solution)/shard_map/ppermute | solution.py:463
  217.6 9.8 %copy-start.9 = (s32[16,8]{1,0:T(8,128)}, s32[16,8]{1,0:T(8,128)S(1)}, u32[]{:S(2)}) copy-start(s32[16,8]{1,0:T(8,128)S(1)} %collective-permute-done.4.refs_1_.refs_2_) | copy-start | bytes 1540
  217.6 5.9 collective-permute-start.11
  221.5 11.8 %copy-start.6 = (s32[16,8]{1,0:T(8,128)}, s32[16,8]{1,0:T(8,128)S(1)}, u32[]{:S(2)}) copy-start(s32[16,8]{1,0:T(8,128)S(1)} %collective-permute-done.10.refs_0_.refs_1_) | copy-start | bytes 1540
  221.5 11.8 %collective-permute-start.19 = (s32[16,8]{1,0:T(8,128)S(1)}, s32[16,8]{1,0:T(8,128)S(1)}, u32[]{:S(2)}, u32[]{:S(2)}) collective-permute-start(s32[16,8]{1,0:T(8,128)S(1)} %collective-permute-done.10.refs_0_.refs_1_), channel_id=1, source_target_pairs={{0,8},{2,10},{4,12},{6,14},{8,16},{10,18},{12,20},{14,22},{16,24},... | collective-permute-start | bytes 1544 | tf_op jit(solution)/shard_map/ppermute | solution.py:463
  223.5 9.8 %copy-start.7 = (s32[16,8]{1,0:T(8,128)}, s32[16,8]{1,0:T(8,128)S(1)}, u32[]{:S(2)}) copy-start(s32[16,8]{1,0:T(8,128)S(1)} %collective-permute-done.11.refs_3_.refs_2_) | copy-start | bytes 1540
  223.5 10.4 %collective-permute-start.20 = (s32[16,8]{1,0:T(8,128)S(1)}, s32[16,8]{1,0:T(8,128)S(1)}, u32[]{:S(2)}, u32[]{:S(2)}) collective-permute-start(s32[16,8]{1,0:T(8,128)S(1)} %collective-permute-done.11.refs_3_.refs_2_), channel_id=1, source_target_pairs={{8,0},{10,2},{12,4},{14,6},{16,8},{18,10},{20,12},{22,14},{24,16},... | collective-permute-start | bytes 1544 | tf_op jit(solution)/shard_map/ppermute | solution.py:463
  233.3 10.0 %copy-start.10 = (s32[16,8]{1,0:T(8,128)}, s32[16,8]{1,0:T(8,128)S(1)}, u32[]{:S(2)}) copy-start(s32[16,8]{1,0:T(8,128)S(1)} %collective-permute-done.19.refs_0_) | copy-start | bytes 1540
  233.3 66.7 %collective-permute-start.1 = (bf16[8,128,768]{2,1,0:T(8,128)(2,1)}, bf16[8,128,768]{2,1,0:T(8,128)(2,1)}, u32[]{:S(2)}, u32[]{:S(2)}) collective-permute-start(bf16[8,128,768]{2,1,0:T(8,128)(2,1)} %get-tuple-element.26), channel_id=1, source_target_pairs={{0,4},{2,6},{4,0},{6,2},{8,12},{10,14},{12,8},{14,10},{16,20},{18,... | collective-permute-start | bytes 4718600 | tf_op jit(solution)/shard_map/ppermute | solution.py:467
  233.9 9.4 %copy-start.11 = (s32[16,8]{1,0:T(8,128)}, s32[16,8]{1,0:T(8,128)S(1)}, u32[]{:S(2)}) copy-start(s32[16,8]{1,0:T(8,128)S(1)} %collective-permute-done.20.refs_3_) | copy-start | bytes 1540
  233.9 66.7 %collective-permute-start.2 = (bf16[8,128,768]{2,1,0:T(8,128)(2,1)}, bf16[8,128,768]{2,1,0:T(8,128)(2,1)}, u32[]{:S(2)}, u32[]{:S(2)}) collective-permute-start(bf16[8,128,768]{2,1,0:T(8,128)(2,1)} %get-tuple-element.27), channel_id=1, source_target_pairs={{0,6},{2,4},{4,2},{6,0},{8,14},{10,12},{12,10},{14,8},{16,22},{18,... | collective-permute-start | bytes 4718600 | tf_op jit(solution)/shard_map/ppermute | solution.py:467
  235.4 66.7 %collective-permute-start.7 = (bf16[8,128,768]{2,1,0:T(8,128)(2,1)}, bf16[8,128,768]{2,1,0:T(8,128)(2,1)}, u32[]{:S(2)}, u32[]{:S(2)}) collective-permute-start(bf16[8,128,768]{2,1,0:T(8,128)(2,1)} %get-tuple-element.28), channel_id=1, source_target_pairs={{0,2},{2,0},{4,6},{6,4},{8,10},{10,8},{12,14},{14,12},{16,18},{18,... | collective-permute-start | bytes 4718600 | tf_op jit(solution)/shard_map/ppermute | solution.py:467
  300.1 72.8 %collective-permute-start.8 = (bf16[8,128,768]{2,1,0:T(8,128)(2,1)}, bf16[8,128,768]{2,1,0:T(8,128)(2,1)}, u32[]{:S(2)}, u32[]{:S(2)}) collective-permute-start(bf16[8,128,768]{2,1,0:T(8,128)(2,1)} %get-tuple-element.29), channel_id=1, source_target_pairs={{0,4},{2,6},{4,0},{6,2},{8,12},{10,14},{12,8},{14,10},{16,20},{18,... | collective-permute-start | bytes 4718600 | tf_op jit(solution)/shard_map/ppermute | solution.py:467
  300.6 72.8 %collective-permute-start.9 = (bf16[8,128,768]{2,1,0:T(8,128)(2,1)}, bf16[8,128,768]{2,1,0:T(8,128)(2,1)}, u32[]{:S(2)}, u32[]{:S(2)}) collective-permute-start(bf16[8,128,768]{2,1,0:T(8,128)(2,1)} %get-tuple-element.30), channel_id=1, source_target_pairs={{0,6},{2,4},{4,2},{6,0},{8,14},{10,12},{12,10},{14,8},{16,22},{18,... | collective-permute-start | bytes 4718600 | tf_op jit(solution)/shard_map/ppermute | solution.py:467
  302.1 72.5 %collective-permute-start.14 = (bf16[8,128,768]{2,1,0:T(8,128)(2,1)}, bf16[8,128,768]{2,1,0:T(8,128)(2,1)}, u32[]{:S(2)}, u32[]{:S(2)}) collective-permute-start(bf16[8,128,768]{2,1,0:T(8,128)(2,1)} %get-tuple-element.31), channel_id=1, source_target_pairs={{0,2},{2,0},{4,6},{6,4},{8,10},{10,8},{12,14},{14,12},{16,18},{18,... | collective-permute-start | bytes 4718600 | tf_op jit(solution)/shard_map/ppermute | solution.py:467
  304.7 135.5 %collective-permute-start.15 = (bf16[8,128,768]{2,1,0:T(8,128)(2,1)}, bf16[8,128,768]{2,1,0:T(8,128)(2,1)S(1)}, u32[]{:S(2)}, u32[]{:S(2)}) collective-permute-start(bf16[8,128,768]{2,1,0:T(8,128)(2,1)} %get-tuple-element.32), channel_id=1, source_target_pairs={{0,4},{2,6},{4,0},{6,2},{8,12},{10,14},{12,8},{14,10},{16,20},{18,... | collective-permute-start | bytes 4718600 | tf_op jit(solution)/shard_map/ppermute | solution.py:467
  305.2 134.9 %collective-permute-start.16 = (bf16[8,128,768]{2,1,0:T(8,128)(2,1)}, bf16[8,128,768]{2,1,0:T(8,128)(2,1)}, u32[]{:S(2)}, u32[]{:S(2)}) collective-permute-start(bf16[8,128,768]{2,1,0:T(8,128)(2,1)} %get-tuple-element.33), channel_id=1, source_target_pairs={{0,6},{2,4},{4,2},{6,0},{8,14},{10,12},{12,10},{14,8},{16,22},{18,... | collective-permute-start | bytes 4718600 | tf_op jit(solution)/shard_map/ppermute | solution.py:467
  372.8 99.3 %collective-permute-start.21 = (bf16[8,128,768]{2,1,0:T(8,128)(2,1)}, bf16[8,128,768]{2,1,0:T(8,128)(2,1)S(1)}, u32[]{:S(2)}, u32[]{:S(2)}) collective-permute-start(bf16[8,128,768]{2,1,0:T(8,128)(2,1)} %get-tuple-element.37), channel_id=1, source_target_pairs={{0,2},{2,0},{4,6},{6,4},{8,10},{10,8},{12,14},{14,12},{16,18},{18,... | collective-permute-start | bytes 4718600 | tf_op jit(solution)/shard_map/ppermute | solution.py:467
  373.4 130.7 %collective-permute-start.22 = (bf16[8,128,768]{2,1,0:T(8,128)(2,1)}, bf16[8,128,768]{2,1,0:T(8,128)(2,1)}, u32[]{:S(2)}, u32[]{:S(2)}) collective-permute-start(bf16[8,128,768]{2,1,0:T(8,128)(2,1)} %get-tuple-element.38), channel_id=1, source_target_pairs={{0,4},{2,6},{4,0},{6,2},{8,12},{10,14},{12,8},{14,10},{16,20},{18,... | collective-permute-start | bytes 4718600 | tf_op jit(solution)/shard_map/ppermute | solution.py:467
  374.6 129.5 %collective-permute-start.23 = (bf16[8,128,768]{2,1,0:T(8,128)(2,1)}, bf16[8,128,768]{2,1,0:T(8,128)(2,1)}, u32[]{:S(2)}, u32[]{:S(2)}) collective-permute-start(bf16[8,128,768]{2,1,0:T(8,128)(2,1)} %get-tuple-element.39), channel_id=1, source_target_pairs={{0,6},{2,4},{4,2},{6,0},{8,14},{10,12},{12,10},{14,8},{16,22},{18,... | collective-permute-start | bytes 4718600 | tf_op jit(solution)/shard_map/ppermute | solution.py:467
  440.1 1.1 copy-start.3
  472.2 31.9 %copy-start.4 = (bf16[8,128,768]{2,1,0:T(8,128)(2,1)}, bf16[8,128,768]{2,1,0:T(8,128)(2,1)S(1)}, u32[]{:S(2)}) copy-start(bf16[8,128,768]{2,1,0:T(8,128)(2,1)S(1)} %collective-permute-done.21.refs_4_) | copy-start | bytes 4718596
  529.8 4.4 collective-permute-start.24
  534.2 1.3 copy-start.2
  541.2 54.0 %all-to-all-start = ((bf16[16,8,64,128]{3,2,1,0:T(8,128)(2,1)}), bf16[16,8,64,128]{3,2,1,0:T(8,128)(2,1)S(1)}, u32[]{:S(2)}, u32[]{:S(2)}) async-start(bf16[16,8,64,128]{3,2,1,0:T(8,128)(2,1)} %bitcast.20), calls=%async_computation | async-start | bytes 4194304 | tf_op jit(solution)/shard_map/all_to_all | solution.py:572
  559.6 4.5 collective-permute-start.25
  595.2 1.4 copy-start.1

commit v4 on v3

--- a/solution.py
+++ b/solution.py
@@ -93,7 +93,7 @@
 def gather_kernel(layout, kslots, capacity):
     def body(entry_ref, panel_ref, code_ref, late_ref, omega_ref, own_ref, *refs):
         arrays = refs[: len(layout)]
-        part_ref, rows_ref, omega_late, table, sem = refs[len(layout) :]
+        part_ref, table, omega_late, sem = refs[len(layout) :]
         row = pl.program_id(0)
         block_width = table.shape[1] // kslots
 
@@ -133,7 +133,6 @@
                                 fetch(source, k, c, False)
 
         pltpu.make_async_copy(table.at[row], table.at[row], sem.at[row]).wait()
-        rows_ref[0] = table[row]
         part = jnp.zeros(part_ref.shape[1:], jnp.float32)
         for s in range(kslots):
             omega = omega_ref[0, s].astype(jnp.bfloat16)
@@ -165,7 +164,7 @@
         gather_kernel(layout, kslots, capacity),
         out_shape=[
             jax.ShapeDtypeStruct((row_count, block_width, samples), jnp.float32),
-            jax.ShapeDtypeStruct((row_count, kslots * block_width, samples), jnp.bfloat16),
+            pltpu.VMEM((row_count, kslots * block_width, samples), jnp.bfloat16),
             jax.ShapeDtypeStruct((late_count, block_width, block_width), jnp.bfloat16),
         ],
         grid_spec=pltpu.PrefetchScalarGridSpec(
@@ -175,21 +174,18 @@
             + [pl.BlockSpec(memory_space=pl.ANY)] * (1 + len(arrays)),
             out_specs=[
                 pl.BlockSpec((1, block_width, samples), lambda i, *_: (i, 0, 0)),
-                pl.BlockSpec((1, kslots * block_width, samples), lambda i, *_: (i, 0, 0)),
+                pl.BlockSpec(memory_space=pltpu.VMEM),
                 pl.BlockSpec((late_count, block_width, block_width), lambda i, *_: (0, 0, 0)),
             ],
-            scratch_shapes=[
-                pltpu.VMEM((row_count, kslots * block_width, samples), jnp.bfloat16),
-                pltpu.SemaphoreType.DMA((row_count,)),
-            ],
+            scratch_shapes=[pltpu.SemaphoreType.DMA((row_count,))],
         ),
         compiler_params=pltpu.CompilerParams(
-            dimension_semantics=("arbitrary",), vmem_limit_bytes=56 << 20
+            dimension_semantics=("arbitrary",), vmem_limit_bytes=30 << 20
         ),
         cost_estimate=pl.CostEstimate(
             flops=flops,
             transcendentals=0,
-            bytes_accessed=2 * kslots * row_count * block_width * samples * 2,
+            bytes_accessed= kslots * row_count * block_width * samples * 2,
         ),
         name="gather_early",
     )(entries, panel_ids, codes, late, omega_blocks, own, *arrays)
@@ -198,16 +194,10 @@
 def gram_kernel(line_count, kslots, capacity, half_rows):
     def body(panel_ref, code_ref, late_ref, omega_ref, part_ref, rows_ref, *refs):
         lines = refs[:line_count]
-        came = refs[line_count:-7]
-        grams_ref, send_ref, table, held, w_row, sem, held_sem = refs[-7:]
+        came = refs[line_count:-5]
+        grams_ref, send_ref, held, w_row, held_sem = refs[-5:]
         row = pl.program_id(0)
         block_width = w_row.shape[0]
-
-        slots = table.shape[0]
-        slot = row % slots
-
-        def start(i):
-            pltpu.make_async_copy(rows_ref.at[i], table.at[i % slots], sem.at[i % slots]).start()
 
         @pl.when(row == 0)
         def _():
@@ -223,46 +213,52 @@
                             lines[k].at[panel_ref[c]], held.at[c], held_sem.at[0]
                         ).start()
 
-            for i in range(slots - 1):
-                start(i)
             pltpu.make_async_copy(held, held, held_sem.at[0]).wait()
 
-        @pl.when(row + slots - 1 < pl.num_programs(0))
-        def _():
-            start(row + slots - 1)
-
         w_row[...] = part_ref[0]
-        pltpu.make_async_copy(table.at[slot], table.at[slot], sem.at[slot]).wait()
         for s in range(1, kslots):
             late = late_ref[row * kslots + s]
 
             @pl.when(late >= 0)
-            def _(s=s, late=late):
-                panel = held[late]
-                table[slot, s * block_width : (s + 1) * block_width] = panel
-                w_row[...] += jnp.dot(omega_ref[late], panel, preferred_element_type=jnp.float32)
-
-        flipped = lax.dot_general(
-            table[slot],
-            w_row[...].astype(jnp.bfloat16),
-            (((1,), (1,)), ((), ())),
-            preferred_element_type=jnp.float32,
-        )
+            def _(late=late):
+                w_row[...] += jnp.dot(
+                    omega_ref[late], held[late], preferred_element_type=jnp.float32
+                )
+
+        w_low = w_row[...].astype(jnp.bfloat16)
+        contract = (((1,), (1,)), ((), ()))
         first = code_ref[1] == 0
-        for s in range(kslots):
-            block = flipped[s * block_width : (s + 1) * block_width]
+
+        def store(s, block):
             grams_ref[0, s] = block
             send_ref[0, s] = jnp.where(first, block[half_rows:], block[:half_rows]).astype(
                 jnp.bfloat16
             )
 
+        flipped = lax.dot_general(
+            rows_ref[row], w_low, contract, preferred_element_type=jnp.float32
+        )
+        for s in range(kslots):
+            store(s, flipped[s * block_width : (s + 1) * block_width])
+        for s in range(1, kslots):
+            late = late_ref[row * kslots + s]
+
+            @pl.when(late >= 0)
+            def _(s=s, late=late):
+                block = lax.dot_general(
+                    held[late],
+                    w_row[...].astype(jnp.bfloat16),
+                    contract,
+                    preferred_element_type=jnp.float32,
+                )
+                store(s, block)
+
     return body
 
 
 def grams_of(panel_ids, codes, late, omega_late, part, rows, lines, came, capacity, half_rows):
     row_count, block_width, samples = part.shape
     kslots = rows.shape[1] // block_width
-    slots = min(4, row_count)
     whole = (row_count, kslots, block_width, block_width)
     flops = 2 * row_count * kslots * block_width * block_width * samples
     return pl.pallas_call(
@@ -278,21 +274,20 @@
                 pl.BlockSpec(omega_late.shape, lambda i, *_: (0, 0, 0)),
                 pl.BlockSpec((1, block_width, samples), lambda i, *_: (i, 0, 0)),
             ]
-            + [pl.BlockSpec(memory_space=pl.ANY)] * (1 + len(lines) + len(came)),
+            + [pl.BlockSpec(memory_space=pltpu.VMEM)]
+            + [pl.BlockSpec(memory_space=pl.ANY)] * (len(lines) + len(came)),
             out_specs=[
                 pl.BlockSpec((1, kslots, block_width, block_width), lambda i, *_: (i, 0, 0, 0)),
                 pl.BlockSpec((1, kslots, half_rows, block_width), lambda i, *_: (i, 0, 0, 0)),
             ],
             scratch_shapes=[
-                pltpu.VMEM((slots, kslots * block_width, samples), jnp.bfloat16),
                 pltpu.VMEM(((1 + len(came)) * capacity, block_width, samples), jnp.bfloat16),
                 pltpu.VMEM((block_width, samples), jnp.float32),
-                pltpu.SemaphoreType.DMA((slots,)),
                 pltpu.SemaphoreType.DMA((1,)),
             ],
         ),
         compiler_params=pltpu.CompilerParams(
-            dimension_semantics=("arbitrary",), vmem_limit_bytes=56 << 20
+            dimension_semantics=("arbitrary",), vmem_limit_bytes=30 << 20
         ),
         cost_estimate=pl.CostEstimate(
             flops=flops,
@@ -480,7 +475,7 @@
     came_cols = {0: block_cols}
     for m in range(1, length):
         for step in (-1, 1):
-            came_cols[step * m] = along(came_cols[step * (m - 1)], -step)
+            came_cols[step * m] = along(block_cols, -step * m)
 
     entry_ids = jnp.arange(entries, dtype=jnp.int32)
     remote = entry_ids % kslots != 0
@@ -550,6 +545,7 @@
         capacity,
         plane * capacity,
     )
+    rows = pltpu.with_memory_space_constraint(rows, pltpu.VMEM)
     grams, send_col = grams_of(
         panel_table[early : early + capacity],
         jnp.stack([info[2 + last], sample_part]),

time: 608 us -> 615 us (1.012)
  waiting for transfers between devices: 420 us -> 427 us
    ppermute x12, starting transfers between devices: 41.2 us -> 34.9 us  [along(): return lax.ppermute(array, 'vars', pairs)]
  transfers between devices with their start and end apart: 27 -> 27, of which waited for: 10 -> 11; matrix products, arithmetic and copies ran while one was open for 2% -> 2% of each run, Pallas kernels for 11% -> 11%
where the time goes in v4:
time: 615 us; the launch traced here: 613 us
  waiting for transfers between devices  427 us (69%)
  Pallas kernels  111 us (18%)
  starting transfers between devices  57.5 us (9%)
  local copies, waits for them, and re-layouts  11.6 us (2%)
    ppermute x12, waiting for transfers between devices, across(): return lax.ppermute(array, 'vars', pairs)  207 us
    ppermute x12, waiting for transfers between devices, along(): return lax.ppermute(array, 'vars', pairs)  181 us
    ppermute x12, starting transfers between devices, along(): return lax.ppermute(array, 'vars', pairs)  34.9 us
    all_to_all x1, waiting for transfers between devices, step_on_device(): lax.all_to_all(outgoing.reshape(devices, capacity, half_rows, block_width...  31.1 us
    pallas_call x1, Pallas kernels, grams_of(): pl.pallas_call(gram_kernel(len(lines), kslots, capacity, half_rows), out_...  30.7 us
    pallas_call x1, Pallas kernels, gather_early(): pl.pallas_call(gather_kernel(layout, kslots, capacity), out_shape=[jax.Sh...  27.5 us
    pallas_call x4, Pallas kernels, select_panels(): pl.pallas_call(select_kernel(phase, len(arrays), targets, capacity), out_...  24.9 us
    ppermute x12, starting transfers between devices, across(): return lax.ppermute(array, 'vars', pairs)  13.1 us
  transfers between devices with their start and end apart: 27, of which 11 were waited for; matrix products, arithmetic and copies ran while one was open for 2% of the time, Pallas kernels for 11%

profile of v4, /device:TPU:14, one launch (start us, length us, event | category | flops | bytes accessed | tf_op | source)
XLA Modules:
  0.0 612.6 jit_solution(10964201098422327465)
XLA Ops:
  0.6 3.5 collective-permute-start.5
  4.1 4.0 collective-permute-start.6
  8.1 64.6 %collective-permute-done.5.refs_2_.refs_5_.refs_10_ = bf16[16,128,768]{2,1,0:T(8,128)(2,1)} collective-permute-done((bf16[16,128,768]{2,1,0:T(8,128)(2,1)}, bf16[16,128,768]{2,1,0:T(8,128)(2,1)}, u32[]{:S(2)}, u32[]{:S(2)}) %collective-permute-start.5) | collective-permute-done | bytes 3145760 | tf_op jit(solution)/shard_map/ppermute | solution.py:458
  72.7 3.5 collective-permute-start.12
  76.2 3.7 collective-permute-start.13
  79.9 1.3 copy.23.refs_0_
  81.2 1.3 fusion.6
  82.5 6.2 %select_panels.4 = (bf16[8,128,768]{2,1,0:T(8,128)(2,1)}, bf16[8,128,768]{2,1,0:T(8,128)(2,1)}, bf16[8,128,768]{2,1,0:T(8,128)(2,1)}) custom-call(s32[6]{0:T(128)} %get-tuple-element.52.info_ref, s32[16,8]{1,0:T(8,128)} %copy.23.refs_0_, bf16[16,128,768]{2,1,0:T(8,128)(2,1)} %bitcast.17), custom_call_target="tpu_custom_call" | custom-call | bytes 9437184 | tf_op jit(solution)/shard_map/select_panels/pallas_call | solution.py:76
  89.3 54.5 %collective-permute-done.12.refs_4_.refs_9_.refs_5_.refs_1_ = bf16[16,128,768]{2,1,0:T(8,128)(2,1)S(1)} collective-permute-done((bf16[16,128,768]{2,1,0:T(8,128)(2,1)}, bf16[16,128,768]{2,1,0:T(8,128)(2,1)S(1)}, u32[]{:S(2)}, u32[]{:S(2)}) %collective-permute-start.12) | collective-permute-done | bytes 3145760 | tf_op jit(solution)/shard_map/ppermute | solution.py:458
  143.8 3.5 collective-permute-start.17
  147.3 4.0 collective-permute-start.18
  151.2 1.9 collective-permute-start.3
  153.2 3.9 collective-permute-start.4
  157.1 57.0 %collective-permute-done.3.refs_0_.refs_1_ = s32[16,8]{1,0:T(8,128)S(1)} collective-permute-done((s32[16,8]{1,0:T(8,128)S(1)}, s32[16,8]{1,0:T(8,128)S(1)}, u32[]{:S(2)}, u32[]{:S(2)}) %collective-permute-start.3) | collective-permute-done | bytes 544 | tf_op jit(solution)/shard_map/ppermute | solution.py:458
  214.1 4.4 collective-permute-start.10
  218.5 1.3 collective-permute-start.11
  220.5 4.5 collective-permute-done.11.refs_3_.refs_2_
  225.6 5.8 select_panels.5
  232.1 1.5 collective-permute-start.2
  233.6 1.5 collective-permute-start.7
  235.0 6.4 %select_panels.6 = (bf16[8,128,768]{2,1,0:T(8,128)(2,1)}, bf16[8,128,768]{2,1,0:T(8,128)(2,1)}, bf16[8,128,768]{2,1,0:T(8,128)(2,1)}) custom-call(s32[6]{0:T(128)} %get-tuple-element.52.info_ref, s32[16,8]{1,0:T(8,128)} %copy-done.6, s32[16,8]{1,0:T(8,128)} %copy-done.8, s32[16,8]{1,0:T(8,128)} %copy-done.9, s32[16,8]{1,0:T(8,128)} %copy-done.7, ...), custom_call_target="tpu_custom_call" | custom-call | bytes 9437184 | tf_op jit(solution)/shard_map/select_panels/pallas_call | solution.py:76
  241.5 56.3 %collective-permute-done.1.refs_1_ = bf16[8,128,768]{2,1,0:T(8,128)(2,1)} collective-permute-done((bf16[8,128,768]{2,1,0:T(8,128)(2,1)}, bf16[8,128,768]{2,1,0:T(8,128)(2,1)}, u32[]{:S(2)}, u32[]{:S(2)}) %collective-permute-start.1) | collective-permute-done | bytes 1572896 | tf_op jit(solution)/shard_map/ppermute | solution.py:462
  298.3 1.5 collective-permute-start.9
  299.8 1.5 collective-permute-start.14
  301.4 0.7 constant_dynamic-slice_fusion.1
  302.9 1.5 collective-permute-start.16
  304.4 6.5 %select_panels.7 = (bf16[8,128,768]{2,1,0:T(8,128)(2,1)}, bf16[8,128,768]{2,1,0:T(8,128)(2,1)}, bf16[8,128,768]{2,1,0:T(8,128)(2,1)}) custom-call(s32[6]{0:T(128)} %get-tuple-element.52.info_ref, s32[16,8]{1,0:T(8,128)} %copy-done.10, s32[16,8]{1,0:T(8,128)} %copy-done.6, s32[16,8]{1,0:T(8,128)} %copy-done.7, s32[16,8]{1,0:T(8,128)} %copy-done.11, ...), custom_call_target="tpu_custom_call" | custom-call | bytes 9437184 | tf_op jit(solution)/shard_map/select_panels/pallas_call | solution.py:76
  310.9 59.6 %collective-permute-done.8.refs_4_ = bf16[8,128,768]{2,1,0:T(8,128)(2,1)} collective-permute-done((bf16[8,128,768]{2,1,0:T(8,128)(2,1)}, bf16[8,128,768]{2,1,0:T(8,128)(2,1)}, u32[]{:S(2)}, u32[]{:S(2)}) %collective-permute-start.8) | collective-permute-done | bytes 1572896 | tf_op jit(solution)/shard_map/ppermute | solution.py:462
  371.1 1.3 collective-permute-start.22
  372.4 1.7 collective-permute-start.23
  376.1 0.7 slice.48.panel_ref
  377.4 1.9 stack.8.code_ref
  379.3 1.3 pad_add_fusion.code_ref
  380.6 1.2 and_select_fusion.3
  382.4 55.4 %collective-permute-done.15.refs_7_ = bf16[8,128,768]{2,1,0:T(8,128)(2,1)S(1)} collective-permute-done((bf16[8,128,768]{2,1,0:T(8,128)(2,1)}, bf16[8,128,768]{2,1,0:T(8,128)(2,1)S(1)}, u32[]{:S(2)}, u32[]{:S(2)}) %collective-permute-start.15) | collective-permute-done | bytes 1572896 | tf_op jit(solution)/shard_map/ppermute | solution.py:462
  437.9 1.1 copy-done.3
  439.0 27.5 %gather_early.1 = (f32[16,128,768]{2,1,0:T(8,128)}, bf16[16,1024,768]{2,1,0:T(8,128)(2,1)S(1)}, bf16[32,128,128]{2,1,0:T(8,128)(2,1)}) custom-call(s32[96]{0:T(128)} %slice.46.entry_ref, s32[96]{0:T(128)} %slice.48.panel_ref, s32[12]{0:T(128)} %stack.8.code_ref, s32[128]{0:T(128)} %get-tuple-element.56.late_ref, f32[16,8,128,128]{3,2,1,0:T(8,128)} %omega_ref.3, ...), custom_call_target="tpu_custom_call" | custom-call | flops 3221225472 | bytes 25165824 | tf_op jit(solution)/shard_map/gather_early/pallas_call | solution.py:163
  466.6 35.2 %collective-permute-done.22.refs_5_ = bf16[8,128,768]{2,1,0:T(8,128)(2,1)} collective-permute-done((bf16[8,128,768]{2,1,0:T(8,128)(2,1)}, bf16[8,128,768]{2,1,0:T(8,128)(2,1)}, u32[]{:S(2)}, u32[]{:S(2)}) %collective-permute-start.22) | collective-permute-done | bytes 1572896 | tf_op jit(solution)/shard_map/ppermute | solution.py:462
  501.8 30.7 %grams.1 = (f32[16,8,128,128]{3,2,1,0:T(8,128)}, bf16[16,8,64,128]{3,2,1,0:T(8,128)(2,1)}) custom-call(s32[8]{0:T(128)} %slice_bitcast_fusion.panel_ref, s32[2]{0:T(128)} %pad_add_fusion.code_ref, s32[128]{0:T(128)} %get-tuple-element.56.late_ref, bf16[32,128,128]{2,1,0:T(8,128)(2,1)} %get-tuple-element.34.omega_ref, ...), custom_call_target="tpu_custom_call" | custom-call | flops 3221225472 | bytes 37748736 | tf_op jit(solution)/shard_map/grams/pallas_call | solution.py:264
  532.6 4.4 collective-permute-done.24.came_ref
  537.0 1.3 copy-done.2
  538.3 5.7 outgoing.1
  544.0 9.4 %all-to-all-start = ((bf16[16,8,64,128]{3,2,1,0:T(8,128)(2,1)}), bf16[16,8,64,128]{3,2,1,0:T(8,128)(2,1)S(1)}, u32[]{:S(2)}, u32[]{:S(2)}) async-start(bf16[16,8,64,128]{3,2,1,0:T(8,128)(2,1)} %bitcast.20), calls=%async_computation | async-start | bytes 4194304 | tf_op jit(solution)/shard_map/all_to_all | solution.py:568
  553.4 12.7 %turn.1 = (f32[16,8,64,128]{3,2,1,0:T(8,128)}, bf16[16,8,64,128]{3,2,1,0:T(8,128)(2,1)}) custom-call(s32[1]{0:T(128)} %bitcast.half_ref.part_ref, f32[16,8,128,128]{3,2,1,0:T(8,128)} %get-tuple-element.43.keep_ref.grams_ref), custom_call_target="tpu_custom_call" | custom-call | tf_op jit(solution)/shard_map/turn/pallas_call | solution.py:315
  566.1 4.5 collective-permute-done.25.came_ref
  570.6 31.1 %all-to-all-done = bf16[16,8,64,128]{3,2,1,0:T(8,128)(2,1)S(1)} async-done(((bf16[16,8,64,128]{3,2,1,0:T(8,128)(2,1)}), bf16[16,8,64,128]{3,2,1,0:T(8,128)(2,1)S(1)}, u32[]{:S(2)}, u32[]{:S(2)}) %all-to-all-start) | async-done | bytes 2097184 | tf_op jit(solution)/shard_map/all_to_all | solution.py:568
  601.7 1.3 copy-done.1
  603.1 9.6 %final_step.1 = (f32[16,8,64,128]{3,2,1,0:T(8,128)}, f32[16,8,64,128]{3,2,1,0:T(8,128)}) custom-call(s32[128]{0:T(128)} %get-tuple-element.61.slot_ref, s32[1]{0:T(128)} %bitcast.half_ref.part_ref, f32[16,8,64,128]{3,2,1,0:T(8,128)} %get-tuple-element.44.keep_ref, bf16[16,8,64,128]{3,2,1,0:T(8,128)(2,1)} %collective-permute-done.25.came_ref, ...), custom_call_target="tpu_custom_call" | custom-call | tf_op jit(solution)/shard_map/final_step/pallas_call | solution.py:408
  (64 shorter events, 7.8 us)
Async XLA Ops:
  0.6 72.1 %collective-permute-start.5 = (bf16[16,128,768]{2,1,0:T(8,128)(2,1)}, bf16[16,128,768]{2,1,0:T(8,128)(2,1)}, u32[]{:S(2)}, u32[]{:S(2)}) collective-permute-start(bf16[16,128,768]{2,1,0:T(8,128)(2,1)} %bitcast.15), channel_id=1, source_target_pairs={{0,8},{2,10},{4,12},{6,14},{8,16},{10,18},{12,20},{14,22},{16,24},... | collective-permute-start | bytes 9437192 | tf_op jit(solution)/shard_map/ppermute | solution.py:458
  4.1 72.0 %collective-permute-start.6 = (bf16[16,128,768]{2,1,0:T(8,128)(2,1)}, bf16[16,128,768]{2,1,0:T(8,128)(2,1)}, u32[]{:S(2)}, u32[]{:S(2)}) collective-permute-start(bf16[16,128,768]{2,1,0:T(8,128)(2,1)} %bitcast.16), channel_id=1, source_target_pairs={{8,0},{10,2},{12,4},{14,6},{16,8},{18,10},{20,12},{22,14},{24,16},... | collective-permute-start | bytes 9437192 | tf_op jit(solution)/shard_map/ppermute | solution.py:458
  72.7 71.1 %collective-permute-start.12 = (bf16[16,128,768]{2,1,0:T(8,128)(2,1)}, bf16[16,128,768]{2,1,0:T(8,128)(2,1)S(1)}, u32[]{:S(2)}, u32[]{:S(2)}) collective-permute-start(bf16[16,128,768]{2,1,0:T(8,128)(2,1)} %collective-permute-done.5.refs_2_.refs_5_.refs_10_), channel_id=1, source_target_pairs={{0,8},{2,10},{4,12},{6,14},{8,16},{10,18},{12,20},{14,22},{16,24},... | collective-permute-start | bytes 9437192 | tf_op jit(solution)/shard_map/ppermute | solution.py:458
  76.2 71.1 %collective-permute-start.13 = (bf16[16,128,768]{2,1,0:T(8,128)(2,1)}, bf16[16,128,768]{2,1,0:T(8,128)(2,1)}, u32[]{:S(2)}, u32[]{:S(2)}) collective-permute-start(bf16[16,128,768]{2,1,0:T(8,128)(2,1)} %collective-permute-done.6.refs_3_.refs_6_.refs_11_), channel_id=1, source_target_pairs={{8,0},{10,2},{12,4},{14,6},{16,8},{18,10},{20,12},{22,14},{24,16},... | collective-permute-start | bytes 9437192 | tf_op jit(solution)/shard_map/ppermute | solution.py:458
  82.5 68.8 %copy-start.5 = (s32[16,8]{1,0:T(8,128)S(1)}, s32[16,8]{1,0:T(8,128)}, u32[]{:S(2)}) copy-start(s32[16,8]{1,0:T(8,128)} %copy.23.refs_0_) | copy-start | bytes 1540
  88.7 144.9 %collective-permute-start = (bf16[8,128,768]{2,1,0:T(8,128)(2,1)}, bf16[8,128,768]{2,1,0:T(8,128)(2,1)}, u32[]{:S(2)}, u32[]{:S(2)}) collective-permute-start(bf16[8,128,768]{2,1,0:T(8,128)(2,1)} %get-tuple-element.25), channel_id=1, source_target_pairs={{0,2},{2,0},{4,6},{6,4},{8,10},{10,8},{12,14},{14,12},{16,18},{18,... | collective-permute-start | bytes 4718600 | tf_op jit(solution)/shard_map/ppermute | solution.py:462
  143.8 87.7 %copy-start = (bf16[16,128,768]{2,1,0:T(8,128)(2,1)}, bf16[16,128,768]{2,1,0:T(8,128)(2,1)S(1)}, u32[]{:S(2)}) copy-start(bf16[16,128,768]{2,1,0:T(8,128)(2,1)S(1)} %collective-permute-done.12.refs_4_.refs_9_.refs_5_.refs_1_) | copy-start | bytes 9437188
  143.8 158.6 %collective-permute-start.17 = (bf16[16,128,768]{2,1,0:T(8,128)(2,1)S(1)}, bf16[16,128,768]{2,1,0:T(8,128)(2,1)}, u32[]{:S(2)}, u32[]{:S(2)}) collective-permute-start(bf16[16,128,768]{2,1,0:T(8,128)(2,1)S(1)} %collective-permute-done.12.refs_4_.refs_9_.refs_5_.refs_1_), channel_id=1, source_target_pairs={{0,8},{2,10},{4,12},{6,14},{8,16},{10,18},{12,20},{14,22},{16,24},... | collective-permute-start | bytes 9437192 | tf_op jit(solution)/shard_map/ppermute | solution.py:458
  147.3 155.7 %collective-permute-start.18 = (bf16[16,128,768]{2,1,0:T(8,128)(2,1)}, bf16[16,128,768]{2,1,0:T(8,128)(2,1)}, u32[]{:S(2)}, u32[]{:S(2)}) collective-permute-start(bf16[16,128,768]{2,1,0:T(8,128)(2,1)} %collective-permute-done.13.refs_7_.refs_12_.refs_6_.refs_2_), channel_id=1, source_target_pairs={{8,0},{10,2},{12,4},{14,6},{16,8},{18,10},{20,12},{22,14},{24,16},... | collective-permute-start | bytes 9437192 | tf_op jit(solution)/shard_map/ppermute | solution.py:458
  151.2 62.8 %collective-permute-start.3 = (s32[16,8]{1,0:T(8,128)S(1)}, s32[16,8]{1,0:T(8,128)S(1)}, u32[]{:S(2)}, u32[]{:S(2)}) collective-permute-start(s32[16,8]{1,0:T(8,128)S(1)} %copy-done.5), channel_id=1, source_target_pairs={{0,8},{2,10},{4,12},{6,14},{8,16},{10,18},{12,20},{14,22},{16,24},... | collective-permute-start | bytes 1544 | tf_op jit(solution)/shard_map/ppermute | solution.py:458
  153.2 65.3 %collective-permute-start.4 = (s32[16,8]{1,0:T(8,128)S(1)}, s32[16,8]{1,0:T(8,128)S(1)}, u32[]{:S(2)}, u32[]{:S(2)}) collective-permute-start(s32[16,8]{1,0:T(8,128)S(1)} %copy-done.5), channel_id=1, source_target_pairs={{8,0},{10,2},{12,4},{14,6},{16,8},{18,10},{20,12},{22,14},{24,16},... | collective-permute-start | bytes 1544 | tf_op jit(solution)/shard_map/ppermute | solution.py:458
  214.1 11.5 %copy-start.8 = (s32[16,8]{1,0:T(8,128)}, s32[16,8]{1,0:T(8,128)S(1)}, u32[]{:S(2)}) copy-start(s32[16,8]{1,0:T(8,128)S(1)} %collective-permute-done.3.refs_0_.refs_1_) | copy-start | bytes 1540
  214.1 5.7 collective-permute-start.10
  218.5 7.1 %copy-start.9 = (s32[16,8]{1,0:T(8,128)}, s32[16,8]{1,0:T(8,128)S(1)}, u32[]{:S(2)}) copy-start(s32[16,8]{1,0:T(8,128)S(1)} %collective-permute-done.4.refs_1_.refs_2_) | copy-start | bytes 1540
  218.5 6.4 %collective-permute-start.11 = (s32[16,8]{1,0:T(8,128)S(1)}, s32[16,8]{1,0:T(8,128)S(1)}, u32[]{:S(2)}, u32[]{:S(2)}) collective-permute-start(s32[16,8]{1,0:T(8,128)S(1)} %copy-done.5), channel_id=1, source_target_pairs={{16,0},{18,2},{20,4},{22,6},{24,8},{26,10},{28,12},{30,14},{17,1},... | collective-permute-start | bytes 1544 | tf_op jit(solution)/shard_map/ppermute | solution.py:458
  219.8 11.6 %copy-start.6 = (s32[16,8]{1,0:T(8,128)}, s32[16,8]{1,0:T(8,128)S(1)}, u32[]{:S(2)}) copy-start(s32[16,8]{1,0:T(8,128)S(1)} %collective-permute-done.10.refs_0_.refs_1_) | copy-start | bytes 1540
  219.8 11.7 %collective-permute-start.19 = (s32[16,8]{1,0:T(8,128)S(1)}, s32[16,8]{1,0:T(8,128)S(1)}, u32[]{:S(2)}, u32[]{:S(2)}) collective-permute-start(s32[16,8]{1,0:T(8,128)S(1)} %copy-done.5), channel_id=1, source_target_pairs={{0,24},{2,26},{4,28},{6,30},{1,25},{3,27},{5,29},{7,31}} | collective-permute-start | bytes 1544 | tf_op jit(solution)/shard_map/ppermute | solution.py:458
  224.9 6.5 %copy-start.7 = (s32[16,8]{1,0:T(8,128)}, s32[16,8]{1,0:T(8,128)S(1)}, u32[]{:S(2)}) copy-start(s32[16,8]{1,0:T(8,128)S(1)} %collective-permute-done.11.refs_3_.refs_2_) | copy-start | bytes 1540
  224.9 7.1 %collective-permute-start.20 = (s32[16,8]{1,0:T(8,128)S(1)}, s32[16,8]{1,0:T(8,128)S(1)}, u32[]{:S(2)}, u32[]{:S(2)}) collective-permute-start(s32[16,8]{1,0:T(8,128)S(1)} %copy-done.5), channel_id=1, source_target_pairs={{24,0},{26,2},{28,4},{30,6},{25,1},{27,3},{29,5},{31,7}} | collective-permute-start | bytes 1544 | tf_op jit(solution)/shard_map/ppermute | solution.py:458
  231.5 10.0 %copy-start.10 = (s32[16,8]{1,0:T(8,128)}, s32[16,8]{1,0:T(8,128)S(1)}, u32[]{:S(2)}) copy-start(s32[16,8]{1,0:T(8,128)S(1)} %collective-permute-done.19.refs_0_) | copy-start | bytes 1540
  231.5 66.3 %collective-permute-start.1 = (bf16[8,128,768]{2,1,0:T(8,128)(2,1)}, bf16[8,128,768]{2,1,0:T(8,128)(2,1)}, u32[]{:S(2)}, u32[]{:S(2)}) collective-permute-start(bf16[8,128,768]{2,1,0:T(8,128)(2,1)} %get-tuple-element.26), channel_id=1, source_target_pairs={{0,4},{2,6},{4,0},{6,2},{8,12},{10,14},{12,8},{14,10},{16,20},{18,... | collective-permute-start | bytes 4718600 | tf_op jit(solution)/shard_map/ppermute | solution.py:462
  232.1 9.4 %copy-start.11 = (s32[16,8]{1,0:T(8,128)}, s32[16,8]{1,0:T(8,128)S(1)}, u32[]{:S(2)}) copy-start(s32[16,8]{1,0:T(8,128)S(1)} %collective-permute-done.20.refs_3_) | copy-start | bytes 1540
  232.1 66.2 %collective-permute-start.2 = (bf16[8,128,768]{2,1,0:T(8,128)(2,1)}, bf16[8,128,768]{2,1,0:T(8,128)(2,1)}, u32[]{:S(2)}, u32[]{:S(2)}) collective-permute-start(bf16[8,128,768]{2,1,0:T(8,128)(2,1)} %get-tuple-element.27), channel_id=1, source_target_pairs={{0,6},{2,4},{4,2},{6,0},{8,14},{10,12},{12,10},{14,8},{16,22},{18,... | collective-permute-start | bytes 4718600 | tf_op jit(solution)/shard_map/ppermute | solution.py:462
  233.6 66.2 %collective-permute-start.7 = (bf16[8,128,768]{2,1,0:T(8,128)(2,1)}, bf16[8,128,768]{2,1,0:T(8,128)(2,1)}, u32[]{:S(2)}, u32[]{:S(2)}) collective-permute-start(bf16[8,128,768]{2,1,0:T(8,128)(2,1)} %get-tuple-element.28), channel_id=1, source_target_pairs={{0,2},{2,0},{4,6},{6,4},{8,10},{10,8},{12,14},{14,12},{16,18},{18,... | collective-permute-start | bytes 4718600 | tf_op jit(solution)/shard_map/ppermute | solution.py:462
  297.8 72.8 %collective-permute-start.8 = (bf16[8,128,768]{2,1,0:T(8,128)(2,1)}, bf16[8,128,768]{2,1,0:T(8,128)(2,1)}, u32[]{:S(2)}, u32[]{:S(2)}) collective-permute-start(bf16[8,128,768]{2,1,0:T(8,128)(2,1)} %get-tuple-element.29), channel_id=1, source_target_pairs={{0,4},{2,6},{4,0},{6,2},{8,12},{10,14},{12,8},{14,10},{16,20},{18,... | collective-permute-start | bytes 4718600 | tf_op jit(solution)/shard_map/ppermute | solution.py:462
  298.3 72.8 %collective-permute-start.9 = (bf16[8,128,768]{2,1,0:T(8,128)(2,1)}, bf16[8,128,768]{2,1,0:T(8,128)(2,1)}, u32[]{:S(2)}, u32[]{:S(2)}) collective-permute-start(bf16[8,128,768]{2,1,0:T(8,128)(2,1)} %get-tuple-element.30), channel_id=1, source_target_pairs={{0,6},{2,4},{4,2},{6,0},{8,14},{10,12},{12,10},{14,8},{16,22},{18,... | collective-permute-start | bytes 4718600 | tf_op jit(solution)/shard_map/ppermute | solution.py:462
  299.8 72.5 %collective-permute-start.14 = (bf16[8,128,768]{2,1,0:T(8,128)(2,1)}, bf16[8,128,768]{2,1,0:T(8,128)(2,1)}, u32[]{:S(2)}, u32[]{:S(2)}) collective-permute-start(bf16[8,128,768]{2,1,0:T(8,128)(2,1)} %get-tuple-element.31), channel_id=1, source_target_pairs={{0,2},{2,0},{4,6},{6,4},{8,10},{10,8},{12,14},{14,12},{16,18},{18,... | collective-permute-start | bytes 4718600 | tf_op jit(solution)/shard_map/ppermute | solution.py:462
  302.4 135.5 %collective-permute-start.15 = (bf16[8,128,768]{2,1,0:T(8,128)(2,1)}, bf16[8,128,768]{2,1,0:T(8,128)(2,1)S(1)}, u32[]{:S(2)}, u32[]{:S(2)}) collective-permute-start(bf16[8,128,768]{2,1,0:T(8,128)(2,1)} %get-tuple-element.32), channel_id=1, source_target_pairs={{0,4},{2,6},{4,0},{6,2},{8,12},{10,14},{12,8},{14,10},{16,20},{18,... | collective-permute-start | bytes 4718600 | tf_op jit(solution)/shard_map/ppermute | solution.py:462
  302.9 134.9 %collective-permute-start.16 = (bf16[8,128,768]{2,1,0:T(8,128)(2,1)}, bf16[8,128,768]{2,1,0:T(8,128)(2,1)}, u32[]{:S(2)}, u32[]{:S(2)}) collective-permute-start(bf16[8,128,768]{2,1,0:T(8,128)(2,1)} %get-tuple-element.33), channel_id=1, source_target_pairs={{0,6},{2,4},{4,2},{6,0},{8,14},{10,12},{12,10},{14,8},{16,22},{18,... | collective-permute-start | bytes 4718600 | tf_op jit(solution)/shard_map/ppermute | solution.py:462
  370.6 96.0 %collective-permute-start.21 = (bf16[8,128,768]{2,1,0:T(8,128)(2,1)}, bf16[8,128,768]{2,1,0:T(8,128)(2,1)S(1)}, u32[]{:S(2)}, u32[]{:S(2)}) collective-permute-start(bf16[8,128,768]{2,1,0:T(8,128)(2,1)} %get-tuple-element.37), channel_id=1, source_target_pairs={{0,2},{2,0},{4,6},{6,4},{8,10},{10,8},{12,14},{14,12},{16,18},{18,... | collective-permute-start | bytes 4718600 | tf_op jit(solution)/shard_map/ppermute | solution.py:462
  371.1 130.7 %collective-permute-start.22 = (bf16[8,128,768]{2,1,0:T(8,128)(2,1)}, bf16[8,128,768]{2,1,0:T(8,128)(2,1)}, u32[]{:S(2)}, u32[]{:S(2)}) collective-permute-start(bf16[8,128,768]{2,1,0:T(8,128)(2,1)} %get-tuple-element.38), channel_id=1, source_target_pairs={{0,4},{2,6},{4,0},{6,2},{8,12},{10,14},{12,8},{14,10},{16,20},{18,... | collective-permute-start | bytes 4718600 | tf_op jit(solution)/shard_map/ppermute | solution.py:462
  372.4 129.5 %collective-permute-start.23 = (bf16[8,128,768]{2,1,0:T(8,128)(2,1)}, bf16[8,128,768]{2,1,0:T(8,128)(2,1)}, u32[]{:S(2)}, u32[]{:S(2)}) collective-permute-start(bf16[8,128,768]{2,1,0:T(8,128)(2,1)} %get-tuple-element.39), channel_id=1, source_target_pairs={{0,6},{2,4},{4,2},{6,0},{8,14},{10,12},{12,10},{14,8},{16,22},{18,... | collective-permute-start | bytes 4718600 | tf_op jit(solution)/shard_map/ppermute | solution.py:462
  437.9 1.1 copy-start.3
  466.6 35.3 %copy-start.4 = (bf16[8,128,768]{2,1,0:T(8,128)(2,1)}, bf16[8,128,768]{2,1,0:T(8,128)(2,1)S(1)}, u32[]{:S(2)}) copy-start(bf16[8,128,768]{2,1,0:T(8,128)(2,1)S(1)} %collective-permute-done.21.refs_4_) | copy-start | bytes 4718596
  532.5 4.4 collective-permute-start.24
  537.0 1.3 copy-start.2
  544.0 57.7 %all-to-all-start = ((bf16[16,8,64,128]{3,2,1,0:T(8,128)(2,1)}), bf16[16,8,64,128]{3,2,1,0:T(8,128)(2,1)S(1)}, u32[]{:S(2)}, u32[]{:S(2)}) async-start(bf16[16,8,64,128]{3,2,1,0:T(8,128)(2,1)} %bitcast.20), calls=%async_computation | async-start | bytes 4194304 | tf_op jit(solution)/shard_map/all_to_all | solution.py:568
  566.1 4.5 collective-permute-start.25
  601.7 1.3 copy-start.1

commit v5 on v4

--- a/solution.py
+++ b/solution.py
@@ -192,37 +192,51 @@
 
 
 def gram_kernel(line_count, kslots, capacity, half_rows):
-    def body(panel_ref, code_ref, late_ref, omega_ref, part_ref, rows_ref, *refs):
+    def body(panel_ref, code_ref, late_ref, entry_ref, omega_ref, part_ref, rows_ref, *refs):
         lines = refs[:line_count]
-        came = refs[line_count:-5]
-        grams_ref, send_ref, held, w_row, held_sem = refs[-5:]
+        came = refs[line_count:-6]
+        grams_ref, send_ref, table, spare, w_row, sem = refs[-6:]
         row = pl.program_id(0)
         block_width = w_row.shape[0]
+
+        def place(panel, c):
+            entry = entry_ref[c]
+
+            @pl.when(entry >= 0)
+            def _():
+                at = pl.multiple_of((entry % kslots) * block_width, block_width)
+                pltpu.make_async_copy(
+                    panel, table.at[entry // kslots, pl.ds(at, block_width)], sem.at[0]
+                ).start()
+
+            @pl.when(entry < 0)
+            def _():
+                pltpu.make_async_copy(panel, spare.at[c], sem.at[0]).start()
 
         @pl.when(row == 0)
         def _():
             for mask, block in enumerate(came):
-                at = pl.ds((mask + 1) * capacity, capacity)
-                pltpu.make_async_copy(block, held.at[at], held_sem.at[0]).start()
+                for c in range(capacity):
+                    place(block.at[c], (mask + 1) * capacity + c)
             for k in range(line_count):
 
                 @pl.when(code_ref[0] == k)
                 def _(k=k):
                     for c in range(capacity):
-                        pltpu.make_async_copy(
-                            lines[k].at[panel_ref[c]], held.at[c], held_sem.at[0]
-                        ).start()
-
-            pltpu.make_async_copy(held, held, held_sem.at[0]).wait()
+                        place(lines[k].at[panel_ref[c]], c)
+
+            pltpu.make_async_copy(spare, spare, sem.at[0]).wait()
 
         w_row[...] = part_ref[0]
         for s in range(1, kslots):
             late = late_ref[row * kslots + s]
 
             @pl.when(late >= 0)
-            def _(late=late):
+            def _(s=s, late=late):
                 w_row[...] += jnp.dot(
-                    omega_ref[late], held[late], preferred_element_type=jnp.float32
+                    omega_ref[late],
+                    table[row, s * block_width : (s + 1) * block_width],
+                    preferred_element_type=jnp.float32,
                 )
 
         w_low = w_row[...].astype(jnp.bfloat16)
@@ -236,27 +250,17 @@
             )
 
         flipped = lax.dot_general(
-            rows_ref[row], w_low, contract, preferred_element_type=jnp.float32
+            table[row], w_low, contract, preferred_element_type=jnp.float32
         )
         for s in range(kslots):
             store(s, flipped[s * block_width : (s + 1) * block_width])
-        for s in range(1, kslots):
-            late = late_ref[row * kslots + s]
-
-            @pl.when(late >= 0)
-            def _(s=s, late=late):
-                block = lax.dot_general(
-                    held[late],
-                    w_row[...].astype(jnp.bfloat16),
-                    contract,
-                    preferred_element_type=jnp.float32,
-                )
-                store(s, block)
 
     return body
 
 
-def grams_of(panel_ids, codes, late, omega_late, part, rows, lines, came, capacity, half_rows):
+def grams_of(
+    panel_ids, codes, late, entries, omega_late, part, rows, lines, came, capacity, half_rows
+):
     row_count, block_width, samples = part.shape
     kslots = rows.shape[1] // block_width
     whole = (row_count, kslots, block_width, block_width)
@@ -266,9 +270,10 @@
         out_shape=[
             jax.ShapeDtypeStruct(whole, jnp.float32),
             jax.ShapeDtypeStruct((row_count, kslots, half_rows, block_width), jnp.bfloat16),
+            pltpu.VMEM(rows.shape, rows.dtype),
         ],
         grid_spec=pltpu.PrefetchScalarGridSpec(
-            num_scalar_prefetch=3,
+            num_scalar_prefetch=4,
             grid=(row_count,),
             in_specs=[
                 pl.BlockSpec(omega_late.shape, lambda i, *_: (0, 0, 0)),
@@ -279,6 +284,7 @@
             out_specs=[
                 pl.BlockSpec((1, kslots, block_width, block_width), lambda i, *_: (i, 0, 0, 0)),
                 pl.BlockSpec((1, kslots, half_rows, block_width), lambda i, *_: (i, 0, 0, 0)),
+                pl.BlockSpec(memory_space=pltpu.VMEM),
             ],
             scratch_shapes=[
                 pltpu.VMEM(((1 + len(came)) * capacity, block_width, samples), jnp.bfloat16),
@@ -294,8 +300,9 @@
             transcendentals=0,
             bytes_accessed=(kslots + 4) * row_count * block_width * samples * 2,
         ),
+        input_output_aliases={6: 2},
         name="grams",
-    )(panel_ids, codes, late, omega_late, part, rows, *lines, *came)
+    )(panel_ids, codes, late, entries, omega_late, part, rows, *lines, *came)
 
 
 def turn_kernel(part_ref, grams_ref, keep_ref, send_ref):
@@ -546,10 +553,11 @@
         plane * capacity,
     )
     rows = pltpu.with_memory_space_constraint(rows, pltpu.VMEM)
-    grams, send_col = grams_of(
+    grams, send_col, _ = grams_of(
         panel_table[early : early + capacity],
         jnp.stack([info[2 + last], sample_part]),
         late,
+        entry_table[early:],
         omega_late,
         part,
         rows,

time: 615 us -> 606 us (0.985)
  waiting for transfers between devices: 427 us -> 370 us
  starting transfers between devices: 57.5 us -> 112 us
    ppermute x12, starting transfers between devices: 34.9 us -> 93.2 us  [along(): return lax.ppermute(array, 'vars', pairs)]
    ppermute x12, waiting for transfers between devices: 181 us -> 124 us  [along(): return lax.ppermute(array, 'vars', pairs)]
    pallas_call x1, Pallas kernels: 30.7 us -> 24.4 us  [grams_of(): pl.pallas_call(gram_kernel(len(lines), kslots, capacity, half_rows), out_...]
  transfers between devices with their start and end apart: 27 -> 27, of which waited for: 11 -> 10; matrix products, arithmetic and copies ran while one was open for 2% -> 2% of each run, Pallas kernels for 11% -> 11%
where the time goes in v5:
time: 606 us; the launch traced here: 604 us
  waiting for transfers between devices  370 us (61%)
  starting transfers between devices  112 us (18%)
  Pallas kernels  105 us (17%)
  local copies, waits for them, and re-layouts  12.1 us (2%)
    ppermute x12, waiting for transfers between devices, across(): return lax.ppermute(array, 'vars', pairs)  206 us
    ppermute x12, waiting for transfers between devices, along(): return lax.ppermute(array, 'vars', pairs)  124 us
    ppermute x12, starting transfers between devices, along(): return lax.ppermute(array, 'vars', pairs)  93.2 us
    all_to_all x1, waiting for transfers between devices, step_on_device(): lax.all_to_all(outgoing.reshape(devices, capacity, half_rows, block_width...  31.1 us
    pallas_call x1, Pallas kernels, gather_early(): pl.pallas_call(gather_kernel(layout, kslots, capacity), out_shape=[jax.Sh...  27.5 us
    pallas_call x4, Pallas kernels, select_panels(): pl.pallas_call(select_kernel(phase, len(arrays), targets, capacity), out_...  25 us
    pallas_call x1, Pallas kernels, grams_of(): pl.pallas_call(gram_kernel(len(lines), kslots, capacity, half_rows), out_...  24.4 us
    ppermute x12, starting transfers between devices, across(): return lax.ppermute(array, 'vars', pairs)  13.1 us
  transfers between devices with their start and end apart: 27, of which 10 were waited for; matrix products, arithmetic and copies ran while one was open for 2% of the time, Pallas kernels for 11%

profile of v5, /device:TPU:14, one launch (start us, length us, event | category | flops | bytes accessed | tf_op | source)
XLA Modules:
  0.0 603.9 jit_solution(15153649793053535516)
XLA Ops:
  0.6 2.4 collective-permute-start.6
  3.0 3.5 collective-permute-start.5
  6.5 66.2 %collective-permute-done.6.refs_3_.refs_6_.refs_11_ = bf16[16,128,768]{2,1,0:T(8,128)(2,1)} collective-permute-done((bf16[16,128,768]{2,1,0:T(8,128)(2,1)}, bf16[16,128,768]{2,1,0:T(8,128)(2,1)}, u32[]{:S(2)}, u32[]{:S(2)}) %collective-permute-start.6) | collective-permute-done | bytes 3145760 | tf_op jit(solution)/shard_map/ppermute | solution.py:465
  72.7 2.3 collective-permute-start.13
  75.0 4.0 collective-permute-start.12
  79.0 1.3 copy.24.refs_0_
  80.4 1.3 fusion.6
  81.6 6.2 %select_panels.4 = (bf16[8,128,768]{2,1,0:T(8,128)(2,1)}, bf16[8,128,768]{2,1,0:T(8,128)(2,1)}, bf16[8,128,768]{2,1,0:T(8,128)(2,1)}) custom-call(s32[6]{0:T(128)} %get-tuple-element.52.info_ref, s32[16,8]{1,0:T(8,128)} %copy.24.refs_0_, bf16[16,128,768]{2,1,0:T(8,128)(2,1)} %bitcast.18), custom_call_target="tpu_custom_call" | custom-call | bytes 9437184 | tf_op jit(solution)/shard_map/select_panels/pallas_call | solution.py:76
  88.4 55.3 %collective-permute-done.13.refs_7_.refs_12_.refs_6_.refs_2_ = bf16[16,128,768]{2,1,0:T(8,128)(2,1)S(1)} collective-permute-done((bf16[16,128,768]{2,1,0:T(8,128)(2,1)}, bf16[16,128,768]{2,1,0:T(8,128)(2,1)S(1)}, u32[]{:S(2)}, u32[]{:S(2)}) %collective-permute-start.13) | collective-permute-done | bytes 3145760 | tf_op jit(solution)/shard_map/ppermute | solution.py:465
  143.8 2.3 collective-permute-start.18
  146.1 3.8 collective-permute-start.17
  149.9 0.7 collective-permute-start.20
  150.6 0.7 collective-permute-start.19
  151.3 67.2 %collective-permute-start.4 = (s32[16,8]{1,0:T(8,128)S(1)}, s32[16,8]{1,0:T(8,128)S(1)}, u32[]{:S(2)}, u32[]{:S(2)}) collective-permute-start(s32[16,8]{1,0:T(8,128)S(1)} %copy-done.5), channel_id=1, source_target_pairs={{8,0},{10,2},{12,4},{14,6},{16,8},{18,10},{20,12},{22,14},{24,16},... | collective-permute-start | bytes 1544 | tf_op jit(solution)/shard_map/ppermute | solution.py:465
  218.5 1.9 collective-permute-start.3
  220.5 1.3 collective-permute-start.11
  221.8 2.3 collective-permute-done.3.refs_0_.refs_1_
  224.1 3.2 collective-permute-start.10
  227.3 5.8 select_panels.5
  233.7 1.5 collective-permute-start.2
  235.2 1.5 collective-permute-start.7
  236.7 6.4 %select_panels.6 = (bf16[8,128,768]{2,1,0:T(8,128)(2,1)}, bf16[8,128,768]{2,1,0:T(8,128)(2,1)}, bf16[8,128,768]{2,1,0:T(8,128)(2,1)}) custom-call(s32[6]{0:T(128)} %get-tuple-element.52.info_ref, s32[16,8]{1,0:T(8,128)} %copy-done.7, s32[16,8]{1,0:T(8,128)} %copy-done.9, s32[16,8]{1,0:T(8,128)} %copy-done.8, s32[16,8]{1,0:T(8,128)} %copy-done.6, ...), custom_call_target="tpu_custom_call" | custom-call | bytes 9437184 | tf_op jit(solution)/shard_map/select_panels/pallas_call | solution.py:76
  243.1 56.5 %collective-permute-done.1.refs_1_ = bf16[8,128,768]{2,1,0:T(8,128)(2,1)} collective-permute-done((bf16[8,128,768]{2,1,0:T(8,128)(2,1)}, bf16[8,128,768]{2,1,0:T(8,128)(2,1)}, u32[]{:S(2)}, u32[]{:S(2)}) %collective-permute-start.1) | collective-permute-done | bytes 1572896 | tf_op jit(solution)/shard_map/ppermute | solution.py:469
  300.2 1.5 collective-permute-start.9
  301.7 1.5 collective-permute-start.14
  303.3 0.7 constant_dynamic-slice_fusion.1
  304.8 1.5 collective-permute-start.16
  306.3 6.6 %select_panels.7 = (bf16[8,128,768]{2,1,0:T(8,128)(2,1)}, bf16[8,128,768]{2,1,0:T(8,128)(2,1)}, bf16[8,128,768]{2,1,0:T(8,128)(2,1)}) custom-call(s32[6]{0:T(128)} %get-tuple-element.52.info_ref, s32[16,8]{1,0:T(8,128)} %copy-done.11, s32[16,8]{1,0:T(8,128)} %copy-done.7, s32[16,8]{1,0:T(8,128)} %copy-done.6, s32[16,8]{1,0:T(8,128)} %copy-done.10, ...), custom_call_target="tpu_custom_call" | custom-call | bytes 9437184 | tf_op jit(solution)/shard_map/select_panels/pallas_call | solution.py:76
  312.9 59.6 %collective-permute-done.8.refs_4_ = bf16[8,128,768]{2,1,0:T(8,128)(2,1)} collective-permute-done((bf16[8,128,768]{2,1,0:T(8,128)(2,1)}, bf16[8,128,768]{2,1,0:T(8,128)(2,1)}, u32[]{:S(2)}, u32[]{:S(2)}) %collective-permute-start.8) | collective-permute-done | bytes 1572896 | tf_op jit(solution)/shard_map/ppermute | solution.py:469
  373.0 1.2 collective-permute-start.22
  374.2 1.7 collective-permute-start.23
  379.9 1.9 stack.8.code_ref
  381.7 1.2 pad_add_fusion.code_ref
  383.0 1.2 and_select_fusion.3
  384.8 55.0 %collective-permute-done.15.refs_7_ = bf16[8,128,768]{2,1,0:T(8,128)(2,1)S(1)} collective-permute-done((bf16[8,128,768]{2,1,0:T(8,128)(2,1)}, bf16[8,128,768]{2,1,0:T(8,128)(2,1)S(1)}, u32[]{:S(2)}, u32[]{:S(2)}) %collective-permute-start.15) | collective-permute-done | bytes 1572896 | tf_op jit(solution)/shard_map/ppermute | solution.py:469
  439.8 1.1 copy-done.3
  440.9 27.5 %gather_early.1 = (f32[16,128,768]{2,1,0:T(8,128)}, bf16[16,1024,768]{2,1,0:T(8,128)(2,1)S(1)}, bf16[32,128,128]{2,1,0:T(8,128)(2,1)}) custom-call(s32[96]{0:T(128)} %slice.54.entry_ref, s32[96]{0:T(128)} %slice.56.panel_ref, s32[12]{0:T(128)} %stack.8.code_ref, s32[128]{0:T(128)} %get-tuple-element.56.late_ref, f32[16,8,128,128]{3,2,1,0:T(8,128)} %omega_ref.3, ...), custom_call_target="tpu_custom_call" | custom-call | flops 3221225472 | bytes 25165824 | tf_op jit(solution)/shard_map/gather_early/pallas_call | solution.py:163
  468.5 35.2 %collective-permute-done.22.refs_5_ = bf16[8,128,768]{2,1,0:T(8,128)(2,1)} collective-permute-done((bf16[8,128,768]{2,1,0:T(8,128)(2,1)}, bf16[8,128,768]{2,1,0:T(8,128)(2,1)}, u32[]{:S(2)}, u32[]{:S(2)}) %collective-permute-start.22) | collective-permute-done | bytes 1572896 | tf_op jit(solution)/shard_map/ppermute | solution.py:469
  503.7 24.4 %grams.1 = (f32[16,8,128,128]{3,2,1,0:T(8,128)}, bf16[16,8,64,128]{3,2,1,0:T(8,128)(2,1)}, bf16[16,1024,768]{2,1,0:T(8,128)(2,1)S(1)}) custom-call(s32[8]{0:T(128)} %slice_bitcast_fusion.panel_ref, s32[2]{0:T(128)} %pad_add_fusion.code_ref, s32[128]{0:T(128)} %get-tuple-element.56.late_ref, s32[32]{0:T(128)} %slice.52.entry_ref, ...), custom_call_target="tpu_custom_call", output_to_operand_aliasing={{2}: (6, {})} | custom-call | flops 3221225472 | bytes 37748736 | tf_op jit(solution)/shard_map/grams/pallas_call | solution.py:268
  528.2 4.4 collective-permute-done.24.came_ref
  532.6 1.3 copy-done.2
  533.9 5.7 outgoing.1
  539.6 5.1 all-to-all-start
  544.7 12.7 %turn.1 = (f32[16,8,64,128]{3,2,1,0:T(8,128)}, bf16[16,8,64,128]{3,2,1,0:T(8,128)(2,1)}) custom-call(s32[1]{0:T(128)} %bitcast.half_ref.part_ref, f32[16,8,128,128]{3,2,1,0:T(8,128)} %get-tuple-element.43.keep_ref.grams_ref), custom_call_target="tpu_custom_call" | custom-call | tf_op jit(solution)/shard_map/turn/pallas_call | solution.py:322
  557.4 4.5 collective-permute-done.25.came_ref
  561.9 31.1 %all-to-all-done = bf16[16,8,64,128]{3,2,1,0:T(8,128)(2,1)S(1)} async-done(((bf16[16,8,64,128]{3,2,1,0:T(8,128)(2,1)}), bf16[16,8,64,128]{3,2,1,0:T(8,128)(2,1)S(1)}, u32[]{:S(2)}, u32[]{:S(2)}) %all-to-all-start) | async-done | bytes 2097184 | tf_op jit(solution)/shard_map/all_to_all | solution.py:576
  593.0 1.3 copy-done.1
  594.3 9.6 %final_step.1 = (f32[16,8,64,128]{3,2,1,0:T(8,128)}, f32[16,8,64,128]{3,2,1,0:T(8,128)}) custom-call(s32[128]{0:T(128)} %get-tuple-element.61.slot_ref, s32[1]{0:T(128)} %bitcast.half_ref.part_ref, f32[16,8,64,128]{3,2,1,0:T(8,128)} %get-tuple-element.44.keep_ref, bf16[16,8,64,128]{3,2,1,0:T(8,128)(2,1)} %collective-permute-done.25.came_ref, ...), custom_call_target="tpu_custom_call" | custom-call | tf_op jit(solution)/shard_map/final_step/pallas_call | solution.py:415
  (66 shorter events, 7.7 us)
Async XLA Ops:
  0.6 72.1 %collective-permute-start.6 = (bf16[16,128,768]{2,1,0:T(8,128)(2,1)}, bf16[16,128,768]{2,1,0:T(8,128)(2,1)}, u32[]{:S(2)}, u32[]{:S(2)}) collective-permute-start(bf16[16,128,768]{2,1,0:T(8,128)(2,1)} %bitcast.16), channel_id=1, source_target_pairs={{8,0},{10,2},{12,4},{14,6},{16,8},{18,10},{20,12},{22,14},{24,16},... | collective-permute-start | bytes 9437192 | tf_op jit(solution)/shard_map/ppermute | solution.py:465
  3.0 72.0 %collective-permute-start.5 = (bf16[16,128,768]{2,1,0:T(8,128)(2,1)}, bf16[16,128,768]{2,1,0:T(8,128)(2,1)}, u32[]{:S(2)}, u32[]{:S(2)}) collective-permute-start(bf16[16,128,768]{2,1,0:T(8,128)(2,1)} %bitcast.17), channel_id=1, source_target_pairs={{0,8},{2,10},{4,12},{6,14},{8,16},{10,18},{12,20},{14,22},{16,24},... | collective-permute-start | bytes 9437192 | tf_op jit(solution)/shard_map/ppermute | solution.py:465
  72.7 71.1 %collective-permute-start.13 = (bf16[16,128,768]{2,1,0:T(8,128)(2,1)}, bf16[16,128,768]{2,1,0:T(8,128)(2,1)S(1)}, u32[]{:S(2)}, u32[]{:S(2)}) collective-permute-start(bf16[16,128,768]{2,1,0:T(8,128)(2,1)} %collective-permute-done.6.refs_3_.refs_6_.refs_11_), channel_id=1, source_target_pairs={{8,0},{10,2},{12,4},{14,6},{16,8},{18,10},{20,12},{22,14},{24,16},... | collective-permute-start | bytes 9437192 | tf_op jit(solution)/shard_map/ppermute | solution.py:465
  75.0 71.1 %collective-permute-start.12 = (bf16[16,128,768]{2,1,0:T(8,128)(2,1)}, bf16[16,128,768]{2,1,0:T(8,128)(2,1)}, u32[]{:S(2)}, u32[]{:S(2)}) collective-permute-start(bf16[16,128,768]{2,1,0:T(8,128)(2,1)} %collective-permute-done.5.refs_2_.refs_5_.refs_10_), channel_id=1, source_target_pairs={{0,8},{2,10},{4,12},{6,14},{8,16},{10,18},{12,20},{14,22},{16,24},... | collective-permute-start | bytes 9437192 | tf_op jit(solution)/shard_map/ppermute | solution.py:465
  81.6 68.3 %copy-start.5 = (s32[16,8]{1,0:T(8,128)S(1)}, s32[16,8]{1,0:T(8,128)}, u32[]{:S(2)}) copy-start(s32[16,8]{1,0:T(8,128)} %copy.24.refs_0_) | copy-start | bytes 1540
  87.8 147.4 %collective-permute-start = (bf16[8,128,768]{2,1,0:T(8,128)(2,1)}, bf16[8,128,768]{2,1,0:T(8,128)(2,1)}, u32[]{:S(2)}, u32[]{:S(2)}) collective-permute-start(bf16[8,128,768]{2,1,0:T(8,128)(2,1)} %get-tuple-element.25), channel_id=1, source_target_pairs={{0,2},{2,0},{4,6},{6,4},{8,10},{10,8},{12,14},{14,12},{16,18},{18,... | collective-permute-start | bytes 4718600 | tf_op jit(solution)/shard_map/ppermute | solution.py:469
  143.8 89.4 %copy-start = (bf16[16,128,768]{2,1,0:T(8,128)(2,1)}, bf16[16,128,768]{2,1,0:T(8,128)(2,1)S(1)}, u32[]{:S(2)}) copy-start(bf16[16,128,768]{2,1,0:T(8,128)(2,1)S(1)} %collective-permute-done.13.refs_7_.refs_12_.refs_6_.refs_2_) | copy-start | bytes 9437188
  143.8 160.5 %collective-permute-start.18 = (bf16[16,128,768]{2,1,0:T(8,128)(2,1)S(1)}, bf16[16,128,768]{2,1,0:T(8,128)(2,1)}, u32[]{:S(2)}, u32[]{:S(2)}) collective-permute-start(bf16[16,128,768]{2,1,0:T(8,128)(2,1)S(1)} %collective-permute-done.13.refs_7_.refs_12_.refs_6_.refs_2_), channel_id=1, source_target_pairs={{8,0},{10,2},{12,4},{14,6},{16,8},{18,10},{20,12},{22,14},{24,16},... | collective-permute-start | bytes 9437192 | tf_op jit(solution)/shard_map/ppermute | solution.py:465
  146.1 158.7 %collective-permute-start.17 = (bf16[16,128,768]{2,1,0:T(8,128)(2,1)}, bf16[16,128,768]{2,1,0:T(8,128)(2,1)}, u32[]{:S(2)}, u32[]{:S(2)}) collective-permute-start(bf16[16,128,768]{2,1,0:T(8,128)(2,1)} %collective-permute-done.12.refs_4_.refs_9_.refs_5_.refs_1_), channel_id=1, source_target_pairs={{0,8},{2,10},{4,12},{6,14},{8,16},{10,18},{12,20},{14,22},{16,24},... | collective-permute-start | bytes 9437192 | tf_op jit(solution)/shard_map/ppermute | solution.py:465
  149.9 1.3 collective-permute-start.20
  150.6 67.9 %collective-permute-start.19 = (s32[16,8]{1,0:T(8,128)S(1)}, s32[16,8]{1,0:T(8,128)S(1)}, u32[]{:S(2)}, u32[]{:S(2)}) collective-permute-start(s32[16,8]{1,0:T(8,128)S(1)} %copy-done.5), channel_id=1, source_target_pairs={{0,24},{2,26},{4,28},{6,30},{1,25},{3,27},{5,29},{7,31}} | collective-permute-start | bytes 1544 | tf_op jit(solution)/shard_map/ppermute | solution.py:465
  151.3 91.8 %copy-start.10 = (s32[16,8]{1,0:T(8,128)}, s32[16,8]{1,0:T(8,128)S(1)}, u32[]{:S(2)}) copy-start(s32[16,8]{1,0:T(8,128)S(1)} %collective-permute-done.20.refs_3_) | copy-start | bytes 1540
  151.3 69.2 %collective-permute-start.4 = (s32[16,8]{1,0:T(8,128)S(1)}, s32[16,8]{1,0:T(8,128)S(1)}, u32[]{:S(2)}, u32[]{:S(2)}) collective-permute-start(s32[16,8]{1,0:T(8,128)S(1)} %copy-done.5), channel_id=1, source_target_pairs={{8,0},{10,2},{12,4},{14,6},{16,8},{18,10},{20,12},{22,14},{24,16},... | collective-permute-start | bytes 1544 | tf_op jit(solution)/shard_map/ppermute | solution.py:465
  218.5 24.6 %copy-start.11 = (s32[16,8]{1,0:T(8,128)}, s32[16,8]{1,0:T(8,128)S(1)}, u32[]{:S(2)}) copy-start(s32[16,8]{1,0:T(8,128)S(1)} %collective-permute-done.19.refs_0_) | copy-start | bytes 1540
  218.5 5.5 collective-permute-start.3
  220.5 6.8 %copy-start.8 = (s32[16,8]{1,0:T(8,128)}, s32[16,8]{1,0:T(8,128)S(1)}, u32[]{:S(2)}) copy-start(s32[16,8]{1,0:T(8,128)S(1)} %collective-permute-done.4.refs_1_.refs_2_) | copy-start | bytes 1540
  220.5 12.6 %collective-permute-start.11 = (s32[16,8]{1,0:T(8,128)S(1)}, s32[16,8]{1,0:T(8,128)S(1)}, u32[]{:S(2)}, u32[]{:S(2)}) collective-permute-start(s32[16,8]{1,0:T(8,128)S(1)} %copy-done.5), channel_id=1, source_target_pairs={{16,0},{18,2},{20,4},{22,6},{24,8},{26,10},{28,12},{30,14},{17,1},... | collective-permute-start | bytes 1544 | tf_op jit(solution)/shard_map/ppermute | solution.py:465
  224.1 3.2 copy-start.9
  224.1 9.6 %collective-permute-start.10 = (s32[16,8]{1,0:T(8,128)S(1)}, s32[16,8]{1,0:T(8,128)S(1)}, u32[]{:S(2)}, u32[]{:S(2)}) collective-permute-start(s32[16,8]{1,0:T(8,128)S(1)} %copy-done.5), channel_id=1, source_target_pairs={{0,16},{2,18},{4,20},{6,22},{8,24},{10,26},{12,28},{14,30},{1,17},... | collective-permute-start | bytes 1544 | tf_op jit(solution)/shard_map/ppermute | solution.py:465
  233.1 3.6 copy-start.6
  233.1 66.5 %collective-permute-start.1 = (bf16[8,128,768]{2,1,0:T(8,128)(2,1)}, bf16[8,128,768]{2,1,0:T(8,128)(2,1)}, u32[]{:S(2)}, u32[]{:S(2)}) collective-permute-start(bf16[8,128,768]{2,1,0:T(8,128)(2,1)} %get-tuple-element.26), channel_id=1, source_target_pairs={{0,4},{2,6},{4,0},{6,2},{8,12},{10,14},{12,8},{14,10},{16,20},{18,... | collective-permute-start | bytes 4718600 | tf_op jit(solution)/shard_map/ppermute | solution.py:469
  233.7 3.0 copy-start.7
  233.7 66.5 %collective-permute-start.2 = (bf16[8,128,768]{2,1,0:T(8,128)(2,1)}, bf16[8,128,768]{2,1,0:T(8,128)(2,1)}, u32[]{:S(2)}, u32[]{:S(2)}) collective-permute-start(bf16[8,128,768]{2,1,0:T(8,128)(2,1)} %get-tuple-element.27), channel_id=1, source_target_pairs={{0,6},{2,4},{4,2},{6,0},{8,14},{10,12},{12,10},{14,8},{16,22},{18,... | collective-permute-start | bytes 4718600 | tf_op jit(solution)/shard_map/ppermute | solution.py:469
  235.2 66.5 %collective-permute-start.7 = (bf16[8,128,768]{2,1,0:T(8,128)(2,1)}, bf16[8,128,768]{2,1,0:T(8,128)(2,1)}, u32[]{:S(2)}, u32[]{:S(2)}) collective-permute-start(bf16[8,128,768]{2,1,0:T(8,128)(2,1)} %get-tuple-element.28), channel_id=1, source_target_pairs={{0,2},{2,0},{4,6},{6,4},{8,10},{10,8},{12,14},{14,12},{16,18},{18,... | collective-permute-start | bytes 4718600 | tf_op jit(solution)/shard_map/ppermute | solution.py:469
  299.7 72.8 %collective-permute-start.8 = (bf16[8,128,768]{2,1,0:T(8,128)(2,1)}, bf16[8,128,768]{2,1,0:T(8,128)(2,1)}, u32[]{:S(2)}, u32[]{:S(2)}) collective-permute-start(bf16[8,128,768]{2,1,0:T(8,128)(2,1)} %get-tuple-element.29), channel_id=1, source_target_pairs={{0,4},{2,6},{4,0},{6,2},{8,12},{10,14},{12,8},{14,10},{16,20},{18,... | collective-permute-start | bytes 4718600 | tf_op jit(solution)/shard_map/ppermute | solution.py:469
  300.2 72.8 %collective-permute-start.9 = (bf16[8,128,768]{2,1,0:T(8,128)(2,1)}, bf16[8,128,768]{2,1,0:T(8,128)(2,1)}, u32[]{:S(2)}, u32[]{:S(2)}) collective-permute-start(bf16[8,128,768]{2,1,0:T(8,128)(2,1)} %get-tuple-element.30), channel_id=1, source_target_pairs={{0,6},{2,4},{4,2},{6,0},{8,14},{10,12},{12,10},{14,8},{16,22},{18,... | collective-permute-start | bytes 4718600 | tf_op jit(solution)/shard_map/ppermute | solution.py:469
  301.7 72.5 %collective-permute-start.14 = (bf16[8,128,768]{2,1,0:T(8,128)(2,1)}, bf16[8,128,768]{2,1,0:T(8,128)(2,1)}, u32[]{:S(2)}, u32[]{:S(2)}) collective-permute-start(bf16[8,128,768]{2,1,0:T(8,128)(2,1)} %get-tuple-element.31), channel_id=1, source_target_pairs={{0,2},{2,0},{4,6},{6,4},{8,10},{10,8},{12,14},{14,12},{16,18},{18,... | collective-permute-start | bytes 4718600 | tf_op jit(solution)/shard_map/ppermute | solution.py:469
  304.3 135.5 %collective-permute-start.15 = (bf16[8,128,768]{2,1,0:T(8,128)(2,1)}, bf16[8,128,768]{2,1,0:T(8,128)(2,1)S(1)}, u32[]{:S(2)}, u32[]{:S(2)}) collective-permute-start(bf16[8,128,768]{2,1,0:T(8,128)(2,1)} %get-tuple-element.32), channel_id=1, source_target_pairs={{0,4},{2,6},{4,0},{6,2},{8,12},{10,14},{12,8},{14,10},{16,20},{18,... | collective-permute-start | bytes 4718600 | tf_op jit(solution)/shard_map/ppermute | solution.py:469
  304.8 134.9 %collective-permute-start.16 = (bf16[8,128,768]{2,1,0:T(8,128)(2,1)}, bf16[8,128,768]{2,1,0:T(8,128)(2,1)}, u32[]{:S(2)}, u32[]{:S(2)}) collective-permute-start(bf16[8,128,768]{2,1,0:T(8,128)(2,1)} %get-tuple-element.33), channel_id=1, source_target_pairs={{0,6},{2,4},{4,2},{6,0},{8,14},{10,12},{12,10},{14,8},{16,22},{18,... | collective-permute-start | bytes 4718600 | tf_op jit(solution)/shard_map/ppermute | solution.py:469
  372.4 96.0 %collective-permute-start.21 = (bf16[8,128,768]{2,1,0:T(8,128)(2,1)}, bf16[8,128,768]{2,1,0:T(8,128)(2,1)S(1)}, u32[]{:S(2)}, u32[]{:S(2)}) collective-permute-start(bf16[8,128,768]{2,1,0:T(8,128)(2,1)} %get-tuple-element.37), channel_id=1, source_target_pairs={{0,2},{2,0},{4,6},{6,4},{8,10},{10,8},{12,14},{14,12},{16,18},{18,... | collective-permute-start | bytes 4718600 | tf_op jit(solution)/shard_map/ppermute | solution.py:469
  373.0 130.7 %collective-permute-start.22 = (bf16[8,128,768]{2,1,0:T(8,128)(2,1)}, bf16[8,128,768]{2,1,0:T(8,128)(2,1)}, u32[]{:S(2)}, u32[]{:S(2)}) collective-permute-start(bf16[8,128,768]{2,1,0:T(8,128)(2,1)} %get-tuple-element.38), channel_id=1, source_target_pairs={{0,4},{2,6},{4,0},{6,2},{8,12},{10,14},{12,8},{14,10},{16,20},{18,... | collective-permute-start | bytes 4718600 | tf_op jit(solution)/shard_map/ppermute | solution.py:469
  374.2 129.5 %collective-permute-start.23 = (bf16[8,128,768]{2,1,0:T(8,128)(2,1)}, bf16[8,128,768]{2,1,0:T(8,128)(2,1)}, u32[]{:S(2)}, u32[]{:S(2)}) collective-permute-start(bf16[8,128,768]{2,1,0:T(8,128)(2,1)} %get-tuple-element.39), channel_id=1, source_target_pairs={{0,6},{2,4},{4,2},{6,0},{8,14},{10,12},{12,10},{14,8},{16,22},{18,... | collective-permute-start | bytes 4718600 | tf_op jit(solution)/shard_map/ppermute | solution.py:469
  439.7 1.1 copy-start.3
  468.5 35.3 %copy-start.4 = (bf16[8,128,768]{2,1,0:T(8,128)(2,1)}, bf16[8,128,768]{2,1,0:T(8,128)(2,1)S(1)}, u32[]{:S(2)}) copy-start(bf16[8,128,768]{2,1,0:T(8,128)(2,1)S(1)} %collective-permute-done.21.refs_4_) | copy-start | bytes 4718596
  528.1 4.4 collective-permute-start.24
  532.6 1.3 copy-start.2
  539.6 53.4 %all-to-all-start = ((bf16[16,8,64,128]{3,2,1,0:T(8,128)(2,1)}), bf16[16,8,64,128]{3,2,1,0:T(8,128)(2,1)S(1)}, u32[]{:S(2)}, u32[]{:S(2)}) async-start(bf16[16,8,64,128]{3,2,1,0:T(8,128)(2,1)} %bitcast.21), calls=%async_computation | async-start | bytes 4194304 | tf_op jit(solution)/shard_map/all_to_all | solution.py:576
  557.4 4.5 collective-permute-start.25
  593.0 1.3 copy-start.1

commit v6 on v5

--- a/solution.py
+++ b/solution.py
@@ -350,7 +350,6 @@
 def outgoing_blocks(slots, sample_part, grams, came_col, slot_count):
     row_count, kslots, half_rows, block_width = came_col.shape
     rows = rows_per_step(row_count)
-    spec = pl.BlockSpec((rows, kslots, half_rows, block_width), lambda i, *_: (i, 0, 0, 0))
     return pl.pallas_call(
         outgoing_kernel,
         out_shape=[
@@ -365,7 +364,7 @@
                     (rows, kslots, half_rows, block_width),
                     lambda i, slot, half: (i, 0, half[0], 0),
                 ),
-                spec,
+                pl.BlockSpec((rows, kslots, half_rows, block_width), lambda i, *_: (i, 0, 0, 0)),
             ],
             out_specs=[
                 pl.BlockSpec((rows, half_rows, block_width), lambda i, *_: (i, 0, 0)),
@@ -422,7 +421,7 @@
                 spec,
                 spec,
                 pl.BlockSpec((rows, half_rows, block_width), lambda i, *_: (i, 0, 0)),
-                pl.BlockSpec(incoming.shape, lambda i, *_: (0, 0, 0)),
+                pl.BlockSpec(memory_space=pltpu.VMEM),
                 pl.BlockSpec(
                     (rows, kslots, half_rows, block_width),
                     lambda i, slot, half: (i, 0, half[0], 0),
@@ -580,6 +579,7 @@
         concat_axis=0,
         tiled=True,
     ).reshape(devices * capacity, half_rows, block_width)
+    incoming = pltpu.with_memory_space_constraint(incoming, pltpu.VMEM)
     keep_row, send_row = turned_halves(sample_part, grams, half_rows)
     came_row = lax.ppermute(send_row, "samp", swap)
     return tuple(

time: 606 us -> 604 us (level)
  no operation moved by 1% of the time
where the time goes in v6:
time: 604 us; the launch traced here: 602 us
  waiting for transfers between devices  370 us (61%)
  starting transfers between devices  112 us (19%)
  Pallas kernels  104 us (17%)
  local copies, waits for them, and re-layouts  10.9 us (2%)
    ppermute x12, waiting for transfers between devices, across(): return lax.ppermute(array, 'vars', pairs)  206 us
    ppermute x12, waiting for transfers between devices, along(): return lax.ppermute(array, 'vars', pairs)  124 us
    ppermute x12, starting transfers between devices, along(): return lax.ppermute(array, 'vars', pairs)  93.2 us
    all_to_all x1, waiting for transfers between devices, step_on_device(): lax.all_to_all(outgoing.reshape(devices, capacity, half_rows, block_width...  31.1 us
    pallas_call x1, Pallas kernels, gather_early(): pl.pallas_call(gather_kernel(layout, kslots, capacity), out_shape=[jax.Sh...  27.6 us
    pallas_call x4, Pallas kernels, select_panels(): pl.pallas_call(select_kernel(phase, len(arrays), targets, capacity), out_...  25 us
    pallas_call x1, Pallas kernels, grams_of(): pl.pallas_call(gram_kernel(len(lines), kslots, capacity, half_rows), out_...  24.4 us
    ppermute x12, starting transfers between devices, across(): return lax.ppermute(array, 'vars', pairs)  13.1 us
  transfers between devices with their start and end apart: 27, of which 10 were waited for; matrix products, arithmetic and copies ran while one was open for 2% of the time, Pallas kernels for 11%

profile of v6, /device:TPU:14, one launch (start us, length us, event | category | flops | bytes accessed | tf_op | source)
XLA Modules:
  0.0 601.9 jit_solution(15026023914410044418)
XLA Ops:
  0.6 2.4 collective-permute-start.6
  3.0 3.5 collective-permute-start.5
  6.5 66.2 %collective-permute-done.6.refs_3_.refs_6_.refs_11_ = bf16[16,128,768]{2,1,0:T(8,128)(2,1)} collective-permute-done((bf16[16,128,768]{2,1,0:T(8,128)(2,1)}, bf16[16,128,768]{2,1,0:T(8,128)(2,1)}, u32[]{:S(2)}, u32[]{:S(2)}) %collective-permute-start.6) | collective-permute-done | bytes 3145760 | tf_op jit(solution)/shard_map/ppermute | solution.py:464
  72.7 2.3 collective-permute-start.13
  75.0 4.0 collective-permute-start.12
  79.0 1.4 copy.24.refs_0_
  80.4 1.2 fusion.6
  81.6 6.2 %select_panels.4 = (bf16[8,128,768]{2,1,0:T(8,128)(2,1)}, bf16[8,128,768]{2,1,0:T(8,128)(2,1)}, bf16[8,128,768]{2,1,0:T(8,128)(2,1)}) custom-call(s32[6]{0:T(128)} %get-tuple-element.52.info_ref, s32[16,8]{1,0:T(8,128)} %copy.24.refs_0_, bf16[16,128,768]{2,1,0:T(8,128)(2,1)} %bitcast.19), custom_call_target="tpu_custom_call" | custom-call | bytes 9437184 | tf_op jit(solution)/shard_map/select_panels/pallas_call | solution.py:76
  88.3 55.4 %collective-permute-done.13.refs_7_.refs_12_.refs_6_.refs_2_ = bf16[16,128,768]{2,1,0:T(8,128)(2,1)S(1)} collective-permute-done((bf16[16,128,768]{2,1,0:T(8,128)(2,1)}, bf16[16,128,768]{2,1,0:T(8,128)(2,1)S(1)}, u32[]{:S(2)}, u32[]{:S(2)}) %collective-permute-start.13) | collective-permute-done | bytes 3145760 | tf_op jit(solution)/shard_map/ppermute | solution.py:464
  143.8 2.3 collective-permute-start.18
  146.1 3.8 collective-permute-start.17
  149.9 0.7 collective-permute-start.20
  150.6 0.7 collective-permute-start.19
  151.3 67.2 %collective-permute-start.4 = (s32[16,8]{1,0:T(8,128)S(1)}, s32[16,8]{1,0:T(8,128)S(1)}, u32[]{:S(2)}, u32[]{:S(2)}) collective-permute-start(s32[16,8]{1,0:T(8,128)S(1)} %copy-done.4), channel_id=1, source_target_pairs={{8,0},{10,2},{12,4},{14,6},{16,8},{18,10},{20,12},{22,14},{24,16},... | collective-permute-start | bytes 1544 | tf_op jit(solution)/shard_map/ppermute | solution.py:464
  218.5 1.9 collective-permute-start.3
  220.5 1.3 collective-permute-start.11
  221.8 2.3 collective-permute-done.3.refs_0_.refs_1_
  224.1 3.2 collective-permute-start.10
  227.3 5.8 select_panels.5
  233.7 1.5 collective-permute-start.2
  235.2 1.5 collective-permute-start.7
  236.7 6.4 %select_panels.6 = (bf16[8,128,768]{2,1,0:T(8,128)(2,1)}, bf16[8,128,768]{2,1,0:T(8,128)(2,1)}, bf16[8,128,768]{2,1,0:T(8,128)(2,1)}) custom-call(s32[6]{0:T(128)} %get-tuple-element.52.info_ref, s32[16,8]{1,0:T(8,128)} %copy-done.6, s32[16,8]{1,0:T(8,128)} %copy-done.8, s32[16,8]{1,0:T(8,128)} %copy-done.7, s32[16,8]{1,0:T(8,128)} %copy-done.5, ...), custom_call_target="tpu_custom_call" | custom-call | bytes 9437184 | tf_op jit(solution)/shard_map/select_panels/pallas_call | solution.py:76
  243.2 56.5 %collective-permute-done.1.refs_1_ = bf16[8,128,768]{2,1,0:T(8,128)(2,1)} collective-permute-done((bf16[8,128,768]{2,1,0:T(8,128)(2,1)}, bf16[8,128,768]{2,1,0:T(8,128)(2,1)}, u32[]{:S(2)}, u32[]{:S(2)}) %collective-permute-start.1) | collective-permute-done | bytes 1572896 | tf_op jit(solution)/shard_map/ppermute | solution.py:468
  300.2 1.5 collective-permute-start.9
  301.7 1.5 collective-permute-start.14
  303.3 0.7 constant_dynamic-slice_fusion.1
  304.8 1.5 collective-permute-start.16
  306.3 6.6 %select_panels.7 = (bf16[8,128,768]{2,1,0:T(8,128)(2,1)}, bf16[8,128,768]{2,1,0:T(8,128)(2,1)}, bf16[8,128,768]{2,1,0:T(8,128)(2,1)}) custom-call(s32[6]{0:T(128)} %get-tuple-element.52.info_ref, s32[16,8]{1,0:T(8,128)} %copy-done.10, s32[16,8]{1,0:T(8,128)} %copy-done.6, s32[16,8]{1,0:T(8,128)} %copy-done.5, s32[16,8]{1,0:T(8,128)} %copy-done.9, ...), custom_call_target="tpu_custom_call" | custom-call | bytes 9437184 | tf_op jit(solution)/shard_map/select_panels/pallas_call | solution.py:76
  312.9 59.6 %collective-permute-done.8.refs_4_ = bf16[8,128,768]{2,1,0:T(8,128)(2,1)} collective-permute-done((bf16[8,128,768]{2,1,0:T(8,128)(2,1)}, bf16[8,128,768]{2,1,0:T(8,128)(2,1)}, u32[]{:S(2)}, u32[]{:S(2)}) %collective-permute-start.8) | collective-permute-done | bytes 1572896 | tf_op jit(solution)/shard_map/ppermute | solution.py:468
  373.0 1.2 collective-permute-start.22
  374.3 1.7 collective-permute-start.23
  377.3 0.7 slice.56.panel_ref
  379.9 1.9 stack.8.code_ref
  381.8 1.2 pad_add_fusion.code_ref
  383.0 1.2 and_select_fusion.3
  384.8 55.0 %collective-permute-done.15.refs_7_ = bf16[8,128,768]{2,1,0:T(8,128)(2,1)S(1)} collective-permute-done((bf16[8,128,768]{2,1,0:T(8,128)(2,1)}, bf16[8,128,768]{2,1,0:T(8,128)(2,1)S(1)}, u32[]{:S(2)}, u32[]{:S(2)}) %collective-permute-start.15) | collective-permute-done | bytes 1572896 | tf_op jit(solution)/shard_map/ppermute | solution.py:468
  439.8 1.1 copy-done.2
  440.9 27.6 %gather_early.1 = (f32[16,128,768]{2,1,0:T(8,128)}, bf16[16,1024,768]{2,1,0:T(8,128)(2,1)S(1)}, bf16[32,128,128]{2,1,0:T(8,128)(2,1)}) custom-call(s32[96]{0:T(128)} %slice.54.entry_ref, s32[96]{0:T(128)} %slice.56.panel_ref, s32[12]{0:T(128)} %stack.8.code_ref, s32[128]{0:T(128)} %get-tuple-element.56.late_ref, f32[16,8,128,128]{3,2,1,0:T(8,128)} %omega_ref.3, ...), custom_call_target="tpu_custom_call" | custom-call | flops 3221225472 | bytes 25165824 | tf_op jit(solution)/shard_map/gather_early/pallas_call | solution.py:163
  468.5 35.2 %collective-permute-done.22.refs_5_ = bf16[8,128,768]{2,1,0:T(8,128)(2,1)} collective-permute-done((bf16[8,128,768]{2,1,0:T(8,128)(2,1)}, bf16[8,128,768]{2,1,0:T(8,128)(2,1)}, u32[]{:S(2)}, u32[]{:S(2)}) %collective-permute-start.22) | collective-permute-done | bytes 1572896 | tf_op jit(solution)/shard_map/ppermute | solution.py:468
  503.7 24.4 %grams.1 = (f32[16,8,128,128]{3,2,1,0:T(8,128)}, bf16[16,8,64,128]{3,2,1,0:T(8,128)(2,1)}, bf16[16,1024,768]{2,1,0:T(8,128)(2,1)S(1)}) custom-call(s32[8]{0:T(128)} %slice_bitcast_fusion.panel_ref, s32[2]{0:T(128)} %pad_add_fusion.code_ref, s32[128]{0:T(128)} %get-tuple-element.56.late_ref, s32[32]{0:T(128)} %slice.52.entry_ref, ...), custom_call_target="tpu_custom_call", output_to_operand_aliasing={{2}: (6, {})} | custom-call | flops 3221225472 | bytes 37748736 | tf_op jit(solution)/shard_map/grams/pallas_call | solution.py:268
  528.3 4.4 collective-permute-done.24.came_ref
  532.6 1.3 copy-done.1
  533.9 5.7 outgoing.1
  539.6 5.1 all-to-all-start
  544.7 12.7 %turn.1 = (f32[16,8,64,128]{3,2,1,0:T(8,128)}, bf16[16,8,64,128]{3,2,1,0:T(8,128)(2,1)}) custom-call(s32[1]{0:T(128)} %bitcast.half_ref.part_ref, f32[16,8,128,128]{3,2,1,0:T(8,128)} %get-tuple-element.43.keep_ref.grams_ref), custom_call_target="tpu_custom_call" | custom-call | tf_op jit(solution)/shard_map/turn/pallas_call | solution.py:322
  557.5 4.5 collective-permute-done.25.came_ref
  562.0 31.1 %all-to-all-done = bf16[16,8,64,128]{3,2,1,0:T(8,128)(2,1)S(1)} async-done(((bf16[16,8,64,128]{3,2,1,0:T(8,128)(2,1)}), bf16[16,8,64,128]{3,2,1,0:T(8,128)(2,1)S(1)}, u32[]{:S(2)}, u32[]{:S(2)}) %all-to-all-start) | async-done | bytes 2097184 | tf_op jit(solution)/shard_map/all_to_all | solution.py:575
  593.1 8.8 %final_step.1 = (f32[16,8,64,128]{3,2,1,0:T(8,128)}, f32[16,8,64,128]{3,2,1,0:T(8,128)}) custom-call(s32[128]{0:T(128)} %get-tuple-element.61.slot_ref, s32[1]{0:T(128)} %bitcast.half_ref.part_ref, f32[16,8,64,128]{3,2,1,0:T(8,128)} %get-tuple-element.44.keep_ref, bf16[16,8,64,128]{3,2,1,0:T(8,128)(2,1)} %collective-permute-done.25.came_ref, ...), custom_call_target="tpu_custom_call" | custom-call | tf_op jit(solution)/shard_map/final_step/pallas_call | solution.py:414
  (64 shorter events, 7.2 us)
Async XLA Ops:
  0.6 72.1 %collective-permute-start.6 = (bf16[16,128,768]{2,1,0:T(8,128)(2,1)}, bf16[16,128,768]{2,1,0:T(8,128)(2,1)}, u32[]{:S(2)}, u32[]{:S(2)}) collective-permute-start(bf16[16,128,768]{2,1,0:T(8,128)(2,1)} %bitcast.17), channel_id=1, source_target_pairs={{8,0},{10,2},{12,4},{14,6},{16,8},{18,10},{20,12},{22,14},{24,16},... | collective-permute-start | bytes 9437192 | tf_op jit(solution)/shard_map/ppermute | solution.py:464
  3.0 72.0 %collective-permute-start.5 = (bf16[16,128,768]{2,1,0:T(8,128)(2,1)}, bf16[16,128,768]{2,1,0:T(8,128)(2,1)}, u32[]{:S(2)}, u32[]{:S(2)}) collective-permute-start(bf16[16,128,768]{2,1,0:T(8,128)(2,1)} %bitcast.18), channel_id=1, source_target_pairs={{0,8},{2,10},{4,12},{6,14},{8,16},{10,18},{12,20},{14,22},{16,24},... | collective-permute-start | bytes 9437192 | tf_op jit(solution)/shard_map/ppermute | solution.py:464
  72.7 71.1 %collective-permute-start.13 = (bf16[16,128,768]{2,1,0:T(8,128)(2,1)}, bf16[16,128,768]{2,1,0:T(8,128)(2,1)S(1)}, u32[]{:S(2)}, u32[]{:S(2)}) collective-permute-start(bf16[16,128,768]{2,1,0:T(8,128)(2,1)} %collective-permute-done.6.refs_3_.refs_6_.refs_11_), channel_id=1, source_target_pairs={{8,0},{10,2},{12,4},{14,6},{16,8},{18,10},{20,12},{22,14},{24,16},... | collective-permute-start | bytes 9437192 | tf_op jit(solution)/shard_map/ppermute | solution.py:464
  75.0 71.1 %collective-permute-start.12 = (bf16[16,128,768]{2,1,0:T(8,128)(2,1)}, bf16[16,128,768]{2,1,0:T(8,128)(2,1)}, u32[]{:S(2)}, u32[]{:S(2)}) collective-permute-start(bf16[16,128,768]{2,1,0:T(8,128)(2,1)} %collective-permute-done.5.refs_2_.refs_5_.refs_10_), channel_id=1, source_target_pairs={{0,8},{2,10},{4,12},{6,14},{8,16},{10,18},{12,20},{14,22},{16,24},... | collective-permute-start | bytes 9437192 | tf_op jit(solution)/shard_map/ppermute | solution.py:464
  81.6 68.3 %copy-start.4 = (s32[16,8]{1,0:T(8,128)S(1)}, s32[16,8]{1,0:T(8,128)}, u32[]{:S(2)}) copy-start(s32[16,8]{1,0:T(8,128)} %copy.24.refs_0_) | copy-start | bytes 1540
  87.7 147.5 %collective-permute-start = (bf16[8,128,768]{2,1,0:T(8,128)(2,1)}, bf16[8,128,768]{2,1,0:T(8,128)(2,1)}, u32[]{:S(2)}, u32[]{:S(2)}) collective-permute-start(bf16[8,128,768]{2,1,0:T(8,128)(2,1)} %get-tuple-element.25), channel_id=1, source_target_pairs={{0,2},{2,0},{4,6},{6,4},{8,10},{10,8},{12,14},{14,12},{16,18},{18,... | collective-permute-start | bytes 4718600 | tf_op jit(solution)/shard_map/ppermute | solution.py:468
  143.8 89.4 %copy-start = (bf16[16,128,768]{2,1,0:T(8,128)(2,1)}, bf16[16,128,768]{2,1,0:T(8,128)(2,1)S(1)}, u32[]{:S(2)}) copy-start(bf16[16,128,768]{2,1,0:T(8,128)(2,1)S(1)} %collective-permute-done.13.refs_7_.refs_12_.refs_6_.refs_2_) | copy-start | bytes 9437188
  143.8 160.5 %collective-permute-start.18 = (bf16[16,128,768]{2,1,0:T(8,128)(2,1)S(1)}, bf16[16,128,768]{2,1,0:T(8,128)(2,1)}, u32[]{:S(2)}, u32[]{:S(2)}) collective-permute-start(bf16[16,128,768]{2,1,0:T(8,128)(2,1)S(1)} %collective-permute-done.13.refs_7_.refs_12_.refs_6_.refs_2_), channel_id=1, source_target_pairs={{8,0},{10,2},{12,4},{14,6},{16,8},{18,10},{20,12},{22,14},{24,16},... | collective-permute-start | bytes 9437192 | tf_op jit(solution)/shard_map/ppermute | solution.py:464
  146.1 158.7 %collective-permute-start.17 = (bf16[16,128,768]{2,1,0:T(8,128)(2,1)}, bf16[16,128,768]{2,1,0:T(8,128)(2,1)}, u32[]{:S(2)}, u32[]{:S(2)}) collective-permute-start(bf16[16,128,768]{2,1,0:T(8,128)(2,1)} %collective-permute-done.12.refs_4_.refs_9_.refs_5_.refs_1_), channel_id=1, source_target_pairs={{0,8},{2,10},{4,12},{6,14},{8,16},{10,18},{12,20},{14,22},{16,24},... | collective-permute-start | bytes 9437192 | tf_op jit(solution)/shard_map/ppermute | solution.py:464
  149.9 1.3 collective-permute-start.20
  150.6 67.9 %collective-permute-start.19 = (s32[16,8]{1,0:T(8,128)S(1)}, s32[16,8]{1,0:T(8,128)S(1)}, u32[]{:S(2)}, u32[]{:S(2)}) collective-permute-start(s32[16,8]{1,0:T(8,128)S(1)} %copy-done.4), channel_id=1, source_target_pairs={{0,24},{2,26},{4,28},{6,30},{1,25},{3,27},{5,29},{7,31}} | collective-permute-start | bytes 1544 | tf_op jit(solution)/shard_map/ppermute | solution.py:464
  151.3 91.9 %copy-start.9 = (s32[16,8]{1,0:T(8,128)}, s32[16,8]{1,0:T(8,128)S(1)}, u32[]{:S(2)}) copy-start(s32[16,8]{1,0:T(8,128)S(1)} %collective-permute-done.20.refs_3_) | copy-start | bytes 1540
  151.3 69.2 %collective-permute-start.4 = (s32[16,8]{1,0:T(8,128)S(1)}, s32[16,8]{1,0:T(8,128)S(1)}, u32[]{:S(2)}, u32[]{:S(2)}) collective-permute-start(s32[16,8]{1,0:T(8,128)S(1)} %copy-done.4), channel_id=1, source_target_pairs={{8,0},{10,2},{12,4},{14,6},{16,8},{18,10},{20,12},{22,14},{24,16},... | collective-permute-start | bytes 1544 | tf_op jit(solution)/shard_map/ppermute | solution.py:464
  218.5 24.6 %copy-start.10 = (s32[16,8]{1,0:T(8,128)}, s32[16,8]{1,0:T(8,128)S(1)}, u32[]{:S(2)}) copy-start(s32[16,8]{1,0:T(8,128)S(1)} %collective-permute-done.19.refs_0_) | copy-start | bytes 1540
  218.5 5.5 collective-permute-start.3
  220.5 6.8 %copy-start.7 = (s32[16,8]{1,0:T(8,128)}, s32[16,8]{1,0:T(8,128)S(1)}, u32[]{:S(2)}) copy-start(s32[16,8]{1,0:T(8,128)S(1)} %collective-permute-done.4.refs_1_.refs_2_) | copy-start | bytes 1540
  220.5 12.6 %collective-permute-start.11 = (s32[16,8]{1,0:T(8,128)S(1)}, s32[16,8]{1,0:T(8,128)S(1)}, u32[]{:S(2)}, u32[]{:S(2)}) collective-permute-start(s32[16,8]{1,0:T(8,128)S(1)} %copy-done.4), channel_id=1, source_target_pairs={{16,0},{18,2},{20,4},{22,6},{24,8},{26,10},{28,12},{30,14},{17,1},... | collective-permute-start | bytes 1544 | tf_op jit(solution)/shard_map/ppermute | solution.py:464
  224.1 3.2 copy-start.8
  224.1 9.6 %collective-permute-start.10 = (s32[16,8]{1,0:T(8,128)S(1)}, s32[16,8]{1,0:T(8,128)S(1)}, u32[]{:S(2)}, u32[]{:S(2)}) collective-permute-start(s32[16,8]{1,0:T(8,128)S(1)} %copy-done.4), channel_id=1, source_target_pairs={{0,16},{2,18},{4,20},{6,22},{8,24},{10,26},{12,28},{14,30},{1,17},... | collective-permute-start | bytes 1544 | tf_op jit(solution)/shard_map/ppermute | solution.py:464
  233.1 3.6 copy-start.5
  233.2 66.5 %collective-permute-start.1 = (bf16[8,128,768]{2,1,0:T(8,128)(2,1)}, bf16[8,128,768]{2,1,0:T(8,128)(2,1)}, u32[]{:S(2)}, u32[]{:S(2)}) collective-permute-start(bf16[8,128,768]{2,1,0:T(8,128)(2,1)} %get-tuple-element.26), channel_id=1, source_target_pairs={{0,4},{2,6},{4,0},{6,2},{8,12},{10,14},{12,8},{14,10},{16,20},{18,... | collective-permute-start | bytes 4718600 | tf_op jit(solution)/shard_map/ppermute | solution.py:468
  233.7 3.0 copy-start.6
  233.7 66.5 %collective-permute-start.2 = (bf16[8,128,768]{2,1,0:T(8,128)(2,1)}, bf16[8,128,768]{2,1,0:T(8,128)(2,1)}, u32[]{:S(2)}, u32[]{:S(2)}) collective-permute-start(bf16[8,128,768]{2,1,0:T(8,128)(2,1)} %get-tuple-element.27), channel_id=1, source_target_pairs={{0,6},{2,4},{4,2},{6,0},{8,14},{10,12},{12,10},{14,8},{16,22},{18,... | collective-permute-start | bytes 4718600 | tf_op jit(solution)/shard_map/ppermute | solution.py:468
  235.2 66.5 %collective-permute-start.7 = (bf16[8,128,768]{2,1,0:T(8,128)(2,1)}, bf16[8,128,768]{2,1,0:T(8,128)(2,1)}, u32[]{:S(2)}, u32[]{:S(2)}) collective-permute-start(bf16[8,128,768]{2,1,0:T(8,128)(2,1)} %get-tuple-element.28), channel_id=1, source_target_pairs={{0,2},{2,0},{4,6},{6,4},{8,10},{10,8},{12,14},{14,12},{16,18},{18,... | collective-permute-start | bytes 4718600 | tf_op jit(solution)/shard_map/ppermute | solution.py:468
  299.7 72.8 %collective-permute-start.8 = (bf16[8,128,768]{2,1,0:T(8,128)(2,1)}, bf16[8,128,768]{2,1,0:T(8,128)(2,1)}, u32[]{:S(2)}, u32[]{:S(2)}) collective-permute-start(bf16[8,128,768]{2,1,0:T(8,128)(2,1)} %get-tuple-element.29), channel_id=1, source_target_pairs={{0,4},{2,6},{4,0},{6,2},{8,12},{10,14},{12,8},{14,10},{16,20},{18,... | collective-permute-start | bytes 4718600 | tf_op jit(solution)/shard_map/ppermute | solution.py:468
  300.2 72.8 %collective-permute-start.9 = (bf16[8,128,768]{2,1,0:T(8,128)(2,1)}, bf16[8,128,768]{2,1,0:T(8,128)(2,1)}, u32[]{:S(2)}, u32[]{:S(2)}) collective-permute-start(bf16[8,128,768]{2,1,0:T(8,128)(2,1)} %get-tuple-element.30), channel_id=1, source_target_pairs={{0,6},{2,4},{4,2},{6,0},{8,14},{10,12},{12,10},{14,8},{16,22},{18,... | collective-permute-start | bytes 4718600 | tf_op jit(solution)/shard_map/ppermute | solution.py:468
  301.7 72.5 %collective-permute-start.14 = (bf16[8,128,768]{2,1,0:T(8,128)(2,1)}, bf16[8,128,768]{2,1,0:T(8,128)(2,1)}, u32[]{:S(2)}, u32[]{:S(2)}) collective-permute-start(bf16[8,128,768]{2,1,0:T(8,128)(2,1)} %get-tuple-element.31), channel_id=1, source_target_pairs={{0,2},{2,0},{4,6},{6,4},{8,10},{10,8},{12,14},{14,12},{16,18},{18,... | collective-permute-start | bytes 4718600 | tf_op jit(solution)/shard_map/ppermute | solution.py:468
  304.3 135.5 %collective-permute-start.15 = (bf16[8,128,768]{2,1,0:T(8,128)(2,1)}, bf16[8,128,768]{2,1,0:T(8,128)(2,1)S(1)}, u32[]{:S(2)}, u32[]{:S(2)}) collective-permute-start(bf16[8,128,768]{2,1,0:T(8,128)(2,1)} %get-tuple-element.32), channel_id=1, source_target_pairs={{0,4},{2,6},{4,0},{6,2},{8,12},{10,14},{12,8},{14,10},{16,20},{18,... | collective-permute-start | bytes 4718600 | tf_op jit(solution)/shard_map/ppermute | solution.py:468
  304.8 134.9 %collective-permute-start.16 = (bf16[8,128,768]{2,1,0:T(8,128)(2,1)}, bf16[8,128,768]{2,1,0:T(8,128)(2,1)}, u32[]{:S(2)}, u32[]{:S(2)}) collective-permute-start(bf16[8,128,768]{2,1,0:T(8,128)(2,1)} %get-tuple-element.33), channel_id=1, source_target_pairs={{0,6},{2,4},{4,2},{6,0},{8,14},{10,12},{12,10},{14,8},{16,22},{18,... | collective-permute-start | bytes 4718600 | tf_op jit(solution)/shard_map/ppermute | solution.py:468
  372.5 96.0 %collective-permute-start.21 = (bf16[8,128,768]{2,1,0:T(8,128)(2,1)}, bf16[8,128,768]{2,1,0:T(8,128)(2,1)S(1)}, u32[]{:S(2)}, u32[]{:S(2)}) collective-permute-start(bf16[8,128,768]{2,1,0:T(8,128)(2,1)} %get-tuple-element.37), channel_id=1, source_target_pairs={{0,2},{2,0},{4,6},{6,4},{8,10},{10,8},{12,14},{14,12},{16,18},{18,... | collective-permute-start | bytes 4718600 | tf_op jit(solution)/shard_map/ppermute | solution.py:468
  373.0 130.7 %collective-permute-start.22 = (bf16[8,128,768]{2,1,0:T(8,128)(2,1)}, bf16[8,128,768]{2,1,0:T(8,128)(2,1)}, u32[]{:S(2)}, u32[]{:S(2)}) collective-permute-start(bf16[8,128,768]{2,1,0:T(8,128)(2,1)} %get-tuple-element.38), channel_id=1, source_target_pairs={{0,4},{2,6},{4,0},{6,2},{8,12},{10,14},{12,8},{14,10},{16,20},{18,... | collective-permute-start | bytes 4718600 | tf_op jit(solution)/shard_map/ppermute | solution.py:468
  374.3 129.5 %collective-permute-start.23 = (bf16[8,128,768]{2,1,0:T(8,128)(2,1)}, bf16[8,128,768]{2,1,0:T(8,128)(2,1)}, u32[]{:S(2)}, u32[]{:S(2)}) collective-permute-start(bf16[8,128,768]{2,1,0:T(8,128)(2,1)} %get-tuple-element.39), channel_id=1, source_target_pairs={{0,6},{2,4},{4,2},{6,0},{8,14},{10,12},{12,10},{14,8},{16,22},{18,... | collective-permute-start | bytes 4718600 | tf_op jit(solution)/shard_map/ppermute | solution.py:468
  439.8 1.1 copy-start.2
  468.5 35.3 %copy-start.3 = (bf16[8,128,768]{2,1,0:T(8,128)(2,1)}, bf16[8,128,768]{2,1,0:T(8,128)(2,1)S(1)}, u32[]{:S(2)}) copy-start(bf16[8,128,768]{2,1,0:T(8,128)(2,1)S(1)} %collective-permute-done.21.refs_4_) | copy-start | bytes 4718596
  528.2 4.4 collective-permute-start.24
  532.6 1.3 copy-start.1
  539.6 53.4 %all-to-all-start = ((bf16[16,8,64,128]{3,2,1,0:T(8,128)(2,1)}), bf16[16,8,64,128]{3,2,1,0:T(8,128)(2,1)S(1)}, u32[]{:S(2)}, u32[]{:S(2)}) async-start(bf16[16,8,64,128]{3,2,1,0:T(8,128)(2,1)} %bitcast.21), calls=%async_computation | async-start | bytes 4194304 | tf_op jit(solution)/shard_map/all_to_all | solution.py:575
  557.5 4.5 collective-permute-start.25
